TPU v7x, 256 devices: a whole 4x4x8 slice. The times are simulated.
256 devices in a mesh: tm: 8 (over x, core), space: 32 (over z, y).
Axes of the slice: x: 4, y: 4, z: 8, core: 2. Of those that a mesh axis runs over, the one named last changes fastest.
Arguments:
- span_opening: float32 [8, 128, 64, 128], P('tm', 'space'), may hold values from -8 to 8
- source_power: float32 [8, 2, 128, 64, 128], P('tm', None, 'space'), may hold values from -24 to 24
- warmth_retention: float32 [128, 64, 128], P('space'), may hold values from 0.02 to 0.4
Outputs:
- fpoint: float32 [8, 128, 64, 128], P('tm', 'space')
- updated: float32 [8, 128, 64, 128], P('tm', 'space')
All inputs are finite; a program needn't handle non-finite values.
Results may differ from a plain program's by a relative error of at most 0.0001.
Values sent between devices are 32-bit elements; how exact they have to be, the bound alone decides.
No kernel may reach another device: no remote copies, remote signals or barrier semaphores. Data moves between devices by JAX's collectives and lax.ppermute only.
A program may use at most 64 MiB of HBM per device.

v0:
```python
import jax
import jax.numpy as jnp
from jax import lax
from jax.sharding import PartitionSpec as P

COARSE_SWEEPS = 24


relax_weight = 0.8


def with_halo(cells, sides, width):
    for axis, dim in sides:
        count = lax.axis_size(axis)
        ends = count - 1
        head = lax.slice_in_dim(cells, 0, width, axis=dim)
        tail = lax.slice_in_dim(cells, cells.shape[dim] - width, cells.shape[dim], axis=dim)
        cells = jnp.concatenate(
            [
                lax.ppermute(tail, axis, [(i, (i + 1) % count) for i in range(ends)]),
                cells,
                lax.ppermute(head, axis, [((i + 1) % count, i) for i in range(ends)]),
            ],
            axis=dim,
        )
    return cells


def copy_for_each(x, axis):
    peers = lax.axis_size(axis)
    return lax.all_to_all(jnp.broadcast_to(x[None], (peers, *x.shape)), axis, 0, 0, tiled=True)


def joined_along(pieces, dim):
    dims = list(pieces.shape[1:])
    dims[dim] *= pieces.shape[0]
    return jnp.moveaxis(pieces, 0, dim).reshape(dims)


def collect(x, axis, dim):
    pieces = copy_for_each(x, axis)
    return joined_along(pieces, dim)


def passed_along(x, axis, by):
    peers = lax.axis_size(axis)
    pairs = [(i, i + by) for i in range(peers) if 0 <= i + by < peers]
    return lax.ppermute(x, axis, pairs)


def mean_to_rougher(field):
    extent_layout = field.shape
    blocks = field.reshape(
        extent_layout[0] // 2, 2, extent_layout[1] // 2, 2, extent_layout[2] // 2, 2
    )
    return blocks.mean(axis=(1, 3, 5))


def lift_to_finer(field):
    extent_layout = field.shape
    grown = jnp.broadcast_to(
        field[:, None, :, None, :, None],
        (extent_layout[0], 2, extent_layout[1], 2, extent_layout[2], 2),
    )
    return grown.reshape(2 * extent_layout[0], 2 * extent_layout[1], 2 * extent_layout[2])


def neighbour_sum(field, padded):
    flat = jnp.pad(field, ((0, 0), (1, 1), (1, 1)))
    total = padded[2:] + padded[:-2]
    total = total + flat[:, 2:, 1:-1] + flat[:, :-2, 1:-1]
    return total + flat[:, 1:-1, 2:] + flat[:, 1:-1, :-2]


def apply_nearby_part(field, retention_quantities, conductance):
    padded = jnp.pad(field, ((1, 1), (0, 0), (0, 0)))
    return (retention_quantities + 6.0 * conductance) * field - conductance * neighbour_sum(
        field, padded
    )


def apply_split(field, retention_quantities, conductance):
    padded = with_halo(field, (("space", 0),), 1)
    return (retention_quantities + 6.0 * conductance) * field - conductance * neighbour_sum(
        field, padded
    )


def assemble(gathered, teams_across, fragments):
    depth = gathered.shape[0] // fragments
    rows, cols = (gathered.shape[1], gathered.shape[2])
    blocks = gathered.reshape(fragments // teams_across, teams_across, depth, rows, cols)
    blocks = jnp.transpose(blocks, (0, 2, 1, 3, 4))
    return blocks.reshape(fragments // teams_across * depth, teams_across * rows, cols)


def pull_out(whole, teams_across, location, depth):
    plane_start = location // teams_across * depth
    part_block = lax.dynamic_slice_in_dim(whole, plane_start, depth, 0)
    return part_block


def bottom_grid_inversion(load_components, retention_quantities):
    conductance = 0.125
    diagonal = retention_quantities + 6.0 * conductance
    first_approximation = relax_weight * load_components / diagonal
    for sweep_index in range(COARSE_SWEEPS - 1):
        first_approximation = (
            first_approximation
            + relax_weight
            * (
                load_components
                - apply_nearby_part(first_approximation, retention_quantities, conductance)
            )
            / diagonal
        )
    return first_approximation


def round_division(
    load_components,
    local_caps,
    whole_caps,
    hierarchy_layers,
    last_split,
    location,
    system_matrix,
    teams_across,
    fragments,
):
    conductance = 0.5**hierarchy_layers
    retention_quantities = local_caps[hierarchy_layers]
    diagonal = retention_quantities + 6.0 * conductance
    first_approximation = relax_weight * load_components / diagonal
    first_approximation = (
        first_approximation
        + relax_weight
        * (load_components - system_matrix(first_approximation, retention_quantities, conductance))
        / diagonal
    )
    further_moments = load_components - system_matrix(
        first_approximation, retention_quantities, conductance
    )
    if hierarchy_layers < last_split:
        lower_fix = round_division(
            mean_to_rougher(further_moments),
            local_caps,
            whole_caps,
            hierarchy_layers + 1,
            last_split,
            location,
            system_matrix,
            teams_across,
            fragments,
        )
        adjustment = lift_to_finer(lower_fix)
    else:
        whole_rest = assemble(collect(further_moments, "space", 0), teams_across, fragments)
        complete_adjustment = lift_to_finer(
            bottom_grid_inversion(mean_to_rougher(whole_rest), whole_caps[3])
        )
        adjustment = pull_out(complete_adjustment, teams_across, location, further_moments.shape[0])
    first_approximation = first_approximation + adjustment
    for sweep_index in range(2):
        first_approximation = (
            first_approximation
            + relax_weight
            * (
                load_components
                - system_matrix(first_approximation, retention_quantities, conductance)
            )
            / diagonal
        )
    return first_approximation


def shards(span_opening, source_power, warmth_retention):
    location = lax.axis_index("space")
    fragments = lax.axis_size("space")
    step_count = source_power.shape[1]
    launch_condition = span_opening[0]
    injections = source_power[0]
    teams_across = 1
    mid_cap = mean_to_rougher(warmth_retention)
    low_cap = mean_to_rougher(mid_cap)
    whole_low = assemble(collect(low_cap, "space", 0), teams_across, fragments)
    whole_caps = [None, None, whole_low, mean_to_rougher(whole_low)]
    local_caps = [warmth_retention, mid_cap, low_cap]
    last_split = 2
    warmth_distribution = launch_condition
    opening_condition = warmth_distribution
    for moment_count in range(step_count):
        load_components = warmth_retention * warmth_distribution + injections[moment_count]
        warmth_distribution = round_division(
            load_components,
            local_caps,
            whole_caps,
            0,
            last_split,
            location,
            apply_split,
            teams_across,
            fragments,
        )
        if moment_count == 0:
            opening_condition = warmth_distribution
    shifted_over = passed_along(warmth_distribution, "tm", 1)
    updated = jnp.where(lax.axis_index("tm") == 0, launch_condition, shifted_over)
    return (opening_condition[None], updated[None])


def solution(mesh):
    in_specs = (
        P("tm", "space", None, None),
        P("tm", None, "space", None, None),
        P("space", None, None),
    )
    out_specs = (P("tm", "space", None, None), P("tm", "space", None, None))
    return jax.shard_map(shards, mesh=mesh, in_specs=in_specs, out_specs=out_specs, check_vma=False)
```

profile of v0, /device:TPU:130, one launch (start us, length us, event | category | flops | bytes accessed | tf_op | source)
XLA Modules:
  0.0 427.6 jit_solution(17866311021726871861)
XLA Ops:
  8.1 7.2 %collective-permute-done.1 = f32[1,64,128]{2,1,0:T(8,128)S(1)} collective-permute-done((f32[1,64,128]{2,1,0:T(8,128)S(1)}, f32[1,64,128]{2,1,0:T(8,128)S(1)}, u32[]{:S(2)}, u32[]{:S(2)}) %collective-permute-start.1) | collective-permute-done | bytes 32800 | tf_op jit(solution)/shard_map/ppermute | solution.py:20
  22.4 10.5 %reshape.156 = f32[2,2,32,2,64,2]{5,4,3,2,1,0:T(8,128)} reshape(f32[4,64,128]{2,1,0:T(8,128)} %param.5) | data formatting | bytes 262144 | tf_op jit(solution)/shard_map/reshape | solution.py:53
  37.1 9.8 %reshape.155 = f32[2,2,32,2,64,2]{5,4,3,2,1,0:T(8,128)} reshape(f32[4,64,128]{2,1,0:T(8,128)S(1)} %fusion.14) | data formatting | bytes 262144 | tf_op jit(solution)/shard_map/reshape | solution.py:53
  51.0 5.2 %collective-permute-start.4 = (f32[1,32,64]{2,1,0:T(8,128)S(1)}, f32[1,32,64]{2,1,0:T(8,128)S(1)}, u32[]{:S(2)}, u32[]{:S(2)}) collective-permute-start(f32[1,32,64]{2,1,0:T(8,128)S(1)} %get-tuple-element.39), channel_id=1, source_target_pairs={{1,0},{2,1},{3,2},{4,3},{5,4},{6,5},{7,6},{8,7},{9,8},{10,9},{11,1... | collective-permute-start | bytes 24584 | tf_op jit(solution)/shard_map/ppermute | solution.py:22
  58.1 7.0 %collective-permute-done.5 = f32[1,32,64]{2,1,0:T(8,128)S(1)} collective-permute-done((f32[1,32,64]{2,1,0:T(8,128)S(1)}, f32[1,32,64]{2,1,0:T(8,128)S(1)}, u32[]{:S(2)}, u32[]{:S(2)}) %collective-permute-start.5) | collective-permute-done | bytes 8224 | tf_op jit(solution)/shard_map/ppermute | solution.py:20
  79.6 7.2 %collective-permute-start.8 = (f32[1,16,32]{2,1,0:T(8,128)S(1)}, f32[1,16,32]{2,1,0:T(8,128)S(1)}, u32[]{:S(2)}, u32[]{:S(2)}) collective-permute-start(f32[1,16,32]{2,1,0:T(8,128)S(1)} %bitcast_divide_fusion.1), channel_id=1, source_target_pairs={{1,0},{2,1},{3,2},{4,3},{5,4},{6,5},{7,6},{8,7},{9,8},{10,9},{11,1... | collective-permute-start | bytes 6152 | tf_op jit(solution)/shard_map/ppermute | solution.py:22
  90.2 7.5 %collective-permute-start.10 = (f32[1,16,32]{2,1,0:T(8,128)S(1)}, f32[1,16,32]{2,1,0:T(8,128)S(1)}, u32[]{:S(2)}, u32[]{:S(2)}) collective-permute-start(f32[1,16,32]{2,1,0:T(8,128)S(1)} %fusion.674), channel_id=1, source_target_pairs={{1,0},{2,1},{3,2},{4,3},{5,4},{6,5},{7,6},{8,7},{9,8},{10,9},{11,1... | collective-permute-start | bytes 6152 | tf_op jit(solution)/shard_map/ppermute | solution.py:22
  98.5 7.4 %all-to-all-start.1 = ((f32[32,1,512]{2,1,0:T(1,128)}), f32[32,1,512]{2,1,0:T(1,128)S(1)}, u32[]{:S(2)}, u32[]{:S(2)}) async-start(f32[32,1,512]{2,1,0:T(1,128)} %reshape.164), calls=%async_computation.1 | async-start | bytes 131072 | tf_op jit(solution)/shard_map/all_to_all | solution.py:31
  111.2 8.5 %all-to-all-start = ((f32[32,1,512]{2,1,0:T(1,128)}), f32[32,1,512]{2,1,0:T(1,128)S(1)}, u32[]{:S(2)}, u32[]{:S(2)}) async-start(f32[32,1,512]{2,1,0:T(1,128)} %reshape.162), calls=%async_computation | async-start | bytes 131072 | tf_op jit(solution)/shard_map/all_to_all | solution.py:31
  146.2 5.8 %collective-permute-start.12 = (f32[1,16,32]{2,1,0:T(8,128)S(1)}, f32[1,16,32]{2,1,0:T(8,128)S(1)}, u32[]{:S(2)}, u32[]{:S(2)}) collective-permute-start(f32[1,16,32]{2,1,0:T(8,128)S(1)} %dynamic-slice_add_fusion.1), channel_id=1, source_target_pairs={{1,0},{2,1},{3,2},{4,3},{5,4},{6,5},{7,6},{8,7},{9,8},{10,9},{11,1... | collective-permute-start | bytes 6152 | tf_op jit(solution)/shard_map/ppermute | solution.py:22
  155.4 7.5 %collective-permute-start.14 = (f32[1,16,32]{2,1,0:T(8,128)S(1)}, f32[1,16,32]{2,1,0:T(8,128)S(1)}, u32[]{:S(2)}, u32[]{:S(2)}) collective-permute-start(f32[1,16,32]{2,1,0:T(8,128)S(1)} %fusion.692), channel_id=1, source_target_pairs={{1,0},{2,1},{3,2},{4,3},{5,4},{6,5},{7,6},{8,7},{9,8},{10,9},{11,1... | collective-permute-start | bytes 6152 | tf_op jit(solution)/shard_map/ppermute | solution.py:22
  164.8 7.5 %collective-permute-start.16 = (f32[1,32,64]{2,1,0:T(8,128)S(1)}, f32[1,32,64]{2,1,0:T(8,128)S(1)}, u32[]{:S(2)}, u32[]{:S(2)}) collective-permute-start(f32[1,32,64]{2,1,0:T(8,128)S(1)} %get-tuple-element.35), channel_id=1, source_target_pairs={{1,0},{2,1},{3,2},{4,3},{5,4},{6,5},{7,6},{8,7},{9,8},{10,9},{11,1... | collective-permute-start | bytes 24584 | tf_op jit(solution)/shard_map/ppermute | solution.py:22
  174.2 7.0 %collective-permute-done.17 = f32[1,32,64]{2,1,0:T(8,128)S(1)} collective-permute-done((f32[1,32,64]{2,1,0:T(8,128)S(1)}, f32[1,32,64]{2,1,0:T(8,128)S(1)}, u32[]{:S(2)}, u32[]{:S(2)}) %collective-permute-start.17) | collective-permute-done | bytes 8224 | tf_op jit(solution)/shard_map/ppermute | solution.py:20
  196.2 6.9 %reshape.158 = f32[4,64,128]{2,1,0:T(8,128)S(1)} reshape(f32[2,2,32,2,64,2]{5,4,3,2,1,0:T(8,128)} %broadcast_in_dim.84) | data formatting | bytes 262144 | tf_op jit(solution)/shard_map/reshape | solution.py:65
  220.3 5.2 %collective-permute-done.23 = f32[1,64,128]{2,1,0:T(8,128)S(1)} collective-permute-done((f32[1,64,128]{2,1,0:T(8,128)S(1)}, f32[1,64,128]{2,1,0:T(8,128)S(1)}, u32[]{:S(2)}, u32[]{:S(2)}) %collective-permute-start.23) | collective-permute-done | bytes 32800 | tf_op jit(solution)/shard_map/ppermute | solution.py:20
  248.7 9.8 %reshape.159 = f32[2,2,32,2,64,2]{5,4,3,2,1,0:T(8,128)} reshape(f32[4,64,128]{2,1,0:T(8,128)S(1)} %fusion.47) | data formatting | bytes 262144 | tf_op jit(solution)/shard_map/reshape | solution.py:53
  287.1 7.2 %collective-permute-start.32 = (f32[1,16,32]{2,1,0:T(8,128)S(1)}, f32[1,16,32]{2,1,0:T(8,128)S(1)}, u32[]{:S(2)}, u32[]{:S(2)}) collective-permute-start(f32[1,16,32]{2,1,0:T(8,128)S(1)} %bitcast_divide_fusion), channel_id=1, source_target_pairs={{1,0},{2,1},{3,2},{4,3},{5,4},{6,5},{7,6},{8,7},{9,8},{10,9},{11,1... | collective-permute-start | bytes 6152 | tf_op jit(solution)/shard_map/ppermute | solution.py:22
  297.7 7.5 %collective-permute-start.34 = (f32[1,16,32]{2,1,0:T(8,128)S(1)}, f32[1,16,32]{2,1,0:T(8,128)S(1)}, u32[]{:S(2)}, u32[]{:S(2)}) collective-permute-start(f32[1,16,32]{2,1,0:T(8,128)S(1)} %fusion.712), channel_id=1, source_target_pairs={{1,0},{2,1},{3,2},{4,3},{5,4},{6,5},{7,6},{8,7},{9,8},{10,9},{11,1... | collective-permute-start | bytes 6152 | tf_op jit(solution)/shard_map/ppermute | solution.py:22
  306.9 15.4 %all_to_all.15 = f32[32,1,512]{2,1,0:T(1,128)S(1)} all-to-all(f32[32,1,512]{2,1,0:T(1,128)S(1)} %reshape.166), channel_id=1, replica_groups=mesh['tm'=8,'space'=32] {'space'}, dimensions={0} | all-to-all | bytes 131072 | tf_op jit(solution)/shard_map/all_to_all | solution.py:31
  340.4 6.7 %collective-permute-start.36 = (f32[1,16,32]{2,1,0:T(8,128)S(1)}, f32[1,16,32]{2,1,0:T(8,128)S(1)}, u32[]{:S(2)}, u32[]{:S(2)}) collective-permute-start(f32[1,16,32]{2,1,0:T(8,128)S(1)} %dynamic-slice_add_fusion), channel_id=1, source_target_pairs={{1,0},{2,1},{3,2},{4,3},{5,4},{6,5},{7,6},{8,7},{9,8},{10,9},{11,1... | collective-permute-start | bytes 6152 | tf_op jit(solution)/shard_map/ppermute | solution.py:22
  350.4 7.5 %collective-permute-start.38 = (f32[1,16,32]{2,1,0:T(8,128)S(1)}, f32[1,16,32]{2,1,0:T(8,128)S(1)}, u32[]{:S(2)}, u32[]{:S(2)}) collective-permute-start(f32[1,16,32]{2,1,0:T(8,128)S(1)} %fusion.730), channel_id=1, source_target_pairs={{1,0},{2,1},{3,2},{4,3},{5,4},{6,5},{7,6},{8,7},{9,8},{10,9},{11,1... | collective-permute-start | bytes 6152 | tf_op jit(solution)/shard_map/ppermute | solution.py:22
  359.8 7.5 %collective-permute-start.40 = (f32[1,32,64]{2,1,0:T(8,128)S(1)}, f32[1,32,64]{2,1,0:T(8,128)S(1)}, u32[]{:S(2)}, u32[]{:S(2)}) collective-permute-start(f32[1,32,64]{2,1,0:T(8,128)S(1)} %get-tuple-element.27), channel_id=1, source_target_pairs={{1,0},{2,1},{3,2},{4,3},{5,4},{6,5},{7,6},{8,7},{9,8},{10,9},{11,1... | collective-permute-start | bytes 24584 | tf_op jit(solution)/shard_map/ppermute | solution.py:22
  369.3 7.0 %collective-permute-done.41 = f32[1,32,64]{2,1,0:T(8,128)S(1)} collective-permute-done((f32[1,32,64]{2,1,0:T(8,128)S(1)}, f32[1,32,64]{2,1,0:T(8,128)S(1)}, u32[]{:S(2)}, u32[]{:S(2)}) %collective-permute-start.41) | collective-permute-done | bytes 8224 | tf_op jit(solution)/shard_map/ppermute | solution.py:20
  391.3 6.9 %reshape.161 = f32[4,64,128]{2,1,0:T(8,128)S(1)} reshape(f32[2,2,32,2,64,2]{5,4,3,2,1,0:T(8,128)} %broadcast_in_dim.93) | data formatting | bytes 262144 | tf_op jit(solution)/shard_map/reshape | solution.py:65
  (229 shorter events, 239.6 us)
Async XLA Ops:
  6.2 9.1 %collective-permute-start.1 = (f32[1,64,128]{2,1,0:T(8,128)S(1)}, f32[1,64,128]{2,1,0:T(8,128)S(1)}, u32[]{:S(2)}, u32[]{:S(2)}) collective-permute-start(f32[1,64,128]{2,1,0:T(8,128)S(1)} %get-tuple-element.24), channel_id=1, source_target_pairs={{0,1},{1,2},{2,3},{3,4},{4,5},{5,6},{6,7},{7,8},{8,9},{9,10},{10,1... | collective-permute-start | bytes 98312 | tf_op jit(solution)/shard_map/ppermute | solution.py:20
  16.4 20.6 %collective-permute-start.2 = (f32[1,64,128]{2,1,0:T(8,128)S(1)}, f32[1,64,128]{2,1,0:T(8,128)S(1)}, u32[]{:S(2)}, u32[]{:S(2)}) collective-permute-start(f32[1,64,128]{2,1,0:T(8,128)S(1)} %get-tuple-element.21), channel_id=1, source_target_pairs={{1,0},{2,1},{3,2},{4,3},{5,4},{6,5},{7,6},{8,7},{9,8},{10,9},{11,1... | collective-permute-start | bytes 98312 | tf_op jit(solution)/shard_map/ppermute | solution.py:22
  18.3 18.6 %collective-permute-start.3 = (f32[1,64,128]{2,1,0:T(8,128)S(1)}, f32[1,64,128]{2,1,0:T(8,128)S(1)}, u32[]{:S(2)}, u32[]{:S(2)}) collective-permute-start(f32[1,64,128]{2,1,0:T(8,128)S(1)} %get-tuple-element.22), channel_id=1, source_target_pairs={{0,1},{1,2},{2,3},{3,4},{4,5},{5,6},{6,7},{7,8},{8,9},{9,10},{10,1... | collective-permute-start | bytes 98312 | tf_op jit(solution)/shard_map/ppermute | solution.py:20
  56.2 9.0 %collective-permute-start.5 = (f32[1,32,64]{2,1,0:T(8,128)S(1)}, f32[1,32,64]{2,1,0:T(8,128)S(1)}, u32[]{:S(2)}, u32[]{:S(2)}) collective-permute-start(f32[1,32,64]{2,1,0:T(8,128)S(1)} %get-tuple-element.40), channel_id=1, source_target_pairs={{0,1},{1,2},{2,3},{3,4},{4,5},{5,6},{6,7},{7,8},{8,9},{9,10},{10,1... | collective-permute-start | bytes 24584 | tf_op jit(solution)/shard_map/ppermute | solution.py:20
  67.2 9.0 %collective-permute-start.7 = (f32[1,32,64]{2,1,0:T(8,128)S(1)}, f32[1,32,64]{2,1,0:T(8,128)S(1)}, u32[]{:S(2)}, u32[]{:S(2)}) collective-permute-start(f32[1,32,64]{2,1,0:T(8,128)S(1)} %get-tuple-element.38), channel_id=1, source_target_pairs={{0,1},{1,2},{2,3},{3,4},{4,5},{5,6},{6,7},{7,8},{8,9},{9,10},{10,1... | collective-permute-start | bytes 24584 | tf_op jit(solution)/shard_map/ppermute | solution.py:20
  77.6 9.2 %collective-permute-start.9 = (f32[1,16,32]{2,1,0:T(8,128)S(1)}, f32[1,16,32]{2,1,0:T(8,128)S(1)}, u32[]{:S(2)}, u32[]{:S(2)}) collective-permute-start(f32[1,16,32]{2,1,0:T(8,128)S(1)} %bitcast_divide_fusion.1), channel_id=1, source_target_pairs={{0,1},{1,2},{2,3},{3,4},{4,5},{5,6},{6,7},{7,8},{8,9},{9,10},{10,1... | collective-permute-start | bytes 6152 | tf_op jit(solution)/shard_map/ppermute | solution.py:20
  88.2 17.7 %collective-permute-start.11 = (f32[1,16,32]{2,1,0:T(8,128)S(1)}, f32[1,16,32]{2,1,0:T(8,128)S(1)}, u32[]{:S(2)}, u32[]{:S(2)}) collective-permute-start(f32[1,16,32]{2,1,0:T(8,128)S(1)} %fusion.674), channel_id=1, source_target_pairs={{0,1},{1,2},{2,3},{3,4},{4,5},{5,6},{6,7},{7,8},{8,9},{9,10},{10,1... | collective-permute-start | bytes 6152 | tf_op jit(solution)/shard_map/ppermute | solution.py:20
  90.2 15.7 %collective-permute-start.10 = (f32[1,16,32]{2,1,0:T(8,128)S(1)}, f32[1,16,32]{2,1,0:T(8,128)S(1)}, u32[]{:S(2)}, u32[]{:S(2)}) collective-permute-start(f32[1,16,32]{2,1,0:T(8,128)S(1)} %fusion.674), channel_id=1, source_target_pairs={{1,0},{2,1},{3,2},{4,3},{5,4},{6,5},{7,6},{8,7},{9,8},{10,9},{11,1... | collective-permute-start | bytes 6152 | tf_op jit(solution)/shard_map/ppermute | solution.py:22
  98.5 12.7 %all-to-all-start.1 = ((f32[32,1,512]{2,1,0:T(1,128)}), f32[32,1,512]{2,1,0:T(1,128)S(1)}, u32[]{:S(2)}, u32[]{:S(2)}) async-start(f32[32,1,512]{2,1,0:T(1,128)} %reshape.164), calls=%async_computation.1 | async-start | bytes 131072 | tf_op jit(solution)/shard_map/all_to_all | solution.py:31
  111.2 16.0 %all-to-all-start = ((f32[32,1,512]{2,1,0:T(1,128)}), f32[32,1,512]{2,1,0:T(1,128)S(1)}, u32[]{:S(2)}, u32[]{:S(2)}) async-start(f32[32,1,512]{2,1,0:T(1,128)} %reshape.162), calls=%async_computation | async-start | bytes 131072 | tf_op jit(solution)/shard_map/all_to_all | solution.py:31
  142.9 9.2 %collective-permute-start.13 = (f32[1,16,32]{2,1,0:T(8,128)S(1)}, f32[1,16,32]{2,1,0:T(8,128)S(1)}, u32[]{:S(2)}, u32[]{:S(2)}) collective-permute-start(f32[1,16,32]{2,1,0:T(8,128)S(1)} %dynamic-slice_add_fusion.1), channel_id=1, source_target_pairs={{0,1},{1,2},{2,3},{3,4},{4,5},{5,6},{6,7},{7,8},{8,9},{9,10},{10,1... | collective-permute-start | bytes 6152 | tf_op jit(solution)/shard_map/ppermute | solution.py:20
  153.5 9.4 %collective-permute-start.15 = (f32[1,16,32]{2,1,0:T(8,128)S(1)}, f32[1,16,32]{2,1,0:T(8,128)S(1)}, u32[]{:S(2)}, u32[]{:S(2)}) collective-permute-start(f32[1,16,32]{2,1,0:T(8,128)S(1)} %fusion.692), channel_id=1, source_target_pairs={{0,1},{1,2},{2,3},{3,4},{4,5},{5,6},{6,7},{7,8},{8,9},{9,10},{10,1... | collective-permute-start | bytes 6152 | tf_op jit(solution)/shard_map/ppermute | solution.py:20
  164.8 9.5 %collective-permute-start.16 = (f32[1,32,64]{2,1,0:T(8,128)S(1)}, f32[1,32,64]{2,1,0:T(8,128)S(1)}, u32[]{:S(2)}, u32[]{:S(2)}) collective-permute-start(f32[1,32,64]{2,1,0:T(8,128)S(1)} %get-tuple-element.35), channel_id=1, source_target_pairs={{1,0},{2,1},{3,2},{4,3},{5,4},{6,5},{7,6},{8,7},{9,8},{10,9},{11,1... | collective-permute-start | bytes 24584 | tf_op jit(solution)/shard_map/ppermute | solution.py:22
  205.1 9.1 %collective-permute-start.21 = (f32[1,64,128]{2,1,0:T(8,128)S(1)}, f32[1,64,128]{2,1,0:T(8,128)S(1)}, u32[]{:S(2)}, u32[]{:S(2)}) collective-permute-start(f32[1,64,128]{2,1,0:T(8,128)S(1)} %get-tuple-element.20), channel_id=1, source_target_pairs={{0,1},{1,2},{2,3},{3,4},{4,5},{5,6},{6,7},{7,8},{8,9},{9,10},{10,1... | collective-permute-start | bytes 98312 | tf_op jit(solution)/shard_map/ppermute | solution.py:20
  216.3 9.1 %collective-permute-start.23 = (f32[1,64,128]{2,1,0:T(8,128)S(1)}, f32[1,64,128]{2,1,0:T(8,128)S(1)}, u32[]{:S(2)}, u32[]{:S(2)}) collective-permute-start(f32[1,64,128]{2,1,0:T(8,128)S(1)} %get-tuple-element.18), channel_id=1, source_target_pairs={{0,1},{1,2},{2,3},{3,4},{4,5},{5,6},{6,7},{7,8},{8,9},{9,10},{10,1... | collective-permute-start | bytes 98312 | tf_op jit(solution)/shard_map/ppermute | solution.py:20
  228.2 9.1 %collective-permute-start.25 = (f32[1,64,128]{2,1,0:T(8,128)S(1)}, f32[1,64,128]{2,1,0:T(8,128)S(1)}, u32[]{:S(2)}, u32[]{:S(2)}) collective-permute-start(f32[1,64,128]{2,1,0:T(8,128)S(1)} %get-tuple-element.16), channel_id=1, source_target_pairs={{0,1},{1,2},{2,3},{3,4},{4,5},{5,6},{6,7},{7,8},{8,9},{9,10},{10,1... | collective-permute-start | bytes 98312 | tf_op jit(solution)/shard_map/ppermute | solution.py:20
  239.4 9.1 %collective-permute-start.27 = (f32[1,64,128]{2,1,0:T(8,128)S(1)}, f32[1,64,128]{2,1,0:T(8,128)S(1)}, u32[]{:S(2)}, u32[]{:S(2)}) collective-permute-start(f32[1,64,128]{2,1,0:T(8,128)S(1)} %get-tuple-element.14), channel_id=1, source_target_pairs={{0,1},{1,2},{2,3},{3,4},{4,5},{5,6},{6,7},{7,8},{8,9},{9,10},{10,1... | collective-permute-start | bytes 98312 | tf_op jit(solution)/shard_map/ppermute | solution.py:20
  285.2 9.2 %collective-permute-start.33 = (f32[1,16,32]{2,1,0:T(8,128)S(1)}, f32[1,16,32]{2,1,0:T(8,128)S(1)}, u32[]{:S(2)}, u32[]{:S(2)}) collective-permute-start(f32[1,16,32]{2,1,0:T(8,128)S(1)} %bitcast_divide_fusion), channel_id=1, source_target_pairs={{0,1},{1,2},{2,3},{3,4},{4,5},{5,6},{6,7},{7,8},{8,9},{9,10},{10,1... | collective-permute-start | bytes 6152 | tf_op jit(solution)/shard_map/ppermute | solution.py:20
  295.8 9.4 %collective-permute-start.35 = (f32[1,16,32]{2,1,0:T(8,128)S(1)}, f32[1,16,32]{2,1,0:T(8,128)S(1)}, u32[]{:S(2)}, u32[]{:S(2)}) collective-permute-start(f32[1,16,32]{2,1,0:T(8,128)S(1)} %fusion.712), channel_id=1, source_target_pairs={{0,1},{1,2},{2,3},{3,4},{4,5},{5,6},{6,7},{7,8},{8,9},{9,10},{10,1... | collective-permute-start | bytes 6152 | tf_op jit(solution)/shard_map/ppermute | solution.py:20
  337.9 9.2 %collective-permute-start.37 = (f32[1,16,32]{2,1,0:T(8,128)S(1)}, f32[1,16,32]{2,1,0:T(8,128)S(1)}, u32[]{:S(2)}, u32[]{:S(2)}) collective-permute-start(f32[1,16,32]{2,1,0:T(8,128)S(1)} %dynamic-slice_add_fusion), channel_id=1, source_target_pairs={{0,1},{1,2},{2,3},{3,4},{4,5},{5,6},{6,7},{7,8},{8,9},{9,10},{10,1... | collective-permute-start | bytes 6152 | tf_op jit(solution)/shard_map/ppermute | solution.py:20
  348.5 9.4 %collective-permute-start.39 = (f32[1,16,32]{2,1,0:T(8,128)S(1)}, f32[1,16,32]{2,1,0:T(8,128)S(1)}, u32[]{:S(2)}, u32[]{:S(2)}) collective-permute-start(f32[1,16,32]{2,1,0:T(8,128)S(1)} %fusion.730), channel_id=1, source_target_pairs={{0,1},{1,2},{2,3},{3,4},{4,5},{5,6},{6,7},{7,8},{8,9},{9,10},{10,1... | collective-permute-start | bytes 6152 | tf_op jit(solution)/shard_map/ppermute | solution.py:20
  359.8 9.5 %collective-permute-start.40 = (f32[1,32,64]{2,1,0:T(8,128)S(1)}, f32[1,32,64]{2,1,0:T(8,128)S(1)}, u32[]{:S(2)}, u32[]{:S(2)}) collective-permute-start(f32[1,32,64]{2,1,0:T(8,128)S(1)} %get-tuple-element.27), channel_id=1, source_target_pairs={{1,0},{2,1},{3,2},{4,3},{5,4},{6,5},{7,6},{8,7},{9,8},{10,9},{11,1... | collective-permute-start | bytes 24584 | tf_op jit(solution)/shard_map/ppermute | solution.py:22
  400.1 9.1 %collective-permute-start.45 = (f32[1,64,128]{2,1,0:T(8,128)S(1)}, f32[1,64,128]{2,1,0:T(8,128)S(1)}, u32[]{:S(2)}, u32[]{:S(2)}) collective-permute-start(f32[1,64,128]{2,1,0:T(8,128)S(1)} %get-tuple-element.12), channel_id=1, source_target_pairs={{0,1},{1,2},{2,3},{3,4},{4,5},{5,6},{6,7},{7,8},{8,9},{9,10},{10,1... | collective-permute-start | bytes 98312 | tf_op jit(solution)/shard_map/ppermute | solution.py:20
  411.4 9.1 %collective-permute-start.47 = (f32[1,64,128]{2,1,0:T(8,128)S(1)}, f32[1,64,128]{2,1,0:T(8,128)S(1)}, u32[]{:S(2)}, u32[]{:S(2)}) collective-permute-start(f32[1,64,128]{2,1,0:T(8,128)S(1)} %get-tuple-element.10), channel_id=1, source_target_pairs={{0,1},{1,2},{2,3},{3,4},{4,5},{5,6},{6,7},{7,8},{8,9},{9,10},{10,1... | collective-permute-start | bytes 98312 | tf_op jit(solution)/shard_map/ppermute | solution.py:20
  (30 other events, 288.6 us)
where the time goes:
time: 430 us; the launch traced here: 428 us
  starting transfers between devices  195 us (45%)
  waiting for transfers between devices  102 us (24%)
  local copies, waits for them, and re-layouts  79.5 us (18%)
  other arithmetic  33.3 us (8%)
  blocking collectives  15.4 us (4%)
    ppermute x24, starting transfers between devices, with_halo(): lax.ppermute(head, axis, [((i + 1) % count, i) for i in range(ends)])  105 us
    ppermute x24, waiting for transfers between devices, with_halo(): lax.ppermute(tail, axis, [(i, (i + 1) % count) for i in range(ends)])  84.2 us
    ppermute x24, starting transfers between devices, with_halo(): lax.ppermute(tail, axis, [(i, (i + 1) % count) for i in range(ends)])  72.4 us
    reshape x3, local copies, waits for them, and re-layouts, mean_to_rougher(): field.reshape(extent_layout[0] // 2, 2, extent_layout[1] // 2, 2, extent_...  30.1 us
    reshape x4, local copies, waits for them, and re-layouts, lift_to_finer(): grown.reshape(2 * extent_layout[0], 2 * extent_layout[1], 2 * extent_layo...  21.1 us
    reduce_sum x11, other arithmetic, mean_to_rougher(): return blocks.mean(axis=(1, 3, 5))  20.3 us
    all_to_all x2, starting transfers between devices, copy_for_each(): lax.all_to_all(jnp.broadcast_to(x[None], (peers, *x.shape)), axis, 0, 0,...  15.9 us
    all_to_all x1, blocking collectives, copy_for_each(): lax.all_to_all(jnp.broadcast_to(x[None], (peers, *x.shape)), axis, 0, 0,...  15.4 us
  transfers between devices with their start and end apart: 51, of which 24 were waited for; matrix products, arithmetic and copies ran while one was open for 6% of the time, Pallas kernels for 0%

commit v1 on v0

v1 whole, which is shorter than its diff:
```python
import jax
import jax.numpy as jnp
from jax import lax
from jax.experimental import pallas as pl
from jax.experimental.pallas import tpu as pltpu
from jax.sharding import PartitionSpec as P

COARSE_SWEEPS = 24
NY, NX = 64, 128
SLABS = 32
SPANS = 8
DEPTH = 4
OMEGA = 0.8
F32 = jnp.float32
VMEM = pl.BlockSpec(memory_space=pltpu.VMEM)


def f32(*shape):
    return jax.ShapeDtypeStruct(shape, F32)


def call(body, outs, scratch, *args):
    return pl.pallas_call(
        body,
        out_shape=outs,
        in_specs=[VMEM] * len(args),
        out_specs=tuple(VMEM for _ in outs),
        scratch_shapes=[pltpu.VMEM(s, F32) for s in scratch],
    )(*args)


def dot(a, b):
    return jnp.dot(a, b, precision=lax.Precision.HIGHEST, preferred_element_type=F32)


def iota(shape, axis):
    return lax.broadcasted_iota(jnp.int32, shape, axis)


def picks(test, scale):
    i, j = iota((128, 128), 0), iota((128, 128), 1)
    return jnp.where(test(i, j), jnp.float32(scale), jnp.float32(0.0))


def around_plane(c, below, above):
    row, lane = iota(c.shape, 0), iota(c.shape, 1)
    total = below + above
    total = total + jnp.where(lane > 0, pltpu.roll(c, 1, 1), 0.0)
    total = total + jnp.where(lane < NX - 1, pltpu.roll(c, NX - 1, 1), 0.0)
    total = total + jnp.where(row > 0, pltpu.roll(c, 1, 0), 0.0)
    return total + jnp.where(row < NY - 1, pltpu.roll(c, NY - 1, 0), 0.0)


def around_block(c, below, above):
    row, lane = iota(c.shape, 0), iota(c.shape, 1)
    col = lane & 63
    total = pltpu.roll(c + jnp.where(lane < 64, above, below), 64, 1)
    total = total + jnp.where(col > 0, pltpu.roll(c, 1, 1), 0.0)
    total = total + jnp.where(col < 63, pltpu.roll(c, 127, 1), 0.0)
    total = total + jnp.where(row > 0, pltpu.roll(c, 1, 0), 0.0)
    return total + jnp.where(row < 31, pltpu.roll(c, 31, 0), 0.0)


def around_low(v):
    row, lane = iota(v.shape, 0), iota(v.shape, 1)
    y, x = row & 15, lane & 31
    ends = iota((16, 128), 1)
    below = jnp.where(ends >= 32, pltpu.roll(v[112:], 32, 1), 0.0)
    above = jnp.where(ends < 96, pltpu.roll(v[:16], 96, 1), 0.0)
    total = jnp.concatenate([below, v[:112]], 0) + jnp.concatenate([v[16:], above], 0)
    total = total + jnp.where(x > 0, pltpu.roll(v, 1, 1), 0.0)
    total = total + jnp.where(x < 31, pltpu.roll(v, 127, 1), 0.0)
    total = total + jnp.where(y > 0, pltpu.roll(v, 1, 0), 0.0)
    return total + jnp.where(y < 15, pltpu.roll(v, 127, 0), 0.0)


def coarsest(b3, w3):
    lane, row = iota((8, 128), 1), iota((8, 128), 0)
    x = lane & 15
    steps = []
    for k in range(4):
        w = w3[8 * k : 8 * k + 8]
        wh = 0.125 * w
        steps.append(
            (
                w * b3[8 * k : 8 * k + 8],
                wh,
                jnp.where(x > 0, wh, 0.0),
                jnp.where(x < 15, wh, 0.0),
                jnp.where(row > 0, wh, 0.0),
                jnp.where(row < 7, wh, 0.0),
            )
        )
    inside = lane < 64

    def sweep(_, v):
        below = jnp.where(inside, pltpu.roll(v[3], 16, 1), 0.0)
        above = jnp.where(inside, pltpu.roll(v[0], 112, 1), 0.0)
        line = (below, *v, above)
        new = []
        for k in range(4):
            wb, wh, left, right, up, down = steps[k]
            c = v[k]
            t = (0.2 * c + wb) + wh * (line[k] + line[k + 2])
            s = up * pltpu.roll(c, 1, 0) + down * pltpu.roll(c, 7, 0)
            e = left * pltpu.roll(c, 1, 1) + right * pltpu.roll(c, 127, 1)
            new.append((t + s) + e)
        return tuple(new)

    v = lax.fori_loop(0, COARSE_SWEEPS - 1, sweep, tuple(s[0] for s in steps), unroll=True)
    return jnp.concatenate(v, 0)


def pack_body(u, src, cap, b_out, up, dn):
    for p in range(DEPTH):
        c = cap[p]
        b = c * u[0, p] + src[0, 0, p]
        b_out[p] = b
        if p > 0:
            up[p - 1] = b
            up[p + 2] = c
        if p < 3:
            dn[p] = b
            dn[p + 3] = c


def row_pairs(ref, start, count):
    return ref[pl.ds(start, count, stride=2), :] + ref[pl.ds(start + 1, count, stride=2), :]


def fine_down(first, b_own, cap, lo, hi, w, xs, send, ys, rs):
    lo_pick = picks(lambda i, j: (i >> 1) == j, 0.125)
    hi_pick = picks(lambda i, j: (i >> 1) + 64 == j, 0.125)

    def b(p):
        return lo[p + 3] if p < 0 else (b_own[p] if p < DEPTH else hi[p - DEPTH])

    if first:
        s = lax.axis_index("space")
        for p in range(-3, 7):
            c = lo[p + 6] if p < 0 else (cap[p] if p < DEPTH else hi[p - 1])
            v = OMEGA / (c + 6.0)
            if p < 0:
                v = jnp.where(s > 0, v, 0.0)
            if p >= DEPTH:
                v = jnp.where(s < SLABS - 1, v, 0.0)
            w[p + 3] = v
    for p in range(-3, 7):
        ys[p + 3] = w[p + 3] * b(p)
    for p in range(-2, 6):
        i = p + 3
        xs[p + 2] = 1.2 * ys[i] + w[i] * around_plane(ys[i], ys[i - 1], ys[i + 1])
    for half in range(2):
        total = None
        for p in (2 * half, 2 * half + 1):
            i = p + 2
            r = b(p) - (cap[p] + 6.0) * xs[i] + around_plane(xs[i], xs[i - 1], xs[i + 1])
            total = r if total is None else total + r
        rs[pl.ds(64 * half, 64), :] = total
        if first:
            rs[pl.ds(128 + 64 * half, 64), :] = cap[2 * half] + cap[2 * half + 1]
    parts = [(row_pairs(rs, 0, 32), row_pairs(rs, 64, 32))]
    if first:
        parts.append((row_pairs(rs, 128, 32), row_pairs(rs, 192, 32)))
    low = jnp.concatenate([a for a, _ in parts], 0)
    high = jnp.concatenate([a for _, a in parts], 0)
    block = dot(low, lo_pick) + dot(high, hi_pick)
    for peer in range(SLABS):
        send[peer] = block


def first_down_body(b_own, cap, lo, hi, w, xs, send, ys, rs):
    fine_down(True, b_own, cap, lo, hi, w, xs, send, ys, rs)


def next_down_body(b_own, cap, lo, hi, w, xs, send, ys, rs):
    fine_down(False, b_own, cap, lo, hi, w, xs, send, ys, rs)


CHUNK = 8


def over_blocks(body):
    @pl.loop(0, SLABS // CHUNK)
    def _(c):
        for k in range(CHUNK):
            body(c * CHUNK + k)


def to_low(rows):
    total = None
    for q in range(4):
        pick = picks(lambda i, j: ((j >> 5) == q) & (((i & 63) >> 1) == (j & 31)), 0.125)
        part = dot(row_pairs(rows, 256 * q, 128), pick)
        total = part if total is None else total + part
    return total


def to_coarsest(v, t3):
    for k in range(4):
        t3[pl.ds(16 * k, 16), :] = v[32 * k : 32 * k + 16] + v[32 * k + 16 : 32 * k + 32]
    pick = picks(lambda i, j: (j < 64) & ((i >> 5) == (j >> 4)) & (((i & 31) >> 1) == (j & 15)), 0.125)
    return dot(row_pairs(t3, 0, 32), pick)


def from_coarsest(v, t3):
    pick = picks(lambda i, j: (i < 64) & ((j >> 5) == (i >> 4)) & (((j & 31) >> 1) == (i & 15)), 1.0)
    v = dot(v, pick)
    t3[pl.ds(0, 32, stride=2), :] = v
    t3[pl.ds(1, 32, stride=2), :] = v
    parts = []
    for k in range(4):
        block = t3[pl.ds(16 * k, 16), :]
        parts += [block, block]
    return jnp.concatenate(parts, 0)


def coarse_levels(got, caps, first, w1, w2, d2, w3, y1, x1, r1, f1, t3):
    zero = jnp.zeros((32, 128), F32)
    for i in (0, 1, 34, 35):
        y1[i] = zero
        x1[i] = zero
        f1[pl.ds(32 * i, 32), :] = zero
        if first:
            w1[i] = zero

    if first:

        def caps_in(s):
            c = caps[s, pl.ds(32, 32), :]
            w = OMEGA / (c + 3.0)
            w1[s + 2] = w
            y1[s + 2] = w * got[s, pl.ds(0, 32), :]
            r1[pl.ds(pl.multiple_of(s * 32, 32), 32), :] = c

        over_blocks(caps_in)
        c2 = to_low(r1)
        d2[...] = c2 + 1.5
        w2[...] = OMEGA / (c2 + 1.5)
        w3[...] = OMEGA / (to_coarsest(c2, t3) + 0.75)
    else:

        def right_side(s):
            y1[s + 2] = w1[s + 2] * got[s, pl.ds(0, 32), :]

        over_blocks(right_side)

    def sweep(s):
        y = y1[s + 2]
        x1[s + 2] = 1.2 * y + 0.5 * w1[s + 2] * around_block(y, y1[s + 1], y1[s + 3])

    over_blocks(sweep)

    def residual(s):
        x = x1[s + 2]
        r = got[s, pl.ds(0, 32), :] - (caps[s, pl.ds(32, 32), :] + 3.0) * x
        r = r + 0.5 * around_block(x, x1[s + 1], x1[s + 3])
        r1[pl.ds(pl.multiple_of(s * 32, 32), 32), :] = r

    over_blocks(residual)
    b = to_low(r1)
    w, d = w2[...], d2[...]
    y = w * b
    x = 1.2 * y + 0.25 * w * around_low(y)
    r = b - d * x + 0.25 * around_low(x)
    x = x + from_coarsest(coarsest(to_coarsest(r, t3), w3[...]), t3)
    for _ in range(2):
        x = 0.2 * x + y + 0.25 * w * around_low(x)
    for q in range(4):
        pick = picks(lambda i, j: ((i >> 5) == q) & ((i & 31) == ((j & 63) >> 1)), 1.0)
        v = dot(x, pick)
        f1[pl.ds(64 + 256 * q, 128, stride=2), :] = v
        f1[pl.ds(65 + 256 * q, 128, stride=2), :] = v


def fine_up(b_own, lo, hi, w, xs, w1, y1, x1, f1, xa, xb, f0, x0, x9, out):
    s = lax.axis_index("space")
    for j in range(5):
        rows = pl.ds(pl.multiple_of((s + j) * 32, 32), 32)
        xa[j] = x1[s + j] + f1[rows, :]
    xb[0] = jnp.zeros((32, 128), F32)
    xb[4] = jnp.zeros((32, 128), F32)
    for old, new in ((xa, xb), (xb, xa)):
        for j in (1, 2, 3):
            c = old[j]
            t = around_block(c, old[j - 1], old[j + 1])
            new[j] = 0.2 * c + y1[s + j] + 0.5 * w1[s + j] * t
    one, two, three = xa[1], xa[2], xa[3]
    low = dot(jnp.concatenate([two, three], 0), picks(lambda i, j: i == (j >> 1), 1.0))
    high = dot(jnp.concatenate([one, two], 0), picks(lambda i, j: i == (j >> 1) + 64, 1.0))
    for q, v in enumerate((high[:32], low[:32], high[32:], low[32:])):
        f0[pl.ds(64 * q, 32, stride=2), :] = v
        f0[pl.ds(64 * q + 1, 32, stride=2), :] = v
    for i in range(8):
        x0[i] = xs[i] + f0[pl.ds(64 * (i // 2), 64), :]
    for p in range(-1, 5):
        i = p + 2
        b = lo[2] if p < 0 else (b_own[p] if p < DEPTH else hi[0])
        c = x0[i]
        x9[p + 1] = 0.2 * c + w[p + 3] * (b + around_plane(c, x0[i - 1], x0[i + 1]))
    for p in range(DEPTH):
        c = x9[p + 1]
        u = 0.2 * c + w[p + 3] * (b_own[p] + around_plane(c, x9[p], x9[p + 2]))
        out(p, u)


def first_up_body(
    got, b_own, lo, hi, w, xs, cap, src, u_out, b_out, up, dn, w1, w2, d2, w3, *work
):
    y1, x1, r1, f1, t3, xa, xb, f0, x0, x9 = work
    coarse_levels(got, got, True, w1, w2, d2, w3, y1, x1, r1, f1, t3)

    def out(p, u):
        u_out[0, p] = u
        b = cap[p] * u + src[0, 1, p]
        b_out[p] = b
        if p > 0:
            up[p - 1] = b
        if p < 3:
            dn[p] = b

    fine_up(b_own, lo, hi, w, xs, w1, y1, x1, f1, xa, xb, f0, x0, x9, out)


def next_up_body(got, caps, b_own, lo, hi, w, xs, w1, w2, d2, w3, start, u_out, *work):
    y1, x1, r1, f1, t3, xa, xb, f0, x0, x9 = work
    coarse_levels(got, caps, False, w1, w2, d2, w3, y1, x1, r1, f1, t3)
    keep = lax.axis_index("tm") == 0

    def out(p, u):
        u_out[0, p] = jnp.where(keep, start[0, p], u)

    fine_up(b_own, lo, hi, w, xs, w1, y1, x1, f1, xa, xb, f0, x0, x9, out)


WORK = [
    (36, 32, 128),
    (36, 32, 128),
    (1024, 128),
    (36 * 32, 128),
    (64, 128),
    (5, 32, 128),
    (5, 32, 128),
    (256, 128),
    (8, NY, NX),
    (6, NY, NX),
]


def moved(x, spans, slabs):
    pairs = []
    for t in range(SPANS):
        for s in range(SLABS):
            pairs.append((t * SLABS + s, (t + spans) % SPANS * SLABS + (s + slabs) % SLABS))
    return lax.ppermute(x, ("tm", "space"), pairs)


def shards(u0, src, cap):
    plane = (NY, NX)
    b, up, dn = call(
        pack_body, (f32(4, *plane), f32(6, *plane), f32(6, *plane)), [], u0, src, cap
    )
    lo, hi = moved(up, 0, 1), moved(dn, 0, -1)
    w, xs, send = call(
        first_down_body,
        (f32(10, *plane), f32(8, *plane), f32(SLABS, 64, 128)),
        [(10, *plane), (256, 128)],
        b,
        cap,
        lo,
        hi,
    )
    got = lax.all_to_all(send, "space", 0, 0, tiled=True)
    fpoint, b, up, dn, w1, w2, d2, w3 = call(
        first_up_body,
        (
            f32(1, 4, *plane),
            f32(4, *plane),
            f32(3, *plane),
            f32(3, *plane),
            f32(36, 32, 128),
            f32(128, 128),
            f32(128, 128),
            f32(32, 128),
        ),
        WORK,
        got,
        b,
        lo,
        hi,
        w,
        xs,
        cap,
        src,
    )
    b, lo, hi = moved(b, 1, 0), moved(up, 1, 1), moved(dn, 1, -1)
    xs, send = call(
        lambda b, cap, lo, hi, w, xs, send, ys, rs: next_down_body(
            b, cap, lo, hi, w, xs, send, ys, rs
        ),
        (f32(8, *plane), f32(SLABS, 32, 128)),
        [(10, *plane), (256, 128)],
        b,
        cap,
        lo,
        hi,
        w,
    )
    caps = got
    got = lax.all_to_all(send, "space", 0, 0, tiled=True)
    (updated,) = call(
        next_up_body,
        (f32(1, 4, *plane),),
        WORK,
        got,
        caps,
        b,
        lo,
        hi,
        w,
        xs,
        w1,
        w2,
        d2,
        w3,
        u0,
    )
    return fpoint, updated


def solution(mesh):
    in_specs = (
        P("tm", "space", None, None),
        P("tm", None, "space", None, None),
        P("space", None, None),
    )
    out_specs = (P("tm", "space", None, None), P("tm", "space", None, None))
    return jax.shard_map(shards, mesh=mesh, in_specs=in_specs, out_specs=out_specs, check_vma=False)
```

time: 430 us -> 111 us (0.26)
  the two profiles are of different devices: /device:TPU:130 before, /device:TPU:4 now
where the time goes in v1:
time: 111 us; the launch traced here: 110 us
  blocking collectives  60.6 us (55%)
  Pallas kernels  24.4 us (22%)
  starting transfers between devices  14.1 us (13%)
  waiting for transfers between devices  8.42 us (8%)
  local copies, waits for them, and re-layouts  2.02 us (2%)
    all_to_all x2, blocking collectives, shards(): got = lax.all_to_all(send, 'space', 0, 0, tiled=True)  60.6 us
    pallas_call x5, Pallas kernels, call(): pl.pallas_call(body, out_shape=outs, in_specs=[VMEM] * len(args), out_spe...  24.4 us
    ppermute x5, starting transfers between devices, moved(): return lax.ppermute(x, ('tm', 'space'), pairs)  14.1 us
    ppermute x5, waiting for transfers between devices, moved(): return lax.ppermute(x, ('tm', 'space'), pairs)  8.42 us
  transfers between devices with their start and end apart: 5, of which 2 were waited for; matrix products, arithmetic and copies ran while one was open for 0% of the time, Pallas kernels for 0%

profile of v1, /device:TPU:4, one launch (start us, length us, event | category | flops | bytes accessed | tf_op | source)
XLA Modules:
  0.0 110.2 jit_solution(16444867763831826459)
XLA Ops:
  0.6 1.9 %shard_map.50 = (f32[4,64,128]{2,1,0:T(8,128)}, f32[6,64,128]{2,1,0:T(8,128)}, f32[6,64,128]{2,1,0:T(8,128)}) custom-call(f32[1,4,64,128]{3,2,1,0:T(8,128)} %start.1, f32[1,2,4,64,128]{4,3,2,1,0:T(8,128)} %src.3, f32[4,64,128]{2,1,0:T(8,128)} %cap.7), custom_call_target="tpu_custom_call" | custom-call | tf_op jit(solution)/shard_map/pallas_call | solution.py:23
  2.5 1.6 %collective-permute-start = (f32[6,64,128]{2,1,0:T(8,128)}, f32[6,64,128]{2,1,0:T(8,128)S(1)}, u32[]{:S(2)}, u32[]{:S(2)}) collective-permute-start(f32[6,64,128]{2,1,0:T(8,128)} %get-tuple-element.19), channel_id=1, source_target_pairs={{0,1},{1,2},{2,3},{3,4},{4,5},{5,6},{6,7},{7,8},{8,9},{9,10},{10,1... | collective-permute-start | bytes 589832 | tf_op jit(solution)/shard_map/ppermute | solution.py:355
  4.1 6.7 %collective-permute-start.1 = (f32[6,64,128]{2,1,0:T(8,128)}, f32[6,64,128]{2,1,0:T(8,128)S(1)}, u32[]{:S(2)}, u32[]{:S(2)}) collective-permute-start(f32[6,64,128]{2,1,0:T(8,128)} %get-tuple-element.20), channel_id=1, source_target_pairs={{0,31},{1,0},{2,1},{3,2},{4,3},{5,4},{6,5},{7,6},{8,7},{9,8},{10,9... | collective-permute-start | bytes 589832 | tf_op jit(solution)/shard_map/ppermute | solution.py:355
  10.8 5.1 %collective-permute-done.lo = f32[6,64,128]{2,1,0:T(8,128)S(1)} collective-permute-done((f32[6,64,128]{2,1,0:T(8,128)}, f32[6,64,128]{2,1,0:T(8,128)S(1)}, u32[]{:S(2)}, u32[]{:S(2)}) %collective-permute-start) | collective-permute-done | bytes 196640 | tf_op jit(solution)/shard_map/ppermute | solution.py:355
  15.9 0.0 collective-permute-done.1.hi
  15.9 0.0 copy-start.1
  15.9 0.7 copy-done
  16.6 0.1 copy-done.1
  16.6 2.8 %shard_map.51 = (f32[10,64,128]{2,1,0:T(8,128)}, f32[8,64,128]{2,1,0:T(8,128)}, f32[32,64,128]{2,1,0:T(8,128)}) custom-call(f32[4,64,128]{2,1,0:T(8,128)} %get-tuple-element.18.b_own, f32[4,64,128]{2,1,0:T(8,128)} %cap.7, f32[6,64,128]{2,1,0:T(8,128)} %copy-done, f32[6,64,128]{2,1,0:T(8,128)} %copy-done.1), custom_call_target="tpu_custom_call" | custom-call | tf_op jit(solution)/shard_map/pallas_call | solution.py:23
  19.4 35.0 %all_to_all.10.got.caps = f32[32,64,128]{2,1,0:T(8,128)} all-to-all(f32[32,64,128]{2,1,0:T(8,128)} %get-tuple-element.21), channel_id=1, replica_groups=mesh['tm'=8,'space'=32] {'space'}, dimensions={0} | all-to-all | bytes 2097152 | tf_op jit(solution)/shard_map/all_to_all | solution.py:373
  54.4 9.0 %shard_map.52 = (f32[1,4,64,128]{3,2,1,0:T(8,128)}, f32[4,64,128]{2,1,0:T(8,128)}, f32[3,64,128]{2,1,0:T(8,128)}, f32[3,64,128]{2,1,0:T(8,128)}, f32[36,32,128]{...) custom-call(f32[32,64,128]{2,1,0:T(8,128)} %all_to_all.10.got.caps, ...), custom_call_target="tpu_custom_call" | custom-call | tf_op jit(solution)/shard_map/pallas_call | solution.py:23
  63.4 0.0 collective-permute-start.2
  63.4 2.7 %collective-permute-start.3 = (f32[3,64,128]{2,1,0:T(8,128)}, f32[3,64,128]{2,1,0:T(8,128)S(1)}, u32[]{:S(2)}, u32[]{:S(2)}) collective-permute-start(f32[3,64,128]{2,1,0:T(8,128)} %get-tuple-element.26), channel_id=1, source_target_pairs={{0,33},{1,34},{2,35},{3,36},{4,37},{5,38},{6,39},{7,40},{8,41},{9,... | collective-permute-start | bytes 294920 | tf_op jit(solution)/shard_map/ppermute | solution.py:355
  66.1 3.1 %collective-permute-start.4 = (f32[3,64,128]{2,1,0:T(8,128)}, f32[3,64,128]{2,1,0:T(8,128)S(1)}, u32[]{:S(2)}, u32[]{:S(2)}) collective-permute-start(f32[3,64,128]{2,1,0:T(8,128)} %get-tuple-element.27), channel_id=1, source_target_pairs={{0,63},{1,32},{2,33},{3,34},{4,35},{5,36},{6,37},{7,38},{8,39},{9,... | collective-permute-start | bytes 294920 | tf_op jit(solution)/shard_map/ppermute | solution.py:355
  69.2 3.3 %collective-permute-done.3.lo = f32[3,64,128]{2,1,0:T(8,128)S(1)} collective-permute-done((f32[3,64,128]{2,1,0:T(8,128)}, f32[3,64,128]{2,1,0:T(8,128)S(1)}, u32[]{:S(2)}, u32[]{:S(2)}) %collective-permute-start.3) | collective-permute-done | bytes 98336 | tf_op jit(solution)/shard_map/ppermute | solution.py:355
  72.5 0.0 copy-start.3
  72.5 0.0 collective-permute-done.4.hi
  72.5 0.0 collective-permute-done.2.b.b_own
  72.5 0.6 copy-done.3
  73.1 0.0 copy-done.4
  73.2 0.6 copy-done.2
  73.8 2.6 %shard_map.53 = (f32[8,64,128]{2,1,0:T(8,128)}, f32[32,32,128]{2,1,0:T(8,128)}) custom-call(f32[4,64,128]{2,1,0:T(8,128)} %copy-done.2, f32[4,64,128]{2,1,0:T(8,128)} %cap.7, f32[3,64,128]{2,1,0:T(8,128)} %copy-done.3, f32[3,64,128]{2,1,0:T(8,128)} %copy-done.4, f32[10,64,128]{2,1,0:T(8,128)} %get-tuple-element.22.w), custom_call_target="tpu_custom_call" | custom-call | tf_op jit(solution)/shard_map/pallas_call | solution.py:23
  76.4 25.6 %all_to_all.11.got = f32[32,32,128]{2,1,0:T(8,128)} all-to-all(f32[32,32,128]{2,1,0:T(8,128)} %get-tuple-element.28), channel_id=1, replica_groups=mesh['tm'=8,'space'=32] {'space'}, dimensions={0} | all-to-all | bytes 1048576 | tf_op jit(solution)/shard_map/all_to_all | solution.py:410
  102.0 8.2 %shard_map.54 = f32[1,4,64,128]{3,2,1,0:T(8,128)} custom-call(f32[32,32,128]{2,1,0:T(8,128)} %all_to_all.11.got, f32[32,64,128]{2,1,0:T(8,128)} %all_to_all.10.got.caps, f32[4,64,128]{2,1,0:T(8,128)} %copy-done.2, f32[3,64,128]{2,1,0:T(8,128)} %copy-done.3, f32[3,64,128]{2,1,0:T(8,128)} %copy-done.4, f32[10,64,128]{2,1,0:T(8,128)} %get-tuple-element.22.w, ...), custom_call_target="tpu_custom_call" | custom-call | tf_op jit(solution)/shard_map/pallas_call | solution.py:23
  (3 shorter events, 0.0 us)
Async XLA Ops:
  2.5 13.4 %collective-permute-start = (f32[6,64,128]{2,1,0:T(8,128)}, f32[6,64,128]{2,1,0:T(8,128)S(1)}, u32[]{:S(2)}, u32[]{:S(2)}) collective-permute-start(f32[6,64,128]{2,1,0:T(8,128)} %get-tuple-element.19), channel_id=1, source_target_pairs={{0,1},{1,2},{2,3},{3,4},{4,5},{5,6},{6,7},{7,8},{8,9},{9,10},{10,1... | collective-permute-start | bytes 589832 | tf_op jit(solution)/shard_map/ppermute | solution.py:355
  4.1 11.8 %collective-permute-start.1 = (f32[6,64,128]{2,1,0:T(8,128)}, f32[6,64,128]{2,1,0:T(8,128)S(1)}, u32[]{:S(2)}, u32[]{:S(2)}) collective-permute-start(f32[6,64,128]{2,1,0:T(8,128)} %get-tuple-element.20), channel_id=1, source_target_pairs={{0,31},{1,0},{2,1},{3,2},{4,3},{5,4},{6,5},{7,6},{8,7},{9,8},{10,9... | collective-permute-start | bytes 589832 | tf_op jit(solution)/shard_map/ppermute | solution.py:355
  15.9 0.7 copy-start
  15.9 0.7 copy-start.1
  63.4 9.1 %collective-permute-start.2 = (f32[4,64,128]{2,1,0:T(8,128)}, f32[4,64,128]{2,1,0:T(8,128)S(1)}, u32[]{:S(2)}, u32[]{:S(2)}) collective-permute-start(f32[4,64,128]{2,1,0:T(8,128)} %get-tuple-element.25), channel_id=1, source_target_pairs={{0,32},{1,33},{2,34},{3,35},{4,36},{5,37},{6,38},{7,39},{8,40},{9,... | collective-permute-start | bytes 393224 | tf_op jit(solution)/shard_map/ppermute | solution.py:355
  63.4 9.1 %collective-permute-start.3 = (f32[3,64,128]{2,1,0:T(8,128)}, f32[3,64,128]{2,1,0:T(8,128)S(1)}, u32[]{:S(2)}, u32[]{:S(2)}) collective-permute-start(f32[3,64,128]{2,1,0:T(8,128)} %get-tuple-element.26), channel_id=1, source_target_pairs={{0,33},{1,34},{2,35},{3,36},{4,37},{5,38},{6,39},{7,40},{8,41},{9,... | collective-permute-start | bytes 294920 | tf_op jit(solution)/shard_map/ppermute | solution.py:355
  66.1 6.4 %collective-permute-start.4 = (f32[3,64,128]{2,1,0:T(8,128)}, f32[3,64,128]{2,1,0:T(8,128)S(1)}, u32[]{:S(2)}, u32[]{:S(2)}) collective-permute-start(f32[3,64,128]{2,1,0:T(8,128)} %get-tuple-element.27), channel_id=1, source_target_pairs={{0,63},{1,32},{2,33},{3,34},{4,35},{5,36},{6,37},{7,38},{8,39},{9,... | collective-permute-start | bytes 294920 | tf_op jit(solution)/shard_map/ppermute | solution.py:355
  72.5 0.6 copy-start.3
  72.5 0.7 copy-start.4
  73.2 0.6 copy-start.2

commit v2 on v1

--- a/solution.py
+++ b/solution.py
@@ -26,6 +26,7 @@
         in_specs=[VMEM] * len(args),
         out_specs=tuple(VMEM for _ in outs),
         scratch_shapes=[pltpu.VMEM(s, F32) for s in scratch],
+        compiler_params=pltpu.CompilerParams(vmem_limit_bytes=16 << 20),
     )(*args)
 
 

time: 111 us -> 101 us (0.910)
  Pallas kernels: 24.4 us -> 14.5 us
    pallas_call x5, Pallas kernels: 24.4 us -> 14.5 us  [call(): pl.pallas_call(body, out_shape=outs, in_specs=[VMEM] * len(args), out_spe...]
  transfers between devices with their start and end apart: 5 -> 5, of which waited for: 2 -> 3; matrix products, arithmetic and copies ran while one was open for 0% -> 0% of each run, Pallas kernels for 0% -> 0%
where the time goes in v2:
time: 101 us; the launch traced here: 100 us
  blocking collectives  60.3 us (60%)
  Pallas kernels  14.5 us (14%)
  starting transfers between devices  14.2 us (14%)
  waiting for transfers between devices  7.9 us (8%)
  local copies, waits for them, and re-layouts  2.76 us (3%)
    all_to_all x2, blocking collectives, shards(): got = lax.all_to_all(send, 'space', 0, 0, tiled=True)  60.3 us
    pallas_call x5, Pallas kernels, call(): pl.pallas_call(body, out_shape=outs, in_specs=[VMEM] * len(args), out_spe...  14.5 us
    ppermute x5, starting transfers between devices, moved(): return lax.ppermute(x, ('tm', 'space'), pairs)  14.2 us
    ppermute x5, waiting for transfers between devices, moved(): return lax.ppermute(x, ('tm', 'space'), pairs)  7.9 us
    unnamed x10, local copies, waits for them, and re-layouts  2.76 us
  transfers between devices with their start and end apart: 5, of which 3 were waited for; matrix products, arithmetic and copies ran while one was open for 0% of the time, Pallas kernels for 0%

profile of v2, /device:TPU:4, one launch (start us, length us, event | category | flops | bytes accessed | tf_op | source)
XLA Modules:
  0.0 100.3 jit_solution(13996678236984791091)
XLA Ops:
  0.6 0.0 copy-start
  0.6 0.9 copy-done
  1.5 0.0 copy-start.2
  1.5 0.9 copy-done.2
  2.5 0.9 copy-done.4
  3.4 1.7 %collective-permute-start = (f32[6,64,128]{2,1,0:T(8,128)S(1)}, f32[6,64,128]{2,1,0:T(8,128)S(1)}, u32[]{:S(2)}, u32[]{:S(2)}) collective-permute-start(f32[6,64,128]{2,1,0:T(8,128)S(1)} %get-tuple-element.19), channel_id=1, source_target_pairs={{0,1},{1,2},{2,3},{3,4},{4,5},{5,6},{6,7},{7,8},{8,9},{9,10},{10,1... | collective-permute-start | bytes 589832 | tf_op jit(solution)/shard_map/ppermute | solution.py:356
  5.1 6.8 %collective-permute-start.1 = (f32[6,64,128]{2,1,0:T(8,128)S(1)}, f32[6,64,128]{2,1,0:T(8,128)S(1)}, u32[]{:S(2)}, u32[]{:S(2)}) collective-permute-start(f32[6,64,128]{2,1,0:T(8,128)S(1)} %get-tuple-element.20), channel_id=1, source_target_pairs={{0,31},{1,0},{2,1},{3,2},{4,3},{5,4},{6,5},{7,6},{8,7},{9,8},{10,9... | collective-permute-start | bytes 589832 | tf_op jit(solution)/shard_map/ppermute | solution.py:356
  11.9 4.8 %collective-permute-done.lo = f32[6,64,128]{2,1,0:T(8,128)S(1)} collective-permute-done((f32[6,64,128]{2,1,0:T(8,128)S(1)}, f32[6,64,128]{2,1,0:T(8,128)S(1)}, u32[]{:S(2)}, u32[]{:S(2)}) %collective-permute-start) | collective-permute-done | bytes 196640 | tf_op jit(solution)/shard_map/ppermute | solution.py:356
  16.7 0.0 collective-permute-done.1.hi
  16.7 0.0 copy-done.1
  16.7 0.6 shard_map.51
  17.4 0.0 copy-start.3
  17.4 34.8 %all_to_all.10.got.caps = f32[32,64,128]{2,1,0:T(8,128)S(1)} all-to-all(f32[32,64,128]{2,1,0:T(8,128)S(1)} %get-tuple-element.21), channel_id=1, replica_groups=mesh['tm'=8,'space'=32] {'space'}, dimensions={0} | all-to-all | bytes 2097152 | tf_op jit(solution)/shard_map/all_to_all | solution.py:374
  52.2 0.0 copy-done.3
  52.2 7.0 %shard_map.52 = (f32[1,4,64,128]{3,2,1,0:T(8,128)}, f32[4,64,128]{2,1,0:T(8,128)S(1)}, f32[3,64,128]{2,1,0:T(8,128)S(1)}, f32[3,64,128]{2,1,0:T(8,128)S(1)}, f32...) custom-call(f32[32,64,128]{2,1,0:T(8,128)S(1)} %all_to_all.10.got.caps, ...), custom_call_target="tpu_custom_call" | custom-call | tf_op jit(solution)/shard_map/pallas_call | solution.py:23
  59.2 0.0 collective-permute-start.2
  59.2 2.7 %collective-permute-start.3 = (f32[3,64,128]{2,1,0:T(8,128)S(1)}, f32[3,64,128]{2,1,0:T(8,128)S(1)}, u32[]{:S(2)}, u32[]{:S(2)}) collective-permute-start(f32[3,64,128]{2,1,0:T(8,128)S(1)} %get-tuple-element.26), channel_id=1, source_target_pairs={{0,33},{1,34},{2,35},{3,36},{4,37},{5,38},{6,39},{7,40},{8,41},{9,... | collective-permute-start | bytes 294920 | tf_op jit(solution)/shard_map/ppermute | solution.py:356
  61.9 3.0 %collective-permute-start.4 = (f32[3,64,128]{2,1,0:T(8,128)S(1)}, f32[3,64,128]{2,1,0:T(8,128)S(1)}, u32[]{:S(2)}, u32[]{:S(2)}) collective-permute-start(f32[3,64,128]{2,1,0:T(8,128)S(1)} %get-tuple-element.27), channel_id=1, source_target_pairs={{0,63},{1,32},{2,33},{3,34},{4,35},{5,36},{6,37},{7,38},{8,39},{9,... | collective-permute-start | bytes 294920 | tf_op jit(solution)/shard_map/ppermute | solution.py:356
  64.9 3.0 %collective-permute-done.3.lo = f32[3,64,128]{2,1,0:T(8,128)S(1)} collective-permute-done((f32[3,64,128]{2,1,0:T(8,128)S(1)}, f32[3,64,128]{2,1,0:T(8,128)S(1)}, u32[]{:S(2)}, u32[]{:S(2)}) %collective-permute-start.3) | collective-permute-done | bytes 98336 | tf_op jit(solution)/shard_map/ppermute | solution.py:356
  67.9 0.1 collective-permute-done.4.hi
  68.0 0.0 collective-permute-done.2.b.b_own
  68.0 0.6 shard_map.53
  68.6 25.5 %all_to_all.11.got = f32[32,32,128]{2,1,0:T(8,128)S(1)} all-to-all(f32[32,32,128]{2,1,0:T(8,128)S(1)} %get-tuple-element.28), channel_id=1, replica_groups=mesh['tm'=8,'space'=32] {'space'}, dimensions={0} | all-to-all | bytes 1048576 | tf_op jit(solution)/shard_map/all_to_all | solution.py:411
  94.0 6.3 %shard_map.54 = f32[1,4,64,128]{3,2,1,0:T(8,128)} custom-call(f32[32,32,128]{2,1,0:T(8,128)S(1)} %all_to_all.11.got, f32[32,64,128]{2,1,0:T(8,128)S(1)} %all_to_all.10.got.caps, f32[4,64,128]{2,1,0:T(8,128)S(1)} %collective-permute-done.2.b.b_own, f32[3,64,128]{2,1,0:T(8,128)S(1)} %collective-permute-done.3.lo, f32[3,64,128]{2,1,0:T(8,128)S(1)} %collective-permute-done.4.hi, ...), custom_call_target="tpu_custom_call" | custom-call | tf_op jit(solution)/shard_map/pallas_call | solution.py:23
  (3 shorter events, 0.0 us)
Async XLA Ops:
  0.6 0.9 copy-start
  1.5 0.9 copy-start.2
  2.5 0.9 copy-start.4
  3.4 13.3 %copy-start.1 = (f32[4,64,128]{2,1,0:T(8,128)S(1)}, f32[4,64,128]{2,1,0:T(8,128)}, u32[]{:S(2)}) copy-start(f32[4,64,128]{2,1,0:T(8,128)} %cap.7) | copy-start | bytes 393220
  3.4 13.3 %collective-permute-start = (f32[6,64,128]{2,1,0:T(8,128)S(1)}, f32[6,64,128]{2,1,0:T(8,128)S(1)}, u32[]{:S(2)}, u32[]{:S(2)}) collective-permute-start(f32[6,64,128]{2,1,0:T(8,128)S(1)} %get-tuple-element.19), channel_id=1, source_target_pairs={{0,1},{1,2},{2,3},{3,4},{4,5},{5,6},{6,7},{7,8},{8,9},{9,10},{10,1... | collective-permute-start | bytes 589832 | tf_op jit(solution)/shard_map/ppermute | solution.py:356
  5.1 11.6 %collective-permute-start.1 = (f32[6,64,128]{2,1,0:T(8,128)S(1)}, f32[6,64,128]{2,1,0:T(8,128)S(1)}, u32[]{:S(2)}, u32[]{:S(2)}) collective-permute-start(f32[6,64,128]{2,1,0:T(8,128)S(1)} %get-tuple-element.20), channel_id=1, source_target_pairs={{0,31},{1,0},{2,1},{3,2},{4,3},{5,4},{6,5},{7,6},{8,7},{9,8},{10,9... | collective-permute-start | bytes 589832 | tf_op jit(solution)/shard_map/ppermute | solution.py:356
  17.4 34.9 %copy-start.3 = (f32[1,2,4,64,128]{4,3,2,1,0:T(8,128)S(1)}, f32[1,2,4,64,128]{4,3,2,1,0:T(8,128)}, u32[]{:S(2)}) copy-start(f32[1,2,4,64,128]{4,3,2,1,0:T(8,128)} %src.3) | copy-start | bytes 786436
  59.2 8.8 %collective-permute-start.2 = (f32[4,64,128]{2,1,0:T(8,128)S(1)}, f32[4,64,128]{2,1,0:T(8,128)S(1)}, u32[]{:S(2)}, u32[]{:S(2)}) collective-permute-start(f32[4,64,128]{2,1,0:T(8,128)S(1)} %get-tuple-element.25), channel_id=1, source_target_pairs={{0,32},{1,33},{2,34},{3,35},{4,36},{5,37},{6,38},{7,39},{8,40},{9,... | collective-permute-start | bytes 393224 | tf_op jit(solution)/shard_map/ppermute | solution.py:356
  59.2 8.7 %collective-permute-start.3 = (f32[3,64,128]{2,1,0:T(8,128)S(1)}, f32[3,64,128]{2,1,0:T(8,128)S(1)}, u32[]{:S(2)}, u32[]{:S(2)}) collective-permute-start(f32[3,64,128]{2,1,0:T(8,128)S(1)} %get-tuple-element.26), channel_id=1, source_target_pairs={{0,33},{1,34},{2,35},{3,36},{4,37},{5,38},{6,39},{7,40},{8,41},{9,... | collective-permute-start | bytes 294920 | tf_op jit(solution)/shard_map/ppermute | solution.py:356
  61.9 6.1 %collective-permute-start.4 = (f32[3,64,128]{2,1,0:T(8,128)S(1)}, f32[3,64,128]{2,1,0:T(8,128)S(1)}, u32[]{:S(2)}, u32[]{:S(2)}) collective-permute-start(f32[3,64,128]{2,1,0:T(8,128)S(1)} %get-tuple-element.27), channel_id=1, source_target_pairs={{0,63},{1,32},{2,33},{3,34},{4,35},{5,36},{6,37},{7,38},{8,39},{9,... | collective-permute-start | bytes 294920 | tf_op jit(solution)/shard_map/ppermute | solution.py:356

commit v3 on v2

v3 whole, which is shorter than its diff:
```python
import jax
import jax.numpy as jnp
from jax import lax
from jax.experimental import pallas as pl
from jax.experimental.pallas import tpu as pltpu
from jax.sharding import PartitionSpec as P

COARSE_SWEEPS = 24
NY, NX = 64, 128
SLABS = 32
SPANS = 8
DEPTH = 4
OMEGA = 0.8
F32 = jnp.float32
VMEM = pl.BlockSpec(memory_space=pltpu.VMEM)


def f32(*shape):
    return jax.ShapeDtypeStruct(shape, F32)


def call(body, outs, scratch, *args):
    return pl.pallas_call(
        body,
        out_shape=outs,
        in_specs=[VMEM] * len(args),
        out_specs=tuple(VMEM for _ in outs),
        scratch_shapes=[pltpu.VMEM(s, F32) for s in scratch],
        compiler_params=pltpu.CompilerParams(vmem_limit_bytes=16 << 20),
    )(*args)


def dot(a, b):
    return jnp.dot(a, b, precision=lax.Precision.HIGHEST, preferred_element_type=F32)


def iota(shape, axis):
    return lax.broadcasted_iota(jnp.int32, shape, axis)


def picks(test, scale):
    i, j = iota((128, 128), 0), iota((128, 128), 1)
    return jnp.where(test(i, j), jnp.float32(scale), jnp.float32(0.0))


def around_plane(c, below, above):
    row, lane = iota(c.shape, 0), iota(c.shape, 1)
    total = below + above
    total = total + jnp.where(lane > 0, pltpu.roll(c, 1, 1), 0.0)
    total = total + jnp.where(lane < NX - 1, pltpu.roll(c, NX - 1, 1), 0.0)
    total = total + jnp.where(row > 0, pltpu.roll(c, 1, 0), 0.0)
    return total + jnp.where(row < NY - 1, pltpu.roll(c, NY - 1, 0), 0.0)


def around_block(c, below, above):
    row, lane = iota(c.shape, 0), iota(c.shape, 1)
    col = lane & 63
    total = pltpu.roll(c + jnp.where(lane < 64, above, below), 64, 1)
    total = total + jnp.where(col > 0, pltpu.roll(c, 1, 1), 0.0)
    total = total + jnp.where(col < 63, pltpu.roll(c, 127, 1), 0.0)
    total = total + jnp.where(row > 0, pltpu.roll(c, 1, 0), 0.0)
    return total + jnp.where(row < 31, pltpu.roll(c, 31, 0), 0.0)


def around_low(v):
    row, lane = iota(v.shape, 0), iota(v.shape, 1)
    y, x = row & 15, lane & 31
    ends = iota((16, 128), 1)
    below = jnp.where(ends >= 32, pltpu.roll(v[112:], 32, 1), 0.0)
    above = jnp.where(ends < 96, pltpu.roll(v[:16], 96, 1), 0.0)
    total = jnp.concatenate([below, v[:112]], 0) + jnp.concatenate([v[16:], above], 0)
    total = total + jnp.where(x > 0, pltpu.roll(v, 1, 1), 0.0)
    total = total + jnp.where(x < 31, pltpu.roll(v, 127, 1), 0.0)
    total = total + jnp.where(y > 0, pltpu.roll(v, 1, 0), 0.0)
    return total + jnp.where(y < 15, pltpu.roll(v, 127, 0), 0.0)


def coarsest(b3, w3):
    lane, row = iota((8, 128), 1), iota((8, 128), 0)
    x = lane & 15
    steps = []
    for k in range(4):
        w = w3[8 * k : 8 * k + 8]
        wh = 0.125 * w
        steps.append(
            (
                w * b3[8 * k : 8 * k + 8],
                wh,
                jnp.where(x > 0, wh, 0.0),
                jnp.where(x < 15, wh, 0.0),
                jnp.where(row > 0, wh, 0.0),
                jnp.where(row < 7, wh, 0.0),
            )
        )
    inside = lane < 64

    def sweep(_, v):
        below = jnp.where(inside, pltpu.roll(v[3], 16, 1), 0.0)
        above = jnp.where(inside, pltpu.roll(v[0], 112, 1), 0.0)
        line = (below, *v, above)
        new = []
        for k in range(4):
            wb, wh, left, right, up, down = steps[k]
            c = v[k]
            t = (0.2 * c + wb) + wh * (line[k] + line[k + 2])
            s = up * pltpu.roll(c, 1, 0) + down * pltpu.roll(c, 7, 0)
            e = left * pltpu.roll(c, 1, 1) + right * pltpu.roll(c, 127, 1)
            new.append((t + s) + e)
        return tuple(new)

    v = lax.fori_loop(0, COARSE_SWEEPS - 1, sweep, tuple(s[0] for s in steps), unroll=True)
    return jnp.concatenate(v, 0)


def pack_body(u, src, cap, b_out, up, dn):
    for p in range(DEPTH):
        c = cap[p]
        b = c * u[0, p] + src[0, 0, p]
        b_out[p] = b
        ends, i = (dn, p) if p < 2 else (up, p - 2)
        ends[i] = b
        ends[i + 2] = c


def row_pairs(ref, start, count):
    return ref[pl.ds(start, count, stride=2), :] + ref[pl.ds(start + 1, count, stride=2), :]


def block_sweep(y, w, below, above):
    return 1.2 * y + 0.5 * w * around_block(y, below, above)


def fine_down(first, b_own, cap, lo, hi, w, w1, c1, xs, send, up, dn, block, ys, rs):
    lane = iota((32, 128), 1)
    lo_pick = picks(lambda i, j: (i >> 1) == j, 0.125)
    hi_pick = picks(lambda i, j: (i >> 1) + 64 == j, 0.125)

    def b(p):
        return lo[p + 2] if p < 0 else (b_own[p] if p < DEPTH else hi[p - DEPTH])

    def c(p):
        return lo[p + 4] if p < 0 else (cap[p] if p < DEPTH else hi[p - 2])

    if first:
        s = lax.axis_index("space")
        for p in range(-2, 6):
            v = OMEGA / (c(p) + 6.0)
            if p < 0:
                v = jnp.where(s > 0, v, 0.0)
            if p >= DEPTH:
                v = jnp.where(s < SLABS - 1, v, 0.0)
            w[p + 2] = v
    for p in range(-2, 6):
        ys[p + 2] = w[p + 2] * b(p)
    for p in range(-1, 5):
        i = p + 2
        xs[p + 1] = 1.2 * ys[i] + w[i] * around_plane(ys[i], ys[i - 1], ys[i + 1])
    for half in range(2):
        total = None
        for p in (2 * half, 2 * half + 1):
            i = p + 1
            r = b(p) - (cap[p] + 6.0) * xs[i] + around_plane(xs[i], xs[i - 1], xs[i + 1])
            total = r if total is None else total + r
        rs[pl.ds(64 * half, 64), :] = total
    if first:
        for k, p in enumerate((0, 2, 4, -2)):
            rs[pl.ds(128 + 64 * k, 64), :] = c(p) + c(p + 1)
    low, high = [row_pairs(rs, 0, 32)], [row_pairs(rs, 64, 32)]
    if first:
        low += [row_pairs(rs, 128, 32), row_pairs(rs, 256, 32)]
        high += [row_pairs(rs, 192, 32), row_pairs(rs, 320, 32)]
    blocks = dot(jnp.concatenate(low, 0), lo_pick) + dot(jnp.concatenate(high, 0), hi_pick)
    b1 = blocks[:32]
    if first:
        c1[0], c1[1] = blocks[32:64], blocks[64:]
        wide = OMEGA / (blocks[64:] + 3.0)
        w1[0] = jnp.where((lane >= 64) & (s > 0), wide, 0.0)
        w1[1] = OMEGA / (blocks[32:64] + 3.0)
        w1[2] = jnp.where((lane < 64) & (s < SLABS - 1), wide, 0.0)
    rows = 64 if first else 32
    block[...] = blocks[:rows]
    up[pl.ds(0, rows), :] = blocks[:rows]
    dn[pl.ds(0, rows), :] = blocks[:rows]
    up[pl.ds(rows, 64), :] = xs[3]
    dn[pl.ds(rows, 64), :] = xs[2]

    zero = jnp.zeros((32, 128), F32)
    y = w1[1] * b1
    x = [
        block_sweep(zero, w1[0], zero, y),
        block_sweep(y, w1[1], zero, zero),
        block_sweep(zero, w1[2], y, zero),
    ]
    own, beside = c1[0] + 3.0, c1[1] + 3.0
    r = [
        0.5 * around_block(x[0], zero, x[1]) - beside * x[0],
        b1 - own * x[1] + 0.5 * around_block(x[1], x[0], x[2]),
        0.5 * around_block(x[2], x[1], zero) - beside * x[2],
        c1[0],
    ]
    for k in range(4):
        rs[pl.ds(32 * k, 32), :] = r[k]
    low = dot(row_pairs(rs, 0, 64), picks(lambda i, j: ((i & 63) >> 1) == (j & 31), 0.125))
    group = iota((16, 128), 1) >> 5
    message = low[48:]
    for k in range(3):
        message = jnp.where(group == k, low[16 * k : 16 * k + 16], message)
    for peer in range(SLABS):
        send[peer] = message


def first_down_body(b_own, cap, lo, hi, *rest):
    fine_down(True, b_own, cap, lo, hi, *rest)


def next_down_body(*refs):
    fine_down(False, *refs)


def spread(v):
    v = v + pltpu.roll(v, 64, 1)
    return v + pltpu.roll(v, 32, 1)


def to_coarsest(v, t3):
    for k in range(4):
        t3[pl.ds(16 * k, 16), :] = v[32 * k : 32 * k + 16] + v[32 * k + 16 : 32 * k + 32]
    pick = picks(lambda i, j: (j < 64) & ((i >> 5) == (j >> 4)) & (((i & 31) >> 1) == (j & 15)), 0.125)
    return dot(row_pairs(t3, 0, 32), pick)


def from_coarsest(v, t3):
    pick = picks(lambda i, j: (i < 64) & ((j >> 5) == (i >> 4)) & (((j & 31) >> 1) == (i & 15)), 1.0)
    v = dot(v, pick)
    t3[pl.ds(0, 32, stride=2), :] = v
    t3[pl.ds(1, 32, stride=2), :] = v
    parts = []
    for k in range(4):
        block = t3[pl.ds(16 * k, 16), :]
        parts += [block, block]
    return jnp.concatenate(parts, 0)


def low_levels(got, first, w2, d2, w3, x2, t3):
    group = iota((16, 128), 1) >> 5
    parts, caps = [], []
    for zl in range(8):
        total, cap = None, None
        for zh in range(4):
            z = 8 * zh + zl
            v = jnp.where(group == 1, got[z], 0.0)
            if z + 1 < SLABS:
                v = jnp.where(group == 0, got[z + 1], v)
            if z > 0:
                v = jnp.where(group == 2, got[z - 1], v)
            v = spread(v)
            total = v if total is None else jnp.where(group == zh, v, total)
            if first:
                v = spread(jnp.where(group == 3, got[z], 0.0))
                cap = v if cap is None else jnp.where(group == zh, v, cap)
        parts.append(total)
        caps.append(cap)
    b = jnp.concatenate(parts, 0)
    if first:
        c2 = jnp.concatenate(caps, 0)
        d2[...] = c2 + 1.5
        w2[...] = OMEGA / (c2 + 1.5)
        w3[...] = OMEGA / (to_coarsest(c2, t3) + 0.75)
    w, d = w2[...], d2[...]
    y = w * b
    x = 1.2 * y + 0.25 * w * around_low(y)
    r = b - d * x + 0.25 * around_low(x)
    x = x + from_coarsest(coarsest(to_coarsest(r, t3), w3[...]), t3)
    for _ in range(2):
        x = 0.2 * x + y + 0.25 * w * around_low(x)
    x2[...] = x


def fine_up(got, near, first, b_own, lo, hi, w, xs, w1, w2, d2, w3, work, out):
    x2, t3, f1, y1, xa, xb, f0, x0, x9 = work
    low_levels(got, first, w2, d2, w3, x2, t3)
    s = lax.axis_index("space")
    lo2, lo1, block, hi1, hi2 = near
    for j, ref in enumerate(near):
        if first:
            v = OMEGA / (ref[pl.ds(32, 32), :] + 3.0)
            z = s + (j - 2)
            w1[j] = jnp.where((z >= 0) & (z < SLABS), v, 0.0)
        y1[j] = w1[j] * ref[pl.ds(0, 32), :]
    zero = jnp.zeros((32, 128), F32)
    group = iota((16, 128), 1) >> 5
    parts = []
    for j in range(5):
        z = s + (j - 2)
        v = x2[pl.ds(pl.multiple_of((z & 7) * 16, 16), 16), :]
        parts.append(spread(jnp.where(group == (z >> 3), v, 0.0)))
    pick = picks(lambda i, j: i == ((j & 63) >> 1), 1.0)
    v = dot(jnp.concatenate(parts, 0), pick)
    f1[pl.ds(0, 80, stride=2), :] = v
    f1[pl.ds(1, 80, stride=2), :] = v
    for j in range(5):
        below = y1[j - 1] if j > 0 else zero
        above = y1[j + 1] if j < 4 else zero
        xa[j] = block_sweep(y1[j], w1[j], below, above) + f1[pl.ds(32 * j, 32), :]
    xb[0] = zero
    xb[4] = zero
    for old, new in ((xa, xb), (xb, xa)):
        for j in (1, 2, 3):
            c = old[j]
            t = around_block(c, old[j - 1], old[j + 1])
            new[j] = 0.2 * c + y1[j] + 0.5 * w1[j] * t
    one, two, three = xa[1], xa[2], xa[3]
    low = dot(jnp.concatenate([two, three], 0), picks(lambda i, j: i == (j >> 1), 1.0))
    high = dot(jnp.concatenate([one, two], 0), picks(lambda i, j: i == (j >> 1) + 64, 1.0))
    for q, v in enumerate((high[:32], low[:32], high[32:], low[32:])):
        f0[pl.ds(64 * q, 32, stride=2), :] = v
        f0[pl.ds(64 * q + 1, 32, stride=2), :] = v
    rows = 64 if first else 32
    far_below = jnp.where(s > 0, lo1[pl.ds(rows, 64), :], 0.0)
    far_above = jnp.where(s < SLABS - 1, hi1[pl.ds(rows, 64), :], 0.0)
    for i in range(8):
        v = far_below if i == 0 else (far_above if i == 7 else xs[i - 1])
        x0[i] = v + f0[pl.ds(64 * (i // 2), 64), :]
    for p in range(-1, 5):
        i = p + 2
        b = lo[1] if p < 0 else (b_own[p] if p < DEPTH else hi[0])
        c = x0[i]
        x9[p + 1] = 0.2 * c + w[i] * (b + around_plane(c, x0[i - 1], x0[i + 1]))
    for p in range(DEPTH):
        c = x9[p + 1]
        u = 0.2 * c + w[p + 2] * (b_own[p] + around_plane(c, x9[p], x9[p + 2]))
        out(p, u)


def first_up_body(
    got, lo2, lo1, block, hi1, hi2, b_own, lo, hi, w, xs, cap, src,
    u_out, b_out, up, dn, w1, w2, d2, w3, *work
):
    def out(p, u):
        u_out[0, p] = u
        b = cap[p] * u + src[0, 1, p]
        b_out[p] = b
        ends, i = (dn, p) if p < 2 else (up, p - 2)
        ends[i] = b

    near = (lo2, lo1, block, hi1, hi2)
    fine_up(got, near, True, b_own, lo, hi, w, xs, w1, w2, d2, w3, work, out)


def next_up_body(
    got, lo2, lo1, block, hi1, hi2, b_own, lo, hi, w, xs, w1, w2, d2, w3, start, u_out, *work
):
    keep = lax.axis_index("tm") == 0

    def out(p, u):
        u_out[0, p] = jnp.where(keep, start[0, p], u)

    near = (lo2, lo1, block, hi1, hi2)
    fine_up(got, near, False, b_own, lo, hi, w, xs, w1, w2, d2, w3, work, out)


WORK = [
    (128, 128),
    (64, 128),
    (160, 128),
    (5, 32, 128),
    (5, 32, 128),
    (5, 32, 128),
    (256, 128),
    (8, NY, NX),
    (6, NY, NX),
]
DOWN_WORK = [(8, NY, NX), (384, 128)]
PLANE = (NY, NX)
MESSAGE = f32(SLABS, 16, 128)


def moved(x, spans, slabs):
    pairs = []
    for t in range(SPANS):
        for s in range(SLABS):
            pairs.append((t * SLABS + s, (t + spans) % SPANS * SLABS + (s + slabs) % SLABS))
    return lax.ppermute(x, ("tm", "space"), pairs)


def exchanged(send, up, dn, block):
    lo1, hi1 = moved(up, 0, 1), moved(dn, 0, -1)
    lo2, hi2 = moved(block, 0, 2), moved(block, 0, -2)
    got = lax.all_to_all(send, "space", 0, 0, tiled=True)
    return got, lo2, lo1, block, hi1, hi2


def shards(u0, src, cap):
    b, up, dn = call(pack_body, (f32(4, *PLANE), f32(4, *PLANE), f32(4, *PLANE)), [], u0, src, cap)
    lo, hi = moved(up, 0, 1), moved(dn, 0, -1)
    w, w1, c1, xs, send, up, dn, block = call(
        first_down_body,
        (
            f32(8, *PLANE),
            f32(3, 32, 128),
            f32(2, 32, 128),
            f32(6, *PLANE),
            MESSAGE,
            f32(128, 128),
            f32(128, 128),
            f32(64, 128),
        ),
        DOWN_WORK,
        *(b, cap, lo, hi),
    )
    fpoint, b, up, dn, v1, w2, d2, w3 = call(
        first_up_body,
        (
            f32(1, 4, *PLANE),
            f32(4, *PLANE),
            f32(2, *PLANE),
            f32(2, *PLANE),
            f32(5, 32, 128),
            f32(128, 128),
            f32(128, 128),
            f32(32, 128),
        ),
        WORK,
        *exchanged(send, up, dn, block),
        *(b, lo, hi, w, xs, cap, src),
    )
    b, lo, hi = moved(b, 1, 0), moved(up, 1, 1), moved(dn, 1, -1)
    xs, send, up, dn, block = call(
        next_down_body,
        (f32(6, *PLANE), MESSAGE, f32(96, 128), f32(96, 128), f32(32, 128)),
        DOWN_WORK,
        *(b, cap, lo, hi, w, w1, c1),
    )
    (updated,) = call(
        next_up_body,
        (f32(1, 4, *PLANE),),
        WORK,
        *exchanged(send, up, dn, block),
        *(b, lo, hi, w, xs, v1, w2, d2, w3, u0),
    )
    return fpoint, updated


def solution(mesh):
    in_specs = (
        P("tm", "space", None, None),
        P("tm", None, "space", None, None),
        P("space", None, None),
    )
    out_specs = (P("tm", "space", None, None), P("tm", "space", None, None))
    return jax.shard_map(shards, mesh=mesh, in_specs=in_specs, out_specs=out_specs, check_vma=False)
```

time: 101 us -> 83.4 us (0.83)
  blocking collectives: 60.3 us -> 0 us
  starting transfers between devices: 14.2 us -> 49.2 us
  waiting for transfers between devices: 7.9 us -> 18 us
  Pallas kernels: 14.5 us -> 12.2 us
    all_to_all x2 -> x0, blocking collectives: 60.3 us -> none  [shards(): got = lax.all_to_all(send, 'space', 0, 0, tiled=True)]
    ppermute x5 -> x13, starting transfers between devices: 14.2 us -> 32.1 us  [moved(): return lax.ppermute(x, ('tm', 'space'), pairs)]
    all_to_all x0 -> x2, starting transfers between devices: none -> 17.2 us  [exchanged(): got = lax.all_to_all(send, 'space', 0, 0, tiled=True)]
    ppermute x5 -> x13, waiting for transfers between devices: 7.9 us -> 18 us  [moved(): return lax.ppermute(x, ('tm', 'space'), pairs)]
    pallas_call x5, Pallas kernels: 14.5 us -> 12.2 us  [call(): pl.pallas_call(body, out_shape=outs, in_specs=[VMEM] * len(args), out_spe...]
    unnamed x10 -> x12, local copies, waits for them, and re-layouts: 2.76 us -> 2.76 us
  transfers between devices with their start and end apart: 5 -> 15, of which waited for: 3 -> 7; matrix products, arithmetic and copies ran while one was open for 0% -> 0% of each run, Pallas kernels for 0% -> 0%
where the time goes in v3:
time: 83.4 us; the launch traced here: 82.9 us
  starting transfers between devices  49.2 us (59%)
  waiting for transfers between devices  18 us (22%)
  Pallas kernels  12.2 us (15%)
  local copies, waits for them, and re-layouts  2.76 us (3%)
    ppermute x13, starting transfers between devices, moved(): return lax.ppermute(x, ('tm', 'space'), pairs)  32.1 us
    ppermute x13, waiting for transfers between devices, moved(): return lax.ppermute(x, ('tm', 'space'), pairs)  18 us
    all_to_all x2, starting transfers between devices, exchanged(): got = lax.all_to_all(send, 'space', 0, 0, tiled=True)  17.2 us
    pallas_call x5, Pallas kernels, call(): pl.pallas_call(body, out_shape=outs, in_specs=[VMEM] * len(args), out_spe...  12.2 us
    unnamed x12, local copies, waits for them, and re-layouts  2.76 us
  transfers between devices with their start and end apart: 15, of which 7 were waited for; matrix products, arithmetic and copies ran while one was open for 0% of the time, Pallas kernels for 0%

profile of v3, /device:TPU:4, one launch (start us, length us, event | category | flops | bytes accessed | tf_op | source)
XLA Modules:
  0.0 82.9 jit_solution(15921333768533098365)
XLA Ops:
  3.4 1.7 %collective-permute-start = (f32[4,64,128]{2,1,0:T(8,128)S(1)}, f32[4,64,128]{2,1,0:T(8,128)S(1)}, u32[]{:S(2)}, u32[]{:S(2)}) collective-permute-start(f32[4,64,128]{2,1,0:T(8,128)S(1)} %get-tuple-element.27), channel_id=1, source_target_pairs={{0,1},{1,2},{2,3},{3,4},{4,5},{5,6},{6,7},{7,8},{8,9},{9,10},{10,1... | collective-permute-start | bytes 393224 | tf_op jit(solution)/shard_map/ppermute | solution.py:383
  5.1 6.8 %collective-permute-start.1 = (f32[4,64,128]{2,1,0:T(8,128)S(1)}, f32[4,64,128]{2,1,0:T(8,128)S(1)}, u32[]{:S(2)}, u32[]{:S(2)}) collective-permute-start(f32[4,64,128]{2,1,0:T(8,128)S(1)} %get-tuple-element.28), channel_id=1, source_target_pairs={{0,31},{1,0},{2,1},{3,2},{4,3},{5,4},{6,5},{7,6},{8,7},{9,8},{10,9... | collective-permute-start | bytes 393224 | tf_op jit(solution)/shard_map/ppermute | solution.py:383
  11.9 3.4 %collective-permute-done.lo = f32[4,64,128]{2,1,0:T(8,128)S(1)} collective-permute-done((f32[4,64,128]{2,1,0:T(8,128)S(1)}, f32[4,64,128]{2,1,0:T(8,128)S(1)}, u32[]{:S(2)}, u32[]{:S(2)}) %collective-permute-start) | collective-permute-done | bytes 131104 | tf_op jit(solution)/shard_map/ppermute | solution.py:383
  15.3 1.7 %shard_map.51 = (f32[8,64,128]{2,1,0:T(8,128)S(1)}, f32[3,32,128]{2,1,0:T(8,128)S(1)}, f32[2,32,128]{2,1,0:T(8,128)S(1)}, f32[6,64,128]{2,1,0:T(8,128)S(1)}, f32...) custom-call(f32[4,64,128]{2,1,0:T(8,128)S(1)} %get-tuple-element.26.b_own, ...), custom_call_target="tpu_custom_call" | custom-call | tf_op jit(solution)/shard_map/pallas_call | solution.py:23
  17.0 8.1 %all-to-all-start = ((f32[32,16,128]{2,1,0:T(8,128)}), f32[32,16,128]{2,1,0:T(8,128)S(1)}, u32[]{:S(2)}, u32[]{:S(2)}) async-start(f32[32,16,128]{2,1,0:T(8,128)} %get-tuple-element.29), calls=%async_computation | async-start | bytes 524288 | tf_op jit(solution)/shard_map/all_to_all | solution.py:389
  25.2 1.9 %collective-permute-start.3 = (f32[128,128]{1,0:T(8,128)S(1)}, f32[128,128]{1,0:T(8,128)S(1)}, u32[]{:S(2)}, u32[]{:S(2)}) collective-permute-start(f32[128,128]{1,0:T(8,128)S(1)} %get-tuple-element.31), channel_id=1, source_target_pairs={{0,1},{1,2},{2,3},{3,4},{4,5},{5,6},{6,7},{7,8},{8,9},{9,10},{10,1... | collective-permute-start | bytes 196616 | tf_op jit(solution)/shard_map/ppermute | solution.py:383
  27.0 3.6 %collective-permute-start.4 = (f32[128,128]{1,0:T(8,128)S(1)}, f32[128,128]{1,0:T(8,128)S(1)}, u32[]{:S(2)}, u32[]{:S(2)}) collective-permute-start(f32[128,128]{1,0:T(8,128)S(1)} %get-tuple-element.32), channel_id=1, source_target_pairs={{0,31},{1,0},{2,1},{3,2},{4,3},{5,4},{6,5},{7,6},{8,7},{9,8},{10,9... | collective-permute-start | bytes 196616 | tf_op jit(solution)/shard_map/ppermute | solution.py:383
  30.6 2.2 %collective-permute-start.5 = (f32[64,128]{1,0:T(8,128)S(1)}, f32[64,128]{1,0:T(8,128)S(1)}, u32[]{:S(2)}, u32[]{:S(2)}) collective-permute-start(f32[64,128]{1,0:T(8,128)S(1)} %get-tuple-element.30.block), channel_id=1, source_target_pairs={{0,30},{1,31},{2,0},{3,1},{4,2},{5,3},{6,4},{7,5},{8,6},{9,7},{10,... | collective-permute-start | bytes 98312 | tf_op jit(solution)/shard_map/ppermute | solution.py:383
  32.7 1.4 %collective-permute-start.2 = (f32[64,128]{1,0:T(8,128)S(1)}, f32[64,128]{1,0:T(8,128)S(1)}, u32[]{:S(2)}, u32[]{:S(2)}) collective-permute-start(f32[64,128]{1,0:T(8,128)S(1)} %get-tuple-element.30.block), channel_id=1, source_target_pairs={{0,2},{1,3},{2,4},{3,5},{4,6},{5,7},{6,8},{7,9},{8,10},{9,11},{10,... | collective-permute-start | bytes 98312 | tf_op jit(solution)/shard_map/ppermute | solution.py:383
  34.1 2.5 %collective-permute-done.5.hi2 = f32[64,128]{1,0:T(8,128)S(1)} collective-permute-done((f32[64,128]{1,0:T(8,128)S(1)}, f32[64,128]{1,0:T(8,128)S(1)}, u32[]{:S(2)}, u32[]{:S(2)}) %collective-permute-start.5) | collective-permute-done | bytes 32800 | tf_op jit(solution)/shard_map/ppermute | solution.py:383
  36.6 3.7 %collective-permute-done.2.lo2 = f32[64,128]{1,0:T(8,128)S(1)} collective-permute-done((f32[64,128]{1,0:T(8,128)S(1)}, f32[64,128]{1,0:T(8,128)S(1)}, u32[]{:S(2)}, u32[]{:S(2)}) %collective-permute-start.2) | collective-permute-done | bytes 32800 | tf_op jit(solution)/shard_map/ppermute | solution.py:383
  40.3 4.5 %shard_map.52 = (f32[1,4,64,128]{3,2,1,0:T(8,128)}, f32[4,64,128]{2,1,0:T(8,128)S(1)}, f32[2,64,128]{2,1,0:T(8,128)S(1)}, f32[2,64,128]{2,1,0:T(8,128)S(1)}, f32...) custom-call(f32[32,16,128]{2,1,0:T(8,128)S(1)} %all-to-all-done.got, ...), custom_call_target="tpu_custom_call" | custom-call | tf_op jit(solution)/shard_map/pallas_call | solution.py:23
  44.8 1.5 %collective-permute-start.7 = (f32[2,64,128]{2,1,0:T(8,128)S(1)}, f32[2,64,128]{2,1,0:T(8,128)S(1)}, u32[]{:S(2)}, u32[]{:S(2)}) collective-permute-start(f32[2,64,128]{2,1,0:T(8,128)S(1)} %get-tuple-element.37), channel_id=1, source_target_pairs={{0,33},{1,34},{2,35},{3,36},{4,37},{5,38},{6,39},{7,40},{8,41},{9,... | collective-permute-start | bytes 196616 | tf_op jit(solution)/shard_map/ppermute | solution.py:383
  46.3 4.2 %collective-permute-start.8 = (f32[2,64,128]{2,1,0:T(8,128)S(1)}, f32[2,64,128]{2,1,0:T(8,128)S(1)}, u32[]{:S(2)}, u32[]{:S(2)}) collective-permute-start(f32[2,64,128]{2,1,0:T(8,128)S(1)} %get-tuple-element.38), channel_id=1, source_target_pairs={{0,63},{1,32},{2,33},{3,34},{4,35},{5,36},{6,37},{7,38},{8,39},{9,... | collective-permute-start | bytes 196616 | tf_op jit(solution)/shard_map/ppermute | solution.py:383
  50.5 2.3 %collective-permute-done.7.refs_2_.lo = f32[2,64,128]{2,1,0:T(8,128)S(1)} collective-permute-done((f32[2,64,128]{2,1,0:T(8,128)S(1)}, f32[2,64,128]{2,1,0:T(8,128)S(1)}, u32[]{:S(2)}, u32[]{:S(2)}) %collective-permute-start.7) | collective-permute-done | bytes 65568 | tf_op jit(solution)/shard_map/ppermute | solution.py:383
  52.9 1.7 %shard_map.53 = (f32[6,64,128]{2,1,0:T(8,128)S(1)}, f32[32,16,128]{2,1,0:T(8,128)}, f32[96,128]{1,0:T(8,128)S(1)}, f32[96,128]{1,0:T(8,128)S(1)}, f32[32,128]{1,0:T(8,128)S(1)}) custom-call(f32[4,64,128]{2,1,0:T(8,128)S(1)} %collective-permute-done.6.refs_0_.b_own, f32[4,64,128]{2,1,0:T(8,128)S(1)} %copy-done.1, ...), custom_call_target="tpu_custom_call" | custom-call | tf_op jit(solution)/shard_map/pallas_call | solution.py:23
  54.5 9.0 %all-to-all-start.1 = ((f32[32,16,128]{2,1,0:T(8,128)}), f32[32,16,128]{2,1,0:T(8,128)S(1)}, u32[]{:S(2)}, u32[]{:S(2)}) async-start(f32[32,16,128]{2,1,0:T(8,128)} %get-tuple-element.41), calls=%async_computation.1 | async-start | bytes 524288 | tf_op jit(solution)/shard_map/all_to_all | solution.py:389
  63.6 1.9 %collective-permute-start.10 = (f32[96,128]{1,0:T(8,128)S(1)}, f32[96,128]{1,0:T(8,128)S(1)}, u32[]{:S(2)}, u32[]{:S(2)}) collective-permute-start(f32[96,128]{1,0:T(8,128)S(1)} %get-tuple-element.43), channel_id=1, source_target_pairs={{0,1},{1,2},{2,3},{3,4},{4,5},{5,6},{6,7},{7,8},{8,9},{9,10},{10,1... | collective-permute-start | bytes 147464 | tf_op jit(solution)/shard_map/ppermute | solution.py:383
  65.4 3.6 %collective-permute-start.11 = (f32[96,128]{1,0:T(8,128)S(1)}, f32[96,128]{1,0:T(8,128)S(1)}, u32[]{:S(2)}, u32[]{:S(2)}) collective-permute-start(f32[96,128]{1,0:T(8,128)S(1)} %get-tuple-element.44), channel_id=1, source_target_pairs={{0,31},{1,0},{2,1},{3,2},{4,3},{5,4},{6,5},{7,6},{8,7},{9,8},{10,9... | collective-permute-start | bytes 147464 | tf_op jit(solution)/shard_map/ppermute | solution.py:383
  69.0 2.2 %collective-permute-start.12 = (f32[32,128]{1,0:T(8,128)S(1)}, f32[32,128]{1,0:T(8,128)S(1)}, u32[]{:S(2)}, u32[]{:S(2)}) collective-permute-start(f32[32,128]{1,0:T(8,128)S(1)} %get-tuple-element.42.block), channel_id=1, source_target_pairs={{0,30},{1,31},{2,0},{3,1},{4,2},{5,3},{6,4},{7,5},{8,6},{9,7},{10,... | collective-permute-start | bytes 49160 | tf_op jit(solution)/shard_map/ppermute | solution.py:383
  71.1 1.4 %collective-permute-start.9 = (f32[32,128]{1,0:T(8,128)S(1)}, f32[32,128]{1,0:T(8,128)S(1)}, u32[]{:S(2)}, u32[]{:S(2)}) collective-permute-start(f32[32,128]{1,0:T(8,128)S(1)} %get-tuple-element.42.block), channel_id=1, source_target_pairs={{0,2},{1,3},{2,4},{3,5},{4,6},{5,7},{6,8},{7,9},{8,10},{9,11},{10,... | collective-permute-start | bytes 49160 | tf_op jit(solution)/shard_map/ppermute | solution.py:383
  72.5 1.8 %collective-permute-done.12.hi2 = f32[32,128]{1,0:T(8,128)S(1)} collective-permute-done((f32[32,128]{1,0:T(8,128)S(1)}, f32[32,128]{1,0:T(8,128)S(1)}, u32[]{:S(2)}, u32[]{:S(2)}) %collective-permute-start.12) | collective-permute-done | bytes 16416 | tf_op jit(solution)/shard_map/ppermute | solution.py:383
  74.3 4.2 %collective-permute-done.9.lo2 = f32[32,128]{1,0:T(8,128)S(1)} collective-permute-done((f32[32,128]{1,0:T(8,128)S(1)}, f32[32,128]{1,0:T(8,128)S(1)}, u32[]{:S(2)}, u32[]{:S(2)}) %collective-permute-start.9) | collective-permute-done | bytes 16416 | tf_op jit(solution)/shard_map/ppermute | solution.py:383
  78.5 4.3 %shard_map.54 = f32[1,4,64,128]{3,2,1,0:T(8,128)} custom-call(f32[32,16,128]{2,1,0:T(8,128)S(1)} %all-to-all-done.1.got, f32[32,128]{1,0:T(8,128)S(1)} %collective-permute-done.9.lo2, f32[96,128]{1,0:T(8,128)S(1)} %collective-permute-done.10.lo1, f32[32,128]{1,0:T(8,128)S(1)} %get-tuple-element.42.block, f32[96,128]{1,0:T(8,128)S(1)} %collective-permute-done.11.hi1, ...), custom_call_target="tpu_custom_call" | custom-call | tf_op jit(solution)/shard_map/pallas_call | solution.py:23
  (23 shorter events, 2.9 us)
Async XLA Ops:
  0.6 0.9 %copy-start = (f32[4,64,128]{2,1,0:T(8,128)S(1)}, f32[4,64,128]{2,1,0:T(8,128)}, u32[]{:S(2)}) copy-start(f32[4,64,128]{2,1,0:T(8,128)} %refs_1_.1) | copy-start | bytes 393220
  1.5 0.9 %copy-start.2 = (f32[1,2,4,64,128]{4,3,2,1,0:T(8,128)S(1)}, f32[1,2,4,64,128]{4,3,2,1,0:T(8,128)}, u32[]{:S(2)}) copy-start(f32[1,2,4,64,128]{4,3,2,1,0:T(8,128)} %src.3) | copy-start | bytes 786436
  2.5 0.9 %copy-start.4 = (f32[1,4,64,128]{3,2,1,0:T(8,128)S(1)}, f32[1,4,64,128]{3,2,1,0:T(8,128)}, u32[]{:S(2)}) copy-start(f32[1,4,64,128]{3,2,1,0:T(8,128)} %start.1) | copy-start | bytes 393220
  3.4 11.9 %copy-start.1 = (f32[4,64,128]{2,1,0:T(8,128)S(1)}, f32[4,64,128]{2,1,0:T(8,128)}, u32[]{:S(2)}) copy-start(f32[4,64,128]{2,1,0:T(8,128)} %refs_1_.1) | copy-start | bytes 393220
  3.4 11.9 %collective-permute-start = (f32[4,64,128]{2,1,0:T(8,128)S(1)}, f32[4,64,128]{2,1,0:T(8,128)S(1)}, u32[]{:S(2)}, u32[]{:S(2)}) collective-permute-start(f32[4,64,128]{2,1,0:T(8,128)S(1)} %get-tuple-element.27), channel_id=1, source_target_pairs={{0,1},{1,2},{2,3},{3,4},{4,5},{5,6},{6,7},{7,8},{8,9},{9,10},{10,1... | collective-permute-start | bytes 393224 | tf_op jit(solution)/shard_map/ppermute | solution.py:383
  5.1 10.2 %collective-permute-start.1 = (f32[4,64,128]{2,1,0:T(8,128)S(1)}, f32[4,64,128]{2,1,0:T(8,128)S(1)}, u32[]{:S(2)}, u32[]{:S(2)}) collective-permute-start(f32[4,64,128]{2,1,0:T(8,128)S(1)} %get-tuple-element.28), channel_id=1, source_target_pairs={{0,31},{1,0},{2,1},{3,2},{4,3},{5,4},{6,5},{7,6},{8,7},{9,8},{10,9... | collective-permute-start | bytes 393224 | tf_op jit(solution)/shard_map/ppermute | solution.py:383
  17.0 23.3 %copy-start.3 = (f32[1,2,4,64,128]{4,3,2,1,0:T(8,128)S(1)}, f32[1,2,4,64,128]{4,3,2,1,0:T(8,128)}, u32[]{:S(2)}) copy-start(f32[1,2,4,64,128]{4,3,2,1,0:T(8,128)} %src.3) | copy-start | bytes 786436
  17.0 23.3 %all-to-all-start = ((f32[32,16,128]{2,1,0:T(8,128)}), f32[32,16,128]{2,1,0:T(8,128)S(1)}, u32[]{:S(2)}, u32[]{:S(2)}) async-start(f32[32,16,128]{2,1,0:T(8,128)} %get-tuple-element.29), calls=%async_computation | async-start | bytes 524288 | tf_op jit(solution)/shard_map/all_to_all | solution.py:389
  25.2 15.1 %collective-permute-start.3 = (f32[128,128]{1,0:T(8,128)S(1)}, f32[128,128]{1,0:T(8,128)S(1)}, u32[]{:S(2)}, u32[]{:S(2)}) collective-permute-start(f32[128,128]{1,0:T(8,128)S(1)} %get-tuple-element.31), channel_id=1, source_target_pairs={{0,1},{1,2},{2,3},{3,4},{4,5},{5,6},{6,7},{7,8},{8,9},{9,10},{10,1... | collective-permute-start | bytes 196616 | tf_op jit(solution)/shard_map/ppermute | solution.py:383
  27.0 13.3 %collective-permute-start.4 = (f32[128,128]{1,0:T(8,128)S(1)}, f32[128,128]{1,0:T(8,128)S(1)}, u32[]{:S(2)}, u32[]{:S(2)}) collective-permute-start(f32[128,128]{1,0:T(8,128)S(1)} %get-tuple-element.32), channel_id=1, source_target_pairs={{0,31},{1,0},{2,1},{3,2},{4,3},{5,4},{6,5},{7,6},{8,7},{9,8},{10,9... | collective-permute-start | bytes 196616 | tf_op jit(solution)/shard_map/ppermute | solution.py:383
  30.6 6.0 %collective-permute-start.5 = (f32[64,128]{1,0:T(8,128)S(1)}, f32[64,128]{1,0:T(8,128)S(1)}, u32[]{:S(2)}, u32[]{:S(2)}) collective-permute-start(f32[64,128]{1,0:T(8,128)S(1)} %get-tuple-element.30.block), channel_id=1, source_target_pairs={{0,30},{1,31},{2,0},{3,1},{4,2},{5,3},{6,4},{7,5},{8,6},{9,7},{10,... | collective-permute-start | bytes 98312 | tf_op jit(solution)/shard_map/ppermute | solution.py:383
  32.7 7.5 %collective-permute-start.2 = (f32[64,128]{1,0:T(8,128)S(1)}, f32[64,128]{1,0:T(8,128)S(1)}, u32[]{:S(2)}, u32[]{:S(2)}) collective-permute-start(f32[64,128]{1,0:T(8,128)S(1)} %get-tuple-element.30.block), channel_id=1, source_target_pairs={{0,2},{1,3},{2,4},{3,5},{4,6},{5,7},{6,8},{7,9},{8,10},{9,11},{10,... | collective-permute-start | bytes 98312 | tf_op jit(solution)/shard_map/ppermute | solution.py:383
  44.8 8.1 %collective-permute-start.6 = (f32[4,64,128]{2,1,0:T(8,128)S(1)}, f32[4,64,128]{2,1,0:T(8,128)S(1)}, u32[]{:S(2)}, u32[]{:S(2)}) collective-permute-start(f32[4,64,128]{2,1,0:T(8,128)S(1)} %get-tuple-element.36), channel_id=1, source_target_pairs={{0,32},{1,33},{2,34},{3,35},{4,36},{5,37},{6,38},{7,39},{8,40},{9,... | collective-permute-start | bytes 393224 | tf_op jit(solution)/shard_map/ppermute | solution.py:383
  44.8 8.0 %collective-permute-start.7 = (f32[2,64,128]{2,1,0:T(8,128)S(1)}, f32[2,64,128]{2,1,0:T(8,128)S(1)}, u32[]{:S(2)}, u32[]{:S(2)}) collective-permute-start(f32[2,64,128]{2,1,0:T(8,128)S(1)} %get-tuple-element.37), channel_id=1, source_target_pairs={{0,33},{1,34},{2,35},{3,36},{4,37},{5,38},{6,39},{7,40},{8,41},{9,... | collective-permute-start | bytes 196616 | tf_op jit(solution)/shard_map/ppermute | solution.py:383
  46.3 6.6 %collective-permute-start.8 = (f32[2,64,128]{2,1,0:T(8,128)S(1)}, f32[2,64,128]{2,1,0:T(8,128)S(1)}, u32[]{:S(2)}, u32[]{:S(2)}) collective-permute-start(f32[2,64,128]{2,1,0:T(8,128)S(1)} %get-tuple-element.38), channel_id=1, source_target_pairs={{0,63},{1,32},{2,33},{3,34},{4,35},{5,36},{6,37},{7,38},{8,39},{9,... | collective-permute-start | bytes 196616 | tf_op jit(solution)/shard_map/ppermute | solution.py:383
  54.5 24.0 %copy-start.5 = (f32[1,4,64,128]{3,2,1,0:T(8,128)S(1)}, f32[1,4,64,128]{3,2,1,0:T(8,128)}, u32[]{:S(2)}) copy-start(f32[1,4,64,128]{3,2,1,0:T(8,128)} %start.1) | copy-start | bytes 393220
  54.5 24.0 %all-to-all-start.1 = ((f32[32,16,128]{2,1,0:T(8,128)}), f32[32,16,128]{2,1,0:T(8,128)S(1)}, u32[]{:S(2)}, u32[]{:S(2)}) async-start(f32[32,16,128]{2,1,0:T(8,128)} %get-tuple-element.41), calls=%async_computation.1 | async-start | bytes 524288 | tf_op jit(solution)/shard_map/all_to_all | solution.py:389
  63.6 14.9 %collective-permute-start.10 = (f32[96,128]{1,0:T(8,128)S(1)}, f32[96,128]{1,0:T(8,128)S(1)}, u32[]{:S(2)}, u32[]{:S(2)}) collective-permute-start(f32[96,128]{1,0:T(8,128)S(1)} %get-tuple-element.43), channel_id=1, source_target_pairs={{0,1},{1,2},{2,3},{3,4},{4,5},{5,6},{6,7},{7,8},{8,9},{9,10},{10,1... | collective-permute-start | bytes 147464 | tf_op jit(solution)/shard_map/ppermute | solution.py:383
  65.4 13.1 %collective-permute-start.11 = (f32[96,128]{1,0:T(8,128)S(1)}, f32[96,128]{1,0:T(8,128)S(1)}, u32[]{:S(2)}, u32[]{:S(2)}) collective-permute-start(f32[96,128]{1,0:T(8,128)S(1)} %get-tuple-element.44), channel_id=1, source_target_pairs={{0,31},{1,0},{2,1},{3,2},{4,3},{5,4},{6,5},{7,6},{8,7},{9,8},{10,9... | collective-permute-start | bytes 147464 | tf_op jit(solution)/shard_map/ppermute | solution.py:383
  69.0 5.3 %collective-permute-start.12 = (f32[32,128]{1,0:T(8,128)S(1)}, f32[32,128]{1,0:T(8,128)S(1)}, u32[]{:S(2)}, u32[]{:S(2)}) collective-permute-start(f32[32,128]{1,0:T(8,128)S(1)} %get-tuple-element.42.block), channel_id=1, source_target_pairs={{0,30},{1,31},{2,0},{3,1},{4,2},{5,3},{6,4},{7,5},{8,6},{9,7},{10,... | collective-permute-start | bytes 49160 | tf_op jit(solution)/shard_map/ppermute | solution.py:383
  71.1 7.4 %collective-permute-start.9 = (f32[32,128]{1,0:T(8,128)S(1)}, f32[32,128]{1,0:T(8,128)S(1)}, u32[]{:S(2)}, u32[]{:S(2)}) collective-permute-start(f32[32,128]{1,0:T(8,128)S(1)} %get-tuple-element.42.block), channel_id=1, source_target_pairs={{0,2},{1,3},{2,4},{3,5},{4,6},{5,7},{6,8},{7,9},{8,10},{9,11},{10,... | collective-permute-start | bytes 49160 | tf_op jit(solution)/shard_map/ppermute | solution.py:383

commit v4 on v3

--- a/solution.py
+++ b/solution.py
@@ -19,14 +19,15 @@
     return jax.ShapeDtypeStruct(shape, F32)
 
 
-def call(body, outs, scratch, *args):
+def call(body, outs, scratch, *args, space=VMEM, flops=None, sems=()):
     return pl.pallas_call(
         body,
         out_shape=outs,
-        in_specs=[VMEM] * len(args),
+        in_specs=[space] * len(args),
         out_specs=tuple(VMEM for _ in outs),
-        scratch_shapes=[pltpu.VMEM(s, F32) for s in scratch],
+        scratch_shapes=[pltpu.VMEM(s, F32) for s in scratch] + list(sems),
         compiler_params=pltpu.CompilerParams(vmem_limit_bytes=16 << 20),
+        cost_estimate=flops and pl.CostEstimate(flops=flops, transcendentals=0, bytes_accessed=0),
     )(*args)
 
 
@@ -112,10 +113,19 @@
     return jnp.concatenate(v, 0)
 
 
-def pack_body(u, src, cap, b_out, up, dn):
+def pack_body(u, src, cap, b_out, up, dn, cap_out, u_in, src_in, sems):
+    copies = [
+        pltpu.make_async_copy(cap, cap_out, sems.at[0]),
+        pltpu.make_async_copy(u.at[0], u_in, sems.at[1]),
+        pltpu.make_async_copy(src.at[0, 0], src_in, sems.at[2]),
+    ]
+    for copy in copies:
+        copy.start()
+    for copy in copies:
+        copy.wait()
     for p in range(DEPTH):
-        c = cap[p]
-        b = c * u[0, p] + src[0, 0, p]
+        c = cap_out[p]
+        b = c * u_in[p] + src_in[p]
         b_out[p] = b
         ends, i = (dn, p) if p < 2 else (up, p - 2)
         ends[i] = b
@@ -241,7 +251,7 @@
     return jnp.concatenate(parts, 0)
 
 
-def low_levels(got, first, w2, d2, w3, x2, t3):
+def low_levels(first, got, w2, d2, w3, x2, t3):
     group = iota((16, 128), 1) >> 5
     parts, caps = [], []
     for zl in range(8):
@@ -276,9 +286,16 @@
     x2[...] = x
 
 
-def fine_up(got, near, first, b_own, lo, hi, w, xs, w1, w2, d2, w3, work, out):
-    x2, t3, f1, y1, xa, xb, f0, x0, x9 = work
-    low_levels(got, first, w2, d2, w3, x2, t3)
+def first_low_body(got, w2, d2, w3, x2, t3):
+    low_levels(True, got, w2, d2, w3, x2, t3)
+
+
+def next_low_body(*refs):
+    low_levels(False, *refs)
+
+
+def fine_up(x2, near, first, b_own, lo, hi, w, xs, w1, work, out):
+    f1, y1, xa, xb, f0, x0, x9 = work
     s = lax.axis_index("space")
     lo2, lo1, block, hi1, hi2 = near
     for j, ref in enumerate(near):
@@ -333,8 +350,7 @@
 
 
 def first_up_body(
-    got, lo2, lo1, block, hi1, hi2, b_own, lo, hi, w, xs, cap, src,
-    u_out, b_out, up, dn, w1, w2, d2, w3, *work
+    x2, lo2, lo1, block, hi1, hi2, b_own, lo, hi, w, xs, cap, src, u_out, b_out, up, dn, w1, *work
 ):
     def out(p, u):
         u_out[0, p] = u
@@ -344,24 +360,22 @@
         ends[i] = b
 
     near = (lo2, lo1, block, hi1, hi2)
-    fine_up(got, near, True, b_own, lo, hi, w, xs, w1, w2, d2, w3, work, out)
-
-
-def next_up_body(
-    got, lo2, lo1, block, hi1, hi2, b_own, lo, hi, w, xs, w1, w2, d2, w3, start, u_out, *work
-):
+    fine_up(x2, near, True, b_own, lo, hi, w, xs, w1, work, out)
+
+
+def next_up_body(x2, lo2, lo1, block, hi1, hi2, b_own, lo, hi, w, xs, w1, start, u_out, *work):
     keep = lax.axis_index("tm") == 0
 
     def out(p, u):
         u_out[0, p] = jnp.where(keep, start[0, p], u)
 
     near = (lo2, lo1, block, hi1, hi2)
-    fine_up(got, near, False, b_own, lo, hi, w, xs, w1, w2, d2, w3, work, out)
-
-
+    fine_up(x2, near, False, b_own, lo, hi, w, xs, w1, work, out)
+
+
+LOW_WORK = [(64, 128)]
+LOW_FLOPS = 1 << 31
 WORK = [
-    (128, 128),
-    (64, 128),
     (160, 128),
     (5, 32, 128),
     (5, 32, 128),
@@ -372,6 +386,7 @@
 ]
 DOWN_WORK = [(8, NY, NX), (384, 128)]
 PLANE = (NY, NX)
+PLANE4 = (DEPTH, NY, NX)
 MESSAGE = f32(SLABS, 16, 128)
 
 
@@ -391,7 +406,14 @@
 
 
 def shards(u0, src, cap):
-    b, up, dn = call(pack_body, (f32(4, *PLANE), f32(4, *PLANE), f32(4, *PLANE)), [], u0, src, cap)
+    b, up, dn, cap = call(
+        pack_body,
+        (f32(4, *PLANE),) * 4,
+        [PLANE4, PLANE4],
+        *(u0, src, cap),
+        space=pl.BlockSpec(memory_space=pltpu.HBM),
+        sems=[pltpu.SemaphoreType.DMA((3,))],
+    )
     lo, hi = moved(up, 0, 1), moved(dn, 0, -1)
     w, w1, c1, xs, send, up, dn, block = call(
         first_down_body,
@@ -408,21 +430,19 @@
         DOWN_WORK,
         *(b, cap, lo, hi),
     )
-    fpoint, b, up, dn, v1, w2, d2, w3 = call(
+    got, *near = exchanged(send, up, dn, block)
+    w2, d2, w3, x2 = call(
+        first_low_body,
+        (f32(128, 128), f32(128, 128), f32(32, 128), f32(128, 128)),
+        LOW_WORK,
+        got,
+        flops=LOW_FLOPS,
+    )
+    fpoint, b, up, dn, v1 = call(
         first_up_body,
-        (
-            f32(1, 4, *PLANE),
-            f32(4, *PLANE),
-            f32(2, *PLANE),
-            f32(2, *PLANE),
-            f32(5, 32, 128),
-            f32(128, 128),
-            f32(128, 128),
-            f32(32, 128),
-        ),
+        (f32(1, *PLANE4), f32(*PLANE4), f32(2, *PLANE), f32(2, *PLANE), f32(5, 32, 128)),
         WORK,
-        *exchanged(send, up, dn, block),
-        *(b, lo, hi, w, xs, cap, src),
+        *(x2, *near, b, lo, hi, w, xs, cap, src),
     )
     b, lo, hi = moved(b, 1, 0), moved(up, 1, 1), moved(dn, 1, -1)
     xs, send, up, dn, block = call(
@@ -431,12 +451,10 @@
         DOWN_WORK,
         *(b, cap, lo, hi, w, w1, c1),
     )
+    got, *near = exchanged(send, up, dn, block)
+    (x2,) = call(next_low_body, (f32(128, 128),), LOW_WORK, *(got, w2, d2, w3), flops=LOW_FLOPS)
     (updated,) = call(
-        next_up_body,
-        (f32(1, 4, *PLANE),),
-        WORK,
-        *exchanged(send, up, dn, block),
-        *(b, lo, hi, w, xs, v1, w2, d2, w3, u0),
+        next_up_body, (f32(1, *PLANE4),), WORK, *(x2, *near, b, lo, hi, w, xs, v1, u0)
     )
     return fpoint, updated
 

time: 83.4 us -> 78.6 us (0.942)
  waiting for transfers between devices: 18 us -> 10.1 us
  starting transfers between devices: 49.2 us -> 52 us
    ppermute x13, waiting for transfers between devices: 18 us -> 5.82 us  [moved(): return lax.ppermute(x, ('tm', 'space'), pairs)]
    all_to_all x2, waiting for transfers between devices: 0.01 us -> 4.26 us  [exchanged(): got = lax.all_to_all(send, 'space', 0, 0, tiled=True)]
    ppermute x13, starting transfers between devices: 32.1 us -> 36 us  [moved(): return lax.ppermute(x, ('tm', 'space'), pairs)]
    all_to_all x2, starting transfers between devices: 17.2 us -> 16 us  [exchanged(): got = lax.all_to_all(send, 'space', 0, 0, tiled=True)]
    pallas_call x5 -> x7, Pallas kernels: 12.2 us -> 12.6 us  [call(): pl.pallas_call(body, out_shape=outs, in_specs=[space] * len(args), out_sp...]
    unnamed x12 -> x10, local copies, waits for them, and re-layouts: 2.76 us -> 2.76 us
  transfers between devices with their start and end apart: 15 -> 15, of which waited for: 7 -> 5; matrix products, arithmetic and copies ran while one was open for 0% -> 0% of each run, Pallas kernels for 0% -> 7%
where the time goes in v4:
time: 78.6 us; the launch traced here: 78.3 us
  starting transfers between devices  52 us (66%)
  Pallas kernels  12.6 us (16%)
  waiting for transfers between devices  10.1 us (13%)
  local copies, waits for them, and re-layouts  2.76 us (4%)
    ppermute x13, starting transfers between devices, moved(): return lax.ppermute(x, ('tm', 'space'), pairs)  36 us
    all_to_all x2, starting transfers between devices, exchanged(): got = lax.all_to_all(send, 'space', 0, 0, tiled=True)  16 us
    pallas_call x7, Pallas kernels, call(): pl.pallas_call(body, out_shape=outs, in_specs=[space] * len(args), out_sp...  12.6 us
    ppermute x13, waiting for transfers between devices, moved(): return lax.ppermute(x, ('tm', 'space'), pairs)  5.82 us
    all_to_all x2, waiting for transfers between devices, exchanged(): got = lax.all_to_all(send, 'space', 0, 0, tiled=True)  4.26 us
    unnamed x10, local copies, waits for them, and re-layouts  2.76 us
  transfers between devices with their start and end apart: 15, of which 5 were waited for; matrix products, arithmetic and copies ran while one was open for 0% of the time, Pallas kernels for 7%

profile of v4, /device:TPU:4, one launch (start us, length us, event | category | flops | bytes accessed | tf_op | source)
XLA Modules:
  0.0 78.3 jit_solution(8015003664820240646)
XLA Ops:
  0.6 0.9 %copy-done = f32[1,2,4,64,128]{4,3,2,1,0:T(8,128)S(1)} copy-done((f32[1,2,4,64,128]{4,3,2,1,0:T(8,128)S(1)}, f32[1,2,4,64,128]{4,3,2,1,0:T(8,128)}, u32[]{:S(2)}) %copy-start) | copy-done | bytes 262168
  1.6 0.9 %copy-done.2 = f32[1,4,64,128]{3,2,1,0:T(8,128)S(1)} copy-done((f32[1,4,64,128]{3,2,1,0:T(8,128)S(1)}, f32[1,4,64,128]{3,2,1,0:T(8,128)}, u32[]{:S(2)}) %copy-start.2) | copy-done | bytes 131096
  2.5 0.9 %copy-done.4 = f32[4,64,128]{2,1,0:T(8,128)S(1)} copy-done((f32[4,64,128]{2,1,0:T(8,128)S(1)}, f32[4,64,128]{2,1,0:T(8,128)}, u32[]{:S(2)}) %copy-start.4) | copy-done | bytes 131096
  3.9 1.7 %collective-permute-start = (f32[4,64,128]{2,1,0:T(8,128)S(1)}, f32[4,64,128]{2,1,0:T(8,128)S(1)}, u32[]{:S(2)}, u32[]{:S(2)}) collective-permute-start(f32[4,64,128]{2,1,0:T(8,128)S(1)} %get-tuple-element.30), channel_id=1, source_target_pairs={{0,1},{1,2},{2,3},{3,4},{4,5},{5,6},{6,7},{7,8},{8,9},{9,10},{10,1... | collective-permute-start | bytes 393224 | tf_op jit(solution)/shard_map/ppermute | solution.py:398
  5.6 6.8 %collective-permute-start.1 = (f32[4,64,128]{2,1,0:T(8,128)S(1)}, f32[4,64,128]{2,1,0:T(8,128)S(1)}, u32[]{:S(2)}, u32[]{:S(2)}) collective-permute-start(f32[4,64,128]{2,1,0:T(8,128)S(1)} %get-tuple-element.31), channel_id=1, source_target_pairs={{0,31},{1,0},{2,1},{3,2},{4,3},{5,4},{6,5},{7,6},{8,7},{9,8},{10,9... | collective-permute-start | bytes 393224 | tf_op jit(solution)/shard_map/ppermute | solution.py:398
  12.4 3.4 %collective-permute-done.lo = f32[4,64,128]{2,1,0:T(8,128)S(1)} collective-permute-done((f32[4,64,128]{2,1,0:T(8,128)S(1)}, f32[4,64,128]{2,1,0:T(8,128)S(1)}, u32[]{:S(2)}, u32[]{:S(2)}) %collective-permute-start) | collective-permute-done | bytes 131104 | tf_op jit(solution)/shard_map/ppermute | solution.py:398
  15.8 1.7 %shard_map.51 = (f32[8,64,128]{2,1,0:T(8,128)S(1)}, f32[3,32,128]{2,1,0:T(8,128)S(1)}, f32[2,32,128]{2,1,0:T(8,128)S(1)}, f32[6,64,128]{2,1,0:T(8,128)S(1)}, f32...) custom-call(f32[4,64,128]{2,1,0:T(8,128)S(1)} %get-tuple-element.28.b_own, ...), custom_call_target="tpu_custom_call" | custom-call | tf_op jit(solution)/shard_map/pallas_call | solution.py:23
  17.5 8.0 %all-to-all-start = ((f32[32,16,128]{2,1,0:T(8,128)}), f32[32,16,128]{2,1,0:T(8,128)S(1)}, u32[]{:S(2)}, u32[]{:S(2)}) async-start(f32[32,16,128]{2,1,0:T(8,128)} %get-tuple-element.32), calls=%async_computation | async-start | bytes 524288 | tf_op jit(solution)/shard_map/all_to_all | solution.py:404
  25.5 5.6 %collective-permute-start.5 = (f32[64,128]{1,0:T(8,128)S(1)}, f32[64,128]{1,0:T(8,128)S(1)}, u32[]{:S(2)}, u32[]{:S(2)}) collective-permute-start(f32[64,128]{1,0:T(8,128)S(1)} %get-tuple-element.34.block), channel_id=1, source_target_pairs={{0,30},{1,31},{2,0},{3,1},{4,2},{5,3},{6,4},{7,5},{8,6},{9,7},{10,... | collective-permute-start | bytes 98312 | tf_op jit(solution)/shard_map/ppermute | solution.py:398
  31.7 4.8 %collective-permute-start.4 = (f32[128,128]{1,0:T(8,128)S(1)}, f32[128,128]{1,0:T(8,128)S(1)}, u32[]{:S(2)}, u32[]{:S(2)}) collective-permute-start(f32[128,128]{1,0:T(8,128)S(1)} %get-tuple-element.36), channel_id=1, source_target_pairs={{0,31},{1,0},{2,1},{3,2},{4,3},{5,4},{6,5},{7,6},{8,7},{9,8},{10,9... | collective-permute-start | bytes 196616 | tf_op jit(solution)/shard_map/ppermute | solution.py:398
  36.4 1.6 %all-to-all-done.got = f32[32,16,128]{2,1,0:T(8,128)S(1)} async-done(((f32[32,16,128]{2,1,0:T(8,128)}), f32[32,16,128]{2,1,0:T(8,128)S(1)}, u32[]{:S(2)}, u32[]{:S(2)}) %all-to-all-start) | async-done | bytes 262176 | tf_op jit(solution)/shard_map/all_to_all | solution.py:404
  38.1 2.8 %shard_map.52 = (f32[128,128]{1,0:T(8,128)S(1)}, f32[128,128]{1,0:T(8,128)S(1)}, f32[32,128]{1,0:T(8,128)S(1)}, f32[128,128]{1,0:T(8,128)S(1)}) custom-call(f32[32,16,128]{2,1,0:T(8,128)S(1)} %all-to-all-done.got), custom_call_target="tpu_custom_call" | custom-call | flops 2147483648 | tf_op jit(solution)/shard_map/pallas_call | solution.py:23
  40.9 1.6 %shard_map.53 = (f32[1,4,64,128]{3,2,1,0:T(8,128)}, f32[4,64,128]{2,1,0:T(8,128)S(1)}, f32[2,64,128]{2,1,0:T(8,128)S(1)}, f32[2,64,128]{2,1,0:T(8,128)S(1)}, f32[5,32,128]{2,1,0:T(8,128)S(1)}) custom-call(f32[128,128]{1,0:T(8,128)S(1)} %get-tuple-element.33.x2, f32[64,128]{1,0:T(8,128)S(1)} %collective-permute-done.2.lo2, ...), custom_call_target="tpu_custom_call" | custom-call | tf_op jit(solution)/shard_map/pallas_call | solution.py:23
  42.6 0.6 collective-permute-start.7
  43.1 5.1 %collective-permute-start.8 = (f32[2,64,128]{2,1,0:T(8,128)S(1)}, f32[2,64,128]{2,1,0:T(8,128)S(1)}, u32[]{:S(2)}, u32[]{:S(2)}) collective-permute-start(f32[2,64,128]{2,1,0:T(8,128)S(1)} %get-tuple-element.42), channel_id=1, source_target_pairs={{0,63},{1,32},{2,33},{3,34},{4,35},{5,36},{6,37},{7,38},{8,39},{9,... | collective-permute-start | bytes 196616 | tf_op jit(solution)/shard_map/ppermute | solution.py:398
  48.3 2.3 %collective-permute-done.7.refs_2_.lo = f32[2,64,128]{2,1,0:T(8,128)S(1)} collective-permute-done((f32[2,64,128]{2,1,0:T(8,128)S(1)}, f32[2,64,128]{2,1,0:T(8,128)S(1)}, u32[]{:S(2)}, u32[]{:S(2)}) %collective-permute-start.7) | collective-permute-done | bytes 65568 | tf_op jit(solution)/shard_map/ppermute | solution.py:398
  50.7 1.7 %shard_map.54 = (f32[6,64,128]{2,1,0:T(8,128)S(1)}, f32[32,16,128]{2,1,0:T(8,128)}, f32[96,128]{1,0:T(8,128)S(1)}, f32[96,128]{1,0:T(8,128)S(1)}, f32[32,128]{1,0:T(8,128)S(1)}) custom-call(f32[4,64,128]{2,1,0:T(8,128)S(1)} %collective-permute-done.6.refs_0_.b_own, f32[4,64,128]{2,1,0:T(8,128)S(1)} %get-tuple-element.29.cap.refs_1_, ...), custom_call_target="tpu_custom_call" | custom-call | tf_op jit(solution)/shard_map/pallas_call | solution.py:23
  52.3 8.0 %all-to-all-start.1 = ((f32[32,16,128]{2,1,0:T(8,128)}), f32[32,16,128]{2,1,0:T(8,128)S(1)}, u32[]{:S(2)}, u32[]{:S(2)}) async-start(f32[32,16,128]{2,1,0:T(8,128)} %get-tuple-element.45), calls=%async_computation.1 | async-start | bytes 524288 | tf_op jit(solution)/shard_map/all_to_all | solution.py:404
  60.3 5.6 %collective-permute-start.12 = (f32[32,128]{1,0:T(8,128)S(1)}, f32[32,128]{1,0:T(8,128)S(1)}, u32[]{:S(2)}, u32[]{:S(2)}) collective-permute-start(f32[32,128]{1,0:T(8,128)S(1)} %get-tuple-element.49.block), channel_id=1, source_target_pairs={{0,30},{1,31},{2,0},{3,1},{4,2},{5,3},{6,4},{7,5},{8,6},{9,7},{10,... | collective-permute-start | bytes 49160 | tf_op jit(solution)/shard_map/ppermute | solution.py:398
  65.9 0.6 collective-permute-start.10
  66.5 4.8 %collective-permute-start.11 = (f32[96,128]{1,0:T(8,128)S(1)}, f32[96,128]{1,0:T(8,128)S(1)}, u32[]{:S(2)}, u32[]{:S(2)}) collective-permute-start(f32[96,128]{1,0:T(8,128)S(1)} %get-tuple-element.51), channel_id=1, source_target_pairs={{0,31},{1,0},{2,1},{3,2},{4,3},{5,4},{6,5},{7,6},{8,7},{9,8},{10,9... | collective-permute-start | bytes 147464 | tf_op jit(solution)/shard_map/ppermute | solution.py:398
  71.3 2.6 %all-to-all-done.1.refs_0_ = f32[32,16,128]{2,1,0:T(8,128)S(1)} async-done(((f32[32,16,128]{2,1,0:T(8,128)}), f32[32,16,128]{2,1,0:T(8,128)S(1)}, u32[]{:S(2)}, u32[]{:S(2)}) %all-to-all-start.1) | async-done | bytes 262176 | tf_op jit(solution)/shard_map/all_to_all | solution.py:404
  73.9 2.7 %shard_map.55.x2 = f32[128,128]{1,0:T(8,128)S(1)} custom-call(f32[32,16,128]{2,1,0:T(8,128)S(1)} %all-to-all-done.1.refs_0_, f32[128,128]{1,0:T(8,128)S(1)} %get-tuple-element.46.refs_1_, f32[128,128]{1,0:T(8,128)S(1)} %get-tuple-element.47.refs_2_, f32[32,128]{1,0:T(8,128)S(1)} %get-tuple-element.48.refs_3_), custom_call_target="tpu_custom_call" | custom-call | flops 2147483648 | tf_op jit(solution)/shard_map/pallas_call | solution.py:23
  76.6 1.6 %shard_map.56 = f32[1,4,64,128]{3,2,1,0:T(8,128)} custom-call(f32[128,128]{1,0:T(8,128)S(1)} %shard_map.55.x2, f32[32,128]{1,0:T(8,128)S(1)} %collective-permute-done.9.lo2, f32[96,128]{1,0:T(8,128)S(1)} %collective-permute-done.10.lo1, f32[32,128]{1,0:T(8,128)S(1)} %get-tuple-element.49.block, f32[96,128]{1,0:T(8,128)S(1)} %collective-permute-done.11.hi1, ...), custom_call_target="tpu_custom_call" | custom-call | tf_op jit(solution)/shard_map/pallas_call | solution.py:23
  (23 shorter events, 1.2 us)
Async XLA Ops:
  0.6 1.0 %copy-start = (f32[1,2,4,64,128]{4,3,2,1,0:T(8,128)S(1)}, f32[1,2,4,64,128]{4,3,2,1,0:T(8,128)}, u32[]{:S(2)}) copy-start(f32[1,2,4,64,128]{4,3,2,1,0:T(8,128)} %src.3) | copy-start | bytes 786436
  1.6 0.9 %copy-start.2 = (f32[1,4,64,128]{3,2,1,0:T(8,128)S(1)}, f32[1,4,64,128]{3,2,1,0:T(8,128)}, u32[]{:S(2)}) copy-start(f32[1,4,64,128]{3,2,1,0:T(8,128)} %start.1) | copy-start | bytes 393220
  2.5 0.9 %copy-start.4 = (f32[4,64,128]{2,1,0:T(8,128)S(1)}, f32[4,64,128]{2,1,0:T(8,128)}, u32[]{:S(2)}) copy-start(f32[4,64,128]{2,1,0:T(8,128)} %cap.1) | copy-start | bytes 393220
  3.9 11.9 %collective-permute-start = (f32[4,64,128]{2,1,0:T(8,128)S(1)}, f32[4,64,128]{2,1,0:T(8,128)S(1)}, u32[]{:S(2)}, u32[]{:S(2)}) collective-permute-start(f32[4,64,128]{2,1,0:T(8,128)S(1)} %get-tuple-element.30), channel_id=1, source_target_pairs={{0,1},{1,2},{2,3},{3,4},{4,5},{5,6},{6,7},{7,8},{8,9},{9,10},{10,1... | collective-permute-start | bytes 393224 | tf_op jit(solution)/shard_map/ppermute | solution.py:398
  5.6 10.2 %collective-permute-start.1 = (f32[4,64,128]{2,1,0:T(8,128)S(1)}, f32[4,64,128]{2,1,0:T(8,128)S(1)}, u32[]{:S(2)}, u32[]{:S(2)}) collective-permute-start(f32[4,64,128]{2,1,0:T(8,128)S(1)} %get-tuple-element.31), channel_id=1, source_target_pairs={{0,31},{1,0},{2,1},{3,2},{4,3},{5,4},{6,5},{7,6},{8,7},{9,8},{10,9... | collective-permute-start | bytes 393224 | tf_op jit(solution)/shard_map/ppermute | solution.py:398
  17.5 20.6 %all-to-all-start = ((f32[32,16,128]{2,1,0:T(8,128)}), f32[32,16,128]{2,1,0:T(8,128)S(1)}, u32[]{:S(2)}, u32[]{:S(2)}) async-start(f32[32,16,128]{2,1,0:T(8,128)} %get-tuple-element.32), calls=%async_computation | async-start | bytes 524288 | tf_op jit(solution)/shard_map/all_to_all | solution.py:404
  25.5 15.3 %collective-permute-start.5 = (f32[64,128]{1,0:T(8,128)S(1)}, f32[64,128]{1,0:T(8,128)S(1)}, u32[]{:S(2)}, u32[]{:S(2)}) collective-permute-start(f32[64,128]{1,0:T(8,128)S(1)} %get-tuple-element.34.block), channel_id=1, source_target_pairs={{0,30},{1,31},{2,0},{3,1},{4,2},{5,3},{6,4},{7,5},{8,6},{9,7},{10,... | collective-permute-start | bytes 98312 | tf_op jit(solution)/shard_map/ppermute | solution.py:398
  31.1 9.8 %collective-permute-start.2 = (f32[64,128]{1,0:T(8,128)S(1)}, f32[64,128]{1,0:T(8,128)S(1)}, u32[]{:S(2)}, u32[]{:S(2)}) collective-permute-start(f32[64,128]{1,0:T(8,128)S(1)} %get-tuple-element.34.block), channel_id=1, source_target_pairs={{0,2},{1,3},{2,4},{3,5},{4,6},{5,7},{6,8},{7,9},{8,10},{9,11},{10,... | collective-permute-start | bytes 98312 | tf_op jit(solution)/shard_map/ppermute | solution.py:398
  31.1 9.8 %collective-permute-start.3 = (f32[128,128]{1,0:T(8,128)S(1)}, f32[128,128]{1,0:T(8,128)S(1)}, u32[]{:S(2)}, u32[]{:S(2)}) collective-permute-start(f32[128,128]{1,0:T(8,128)S(1)} %get-tuple-element.35), channel_id=1, source_target_pairs={{0,1},{1,2},{2,3},{3,4},{4,5},{5,6},{6,7},{7,8},{8,9},{9,10},{10,1... | collective-permute-start | bytes 196616 | tf_op jit(solution)/shard_map/ppermute | solution.py:398
  31.7 9.2 %copy-start.1 = (f32[1,2,4,64,128]{4,3,2,1,0:T(8,128)S(1)}, f32[1,2,4,64,128]{4,3,2,1,0:T(8,128)}, u32[]{:S(2)}) copy-start(f32[1,2,4,64,128]{4,3,2,1,0:T(8,128)} %src.3) | copy-start | bytes 786436
  31.7 9.2 %collective-permute-start.4 = (f32[128,128]{1,0:T(8,128)S(1)}, f32[128,128]{1,0:T(8,128)S(1)}, u32[]{:S(2)}, u32[]{:S(2)}) collective-permute-start(f32[128,128]{1,0:T(8,128)S(1)} %get-tuple-element.36), channel_id=1, source_target_pairs={{0,31},{1,0},{2,1},{3,2},{4,3},{5,4},{6,5},{7,6},{8,7},{9,8},{10,9... | collective-permute-start | bytes 196616 | tf_op jit(solution)/shard_map/ppermute | solution.py:398
  42.6 8.1 %collective-permute-start.6 = (f32[4,64,128]{2,1,0:T(8,128)S(1)}, f32[4,64,128]{2,1,0:T(8,128)S(1)}, u32[]{:S(2)}, u32[]{:S(2)}) collective-permute-start(f32[4,64,128]{2,1,0:T(8,128)S(1)} %get-tuple-element.40), channel_id=1, source_target_pairs={{0,32},{1,33},{2,34},{3,35},{4,36},{5,37},{6,38},{7,39},{8,40},{9,... | collective-permute-start | bytes 393224 | tf_op jit(solution)/shard_map/ppermute | solution.py:398
  42.6 8.0 %collective-permute-start.7 = (f32[2,64,128]{2,1,0:T(8,128)S(1)}, f32[2,64,128]{2,1,0:T(8,128)S(1)}, u32[]{:S(2)}, u32[]{:S(2)}) collective-permute-start(f32[2,64,128]{2,1,0:T(8,128)S(1)} %get-tuple-element.41), channel_id=1, source_target_pairs={{0,33},{1,34},{2,35},{3,36},{4,37},{5,38},{6,39},{7,40},{8,41},{9,... | collective-permute-start | bytes 196616 | tf_op jit(solution)/shard_map/ppermute | solution.py:398
  43.1 7.5 %collective-permute-start.8 = (f32[2,64,128]{2,1,0:T(8,128)S(1)}, f32[2,64,128]{2,1,0:T(8,128)S(1)}, u32[]{:S(2)}, u32[]{:S(2)}) collective-permute-start(f32[2,64,128]{2,1,0:T(8,128)S(1)} %get-tuple-element.42), channel_id=1, source_target_pairs={{0,63},{1,32},{2,33},{3,34},{4,35},{5,36},{6,37},{7,38},{8,39},{9,... | collective-permute-start | bytes 196616 | tf_op jit(solution)/shard_map/ppermute | solution.py:398
  52.3 21.6 %all-to-all-start.1 = ((f32[32,16,128]{2,1,0:T(8,128)}), f32[32,16,128]{2,1,0:T(8,128)S(1)}, u32[]{:S(2)}, u32[]{:S(2)}) async-start(f32[32,16,128]{2,1,0:T(8,128)} %get-tuple-element.45), calls=%async_computation.1 | async-start | bytes 524288 | tf_op jit(solution)/shard_map/all_to_all | solution.py:404
  60.3 16.2 %collective-permute-start.12 = (f32[32,128]{1,0:T(8,128)S(1)}, f32[32,128]{1,0:T(8,128)S(1)}, u32[]{:S(2)}, u32[]{:S(2)}) collective-permute-start(f32[32,128]{1,0:T(8,128)S(1)} %get-tuple-element.49.block), channel_id=1, source_target_pairs={{0,30},{1,31},{2,0},{3,1},{4,2},{5,3},{6,4},{7,5},{8,6},{9,7},{10,... | collective-permute-start | bytes 49160 | tf_op jit(solution)/shard_map/ppermute | solution.py:398
  65.9 10.7 %collective-permute-start.9 = (f32[32,128]{1,0:T(8,128)S(1)}, f32[32,128]{1,0:T(8,128)S(1)}, u32[]{:S(2)}, u32[]{:S(2)}) collective-permute-start(f32[32,128]{1,0:T(8,128)S(1)} %get-tuple-element.49.block), channel_id=1, source_target_pairs={{0,2},{1,3},{2,4},{3,5},{4,6},{5,7},{6,8},{7,9},{8,10},{9,11},{10,... | collective-permute-start | bytes 49160 | tf_op jit(solution)/shard_map/ppermute | solution.py:398
  65.9 10.7 %collective-permute-start.10 = (f32[96,128]{1,0:T(8,128)S(1)}, f32[96,128]{1,0:T(8,128)S(1)}, u32[]{:S(2)}, u32[]{:S(2)}) collective-permute-start(f32[96,128]{1,0:T(8,128)S(1)} %get-tuple-element.50), channel_id=1, source_target_pairs={{0,1},{1,2},{2,3},{3,4},{4,5},{5,6},{6,7},{7,8},{8,9},{9,10},{10,1... | collective-permute-start | bytes 147464 | tf_op jit(solution)/shard_map/ppermute | solution.py:398
  66.5 10.1 %collective-permute-start.11 = (f32[96,128]{1,0:T(8,128)S(1)}, f32[96,128]{1,0:T(8,128)S(1)}, u32[]{:S(2)}, u32[]{:S(2)}) collective-permute-start(f32[96,128]{1,0:T(8,128)S(1)} %get-tuple-element.51), channel_id=1, source_target_pairs={{0,31},{1,0},{2,1},{3,2},{4,3},{5,4},{6,5},{7,6},{8,7},{9,8},{10,9... | collective-permute-start | bytes 147464 | tf_op jit(solution)/shard_map/ppermute | solution.py:398
  73.9 2.7 %copy-start.3 = (f32[1,4,64,128]{3,2,1,0:T(8,128)S(1)}, f32[1,4,64,128]{3,2,1,0:T(8,128)}, u32[]{:S(2)}) copy-start(f32[1,4,64,128]{3,2,1,0:T(8,128)} %start.1) | copy-start | bytes 393220

commit v5 on v4

--- a/solution.py
+++ b/solution.py
@@ -4,6 +4,7 @@
 from jax.experimental import pallas as pl
 from jax.experimental.pallas import tpu as pltpu
 from jax.sharding import PartitionSpec as P
+
 
 COARSE_SWEEPS = 24
 NY, NX = 64, 128
@@ -140,7 +141,7 @@
     return 1.2 * y + 0.5 * w * around_block(y, below, above)
 
 
-def fine_down(first, b_own, cap, lo, hi, w, w1, c1, xs, send, up, dn, block, ys, rs):
+def fine_down(first, b_own, cap, lo, hi, w, w1, c1, xs, up, dn, block, ys, rs):
     lane = iota((32, 128), 1)
     lo_pick = picks(lambda i, j: (i >> 1) == j, 0.125)
     hi_pick = picks(lambda i, j: (i >> 1) + 64 == j, 0.125)
@@ -180,7 +181,6 @@
         low += [row_pairs(rs, 128, 32), row_pairs(rs, 256, 32)]
         high += [row_pairs(rs, 192, 32), row_pairs(rs, 320, 32)]
     blocks = dot(jnp.concatenate(low, 0), lo_pick) + dot(jnp.concatenate(high, 0), hi_pick)
-    b1 = blocks[:32]
     if first:
         c1[0], c1[1] = blocks[32:64], blocks[64:]
         wide = OMEGA / (blocks[64:] + 3.0)
@@ -194,7 +194,10 @@
     up[pl.ds(rows, 64), :] = xs[3]
     dn[pl.ds(rows, 64), :] = xs[2]
 
+
+def share_body(block, w1, c1, send, rs):
     zero = jnp.zeros((32, 128), F32)
+    b1 = block[pl.ds(0, 32), :]
     y = w1[1] * b1
     x = [
         block_sweep(zero, w1[0], zero, y),
@@ -297,7 +300,7 @@
 def fine_up(x2, near, first, b_own, lo, hi, w, xs, w1, work, out):
     f1, y1, xa, xb, f0, x0, x9 = work
     s = lax.axis_index("space")
-    lo2, lo1, block, hi1, hi2 = near
+    _, lo1, _, hi1, _ = near
     for j, ref in enumerate(near):
         if first:
             v = OMEGA / (ref[pl.ds(32, 32), :] + 3.0)
@@ -398,9 +401,12 @@
     return lax.ppermute(x, ("tm", "space"), pairs)
 
 
-def exchanged(send, up, dn, block):
-    lo1, hi1 = moved(up, 0, 1), moved(dn, 0, -1)
-    lo2, hi2 = moved(block, 0, 2), moved(block, 0, -2)
+def exchanged(up, dn, block, w1, c1):
+    lo1 = moved(up, 0, 1)
+    hi1 = moved(dn, 0, -1)
+    lo2 = moved(block, 0, 2)
+    hi2 = moved(block, 0, -2)
+    (send,) = call(share_body, (MESSAGE,), [(128, 128)], block, w1, c1)
     got = lax.all_to_all(send, "space", 0, 0, tiled=True)
     return got, lo2, lo1, block, hi1, hi2
 
@@ -410,19 +416,18 @@
         pack_body,
         (f32(4, *PLANE),) * 4,
         [PLANE4, PLANE4],
-        *(u0, src, cap),
+        *(pltpu.with_memory_space_constraint(x, pltpu.HBM) for x in (u0, src, cap)),
         space=pl.BlockSpec(memory_space=pltpu.HBM),
         sems=[pltpu.SemaphoreType.DMA((3,))],
     )
     lo, hi = moved(up, 0, 1), moved(dn, 0, -1)
-    w, w1, c1, xs, send, up, dn, block = call(
+    w, w1, c1, xs, up, dn, block = call(
         first_down_body,
         (
             f32(8, *PLANE),
             f32(3, 32, 128),
             f32(2, 32, 128),
             f32(6, *PLANE),
-            MESSAGE,
             f32(128, 128),
             f32(128, 128),
             f32(64, 128),
@@ -430,7 +435,7 @@
         DOWN_WORK,
         *(b, cap, lo, hi),
     )
-    got, *near = exchanged(send, up, dn, block)
+    got, *near = exchanged(up, dn, block, w1, c1)
     w2, d2, w3, x2 = call(
         first_low_body,
         (f32(128, 128), f32(128, 128), f32(32, 128), f32(128, 128)),
@@ -445,13 +450,13 @@
         *(x2, *near, b, lo, hi, w, xs, cap, src),
     )
     b, lo, hi = moved(b, 1, 0), moved(up, 1, 1), moved(dn, 1, -1)
-    xs, send, up, dn, block = call(
+    xs, up, dn, block = call(
         next_down_body,
-        (f32(6, *PLANE), MESSAGE, f32(96, 128), f32(96, 128), f32(32, 128)),
+        (f32(6, *PLANE), f32(96, 128), f32(96, 128), f32(32, 128)),
         DOWN_WORK,
         *(b, cap, lo, hi, w, w1, c1),
     )
-    got, *near = exchanged(send, up, dn, block)
+    got, *near = exchanged(up, dn, block, w1, c1)
     (x2,) = call(next_low_body, (f32(128, 128),), LOW_WORK, *(got, w2, d2, w3), flops=LOW_FLOPS)
     (updated,) = call(
         next_up_body, (f32(1, *PLANE4),), WORK, *(x2, *near, b, lo, hi, w, xs, v1, u0)

time: 78.6 us -> 76.2 us (0.969)
  local copies, waits for them, and re-layouts: 2.76 us -> 0.01 us
    unnamed x10 -> x4, local copies, waits for them, and re-layouts: 2.76 us -> 0.01 us
    pallas_call x7 -> x9, Pallas kernels: 12.6 us -> 13 us  [call(): pl.pallas_call(body, out_shape=outs, in_specs=[space] * len(args), out_sp...]
where the time goes in v5:
time: 76.2 us; the launch traced here: 75.9 us
  starting transfers between devices  52 us (68%)
  Pallas kernels  13 us (17%)
  waiting for transfers between devices  10.1 us (13%)
  between operations  0.77 us (1%)
    ppermute x13, starting transfers between devices, moved(): return lax.ppermute(x, ('tm', 'space'), pairs)  36 us
    all_to_all x2, starting transfers between devices, exchanged(): got = lax.all_to_all(send, 'space', 0, 0, tiled=True)  16 us
    pallas_call x9, Pallas kernels, call(): pl.pallas_call(body, out_shape=outs, in_specs=[space] * len(args), out_sp...  13 us
    ppermute x13, waiting for transfers between devices, moved(): return lax.ppermute(x, ('tm', 'space'), pairs)  5.82 us
    all_to_all x2, waiting for transfers between devices, exchanged(): got = lax.all_to_all(send, 'space', 0, 0, tiled=True)  4.25 us
  transfers between devices with their start and end apart: 15, of which 5 were waited for; matrix products, arithmetic and copies ran while one was open for 0% of the time, Pallas kernels for 7%

profile of v5, /device:TPU:4, one launch (start us, length us, event | category | flops | bytes accessed | tf_op | source)
XLA Modules:
  0.0 75.9 jit_solution(6338478635999835646)
XLA Ops:
  0.6 1.1 %shard_map.50 = (f32[4,64,128]{2,1,0:T(8,128)S(1)}, f32[4,64,128]{2,1,0:T(8,128)S(1)}, f32[4,64,128]{2,1,0:T(8,128)S(1)}, f32[4,64,128]{2,1,0:T(8,128)S(1)}) custom-call(f32[1,4,64,128]{3,2,1,0:T(8,128)} %start.1, f32[1,2,4,64,128]{4,3,2,1,0:T(8,128)} %src.3, f32[4,64,128]{2,1,0:T(8,128)} %cap.1), custom_call_target="tpu_custom_call" | custom-call | tf_op jit(solution)/shard_map/pallas_call | solution.py:24
  1.7 1.7 %collective-permute-start = (f32[4,64,128]{2,1,0:T(8,128)S(1)}, f32[4,64,128]{2,1,0:T(8,128)S(1)}, u32[]{:S(2)}, u32[]{:S(2)}) collective-permute-start(f32[4,64,128]{2,1,0:T(8,128)S(1)} %get-tuple-element.28), channel_id=1, source_target_pairs={{0,1},{1,2},{2,3},{3,4},{4,5},{5,6},{6,7},{7,8},{8,9},{9,10},{10,1... | collective-permute-start | bytes 393224 | tf_op jit(solution)/shard_map/ppermute | solution.py:401
  3.4 6.8 %collective-permute-start.1 = (f32[4,64,128]{2,1,0:T(8,128)S(1)}, f32[4,64,128]{2,1,0:T(8,128)S(1)}, u32[]{:S(2)}, u32[]{:S(2)}) collective-permute-start(f32[4,64,128]{2,1,0:T(8,128)S(1)} %get-tuple-element.29), channel_id=1, source_target_pairs={{0,31},{1,0},{2,1},{3,2},{4,3},{5,4},{6,5},{7,6},{8,7},{9,8},{10,9... | collective-permute-start | bytes 393224 | tf_op jit(solution)/shard_map/ppermute | solution.py:401
  10.2 3.4 %collective-permute-done.lo = f32[4,64,128]{2,1,0:T(8,128)S(1)} collective-permute-done((f32[4,64,128]{2,1,0:T(8,128)S(1)}, f32[4,64,128]{2,1,0:T(8,128)S(1)}, u32[]{:S(2)}, u32[]{:S(2)}) %collective-permute-start) | collective-permute-done | bytes 131104 | tf_op jit(solution)/shard_map/ppermute | solution.py:401
  13.6 0.5 shard_map.51
  14.2 1.1 %shard_map.52 = f32[32,16,128]{2,1,0:T(8,128)} custom-call(f32[64,128]{1,0:T(8,128)S(1)} %get-tuple-element.30.block, f32[3,32,128]{2,1,0:T(8,128)S(1)} %get-tuple-element.31.w1.refs_5_, f32[2,32,128]{2,1,0:T(8,128)S(1)} %get-tuple-element.32.c1.refs_6_), custom_call_target="tpu_custom_call" | custom-call | tf_op jit(solution)/shard_map/pallas_call | solution.py:24
  15.2 8.0 %all-to-all-start = ((f32[32,16,128]{2,1,0:T(8,128)}), f32[32,16,128]{2,1,0:T(8,128)S(1)}, u32[]{:S(2)}, u32[]{:S(2)}) async-start(f32[32,16,128]{2,1,0:T(8,128)} %shard_map.52), calls=%async_computation | async-start | bytes 524288 | tf_op jit(solution)/shard_map/all_to_all | solution.py:410
  23.3 5.6 %collective-permute-start.5 = (f32[64,128]{1,0:T(8,128)S(1)}, f32[64,128]{1,0:T(8,128)S(1)}, u32[]{:S(2)}, u32[]{:S(2)}) collective-permute-start(f32[64,128]{1,0:T(8,128)S(1)} %get-tuple-element.30.block), channel_id=1, source_target_pairs={{0,30},{1,31},{2,0},{3,1},{4,2},{5,3},{6,4},{7,5},{8,6},{9,7},{10,... | collective-permute-start | bytes 98312 | tf_op jit(solution)/shard_map/ppermute | solution.py:401
  28.8 0.6 collective-permute-start.3
  29.4 4.8 %collective-permute-start.4 = (f32[128,128]{1,0:T(8,128)S(1)}, f32[128,128]{1,0:T(8,128)S(1)}, u32[]{:S(2)}, u32[]{:S(2)}) collective-permute-start(f32[128,128]{1,0:T(8,128)S(1)} %get-tuple-element.35), channel_id=1, source_target_pairs={{0,31},{1,0},{2,1},{3,2},{4,3},{5,4},{6,5},{7,6},{8,7},{9,8},{10,9... | collective-permute-start | bytes 196616 | tf_op jit(solution)/shard_map/ppermute | solution.py:401
  34.2 1.6 %all-to-all-done.got = f32[32,16,128]{2,1,0:T(8,128)S(1)} async-done(((f32[32,16,128]{2,1,0:T(8,128)}), f32[32,16,128]{2,1,0:T(8,128)S(1)}, u32[]{:S(2)}, u32[]{:S(2)}) %all-to-all-start) | async-done | bytes 262176 | tf_op jit(solution)/shard_map/all_to_all | solution.py:410
  35.8 2.8 %shard_map.53 = (f32[128,128]{1,0:T(8,128)S(1)}, f32[128,128]{1,0:T(8,128)S(1)}, f32[32,128]{1,0:T(8,128)S(1)}, f32[128,128]{1,0:T(8,128)S(1)}) custom-call(f32[32,16,128]{2,1,0:T(8,128)S(1)} %all-to-all-done.got), custom_call_target="tpu_custom_call" | custom-call | flops 2147483648 | tf_op jit(solution)/shard_map/pallas_call | solution.py:24
  38.6 1.6 %shard_map.54 = (f32[1,4,64,128]{3,2,1,0:T(8,128)}, f32[4,64,128]{2,1,0:T(8,128)S(1)}, f32[2,64,128]{2,1,0:T(8,128)S(1)}, f32[2,64,128]{2,1,0:T(8,128)S(1)}, f32[5,32,128]{2,1,0:T(8,128)S(1)}) custom-call(f32[128,128]{1,0:T(8,128)S(1)} %get-tuple-element.33.x2, f32[64,128]{1,0:T(8,128)S(1)} %collective-permute-done.2.lo2, ...), custom_call_target="tpu_custom_call" | custom-call | tf_op jit(solution)/shard_map/pallas_call | solution.py:24
  40.3 0.6 collective-permute-start.7
  40.9 5.1 %collective-permute-start.8 = (f32[2,64,128]{2,1,0:T(8,128)S(1)}, f32[2,64,128]{2,1,0:T(8,128)S(1)}, u32[]{:S(2)}, u32[]{:S(2)}) collective-permute-start(f32[2,64,128]{2,1,0:T(8,128)S(1)} %get-tuple-element.41), channel_id=1, source_target_pairs={{0,63},{1,32},{2,33},{3,34},{4,35},{5,36},{6,37},{7,38},{8,39},{9,... | collective-permute-start | bytes 196616 | tf_op jit(solution)/shard_map/ppermute | solution.py:401
  46.0 2.3 %collective-permute-done.7.refs_2_.lo = f32[2,64,128]{2,1,0:T(8,128)S(1)} collective-permute-done((f32[2,64,128]{2,1,0:T(8,128)S(1)}, f32[2,64,128]{2,1,0:T(8,128)S(1)}, u32[]{:S(2)}, u32[]{:S(2)}) %collective-permute-start.7) | collective-permute-done | bytes 65568 | tf_op jit(solution)/shard_map/ppermute | solution.py:401
  48.9 1.1 %shard_map.56 = f32[32,16,128]{2,1,0:T(8,128)} custom-call(f32[32,128]{1,0:T(8,128)S(1)} %get-tuple-element.42.block, f32[3,32,128]{2,1,0:T(8,128)S(1)} %get-tuple-element.31.w1.refs_5_, f32[2,32,128]{2,1,0:T(8,128)S(1)} %get-tuple-element.32.c1.refs_6_), custom_call_target="tpu_custom_call" | custom-call | tf_op jit(solution)/shard_map/pallas_call | solution.py:24
  50.0 8.0 %all-to-all-start.1 = ((f32[32,16,128]{2,1,0:T(8,128)}), f32[32,16,128]{2,1,0:T(8,128)S(1)}, u32[]{:S(2)}, u32[]{:S(2)}) async-start(f32[32,16,128]{2,1,0:T(8,128)} %shard_map.56), calls=%async_computation.1 | async-start | bytes 524288 | tf_op jit(solution)/shard_map/all_to_all | solution.py:410
  58.0 5.6 %collective-permute-start.12 = (f32[32,128]{1,0:T(8,128)S(1)}, f32[32,128]{1,0:T(8,128)S(1)}, u32[]{:S(2)}, u32[]{:S(2)}) collective-permute-start(f32[32,128]{1,0:T(8,128)S(1)} %get-tuple-element.42.block), channel_id=1, source_target_pairs={{0,30},{1,31},{2,0},{3,1},{4,2},{5,3},{6,4},{7,5},{8,6},{9,7},{10,... | collective-permute-start | bytes 49160 | tf_op jit(solution)/shard_map/ppermute | solution.py:401
  63.6 0.6 collective-permute-start.10
  64.1 4.8 %collective-permute-start.11 = (f32[96,128]{1,0:T(8,128)S(1)}, f32[96,128]{1,0:T(8,128)S(1)}, u32[]{:S(2)}, u32[]{:S(2)}) collective-permute-start(f32[96,128]{1,0:T(8,128)S(1)} %get-tuple-element.47), channel_id=1, source_target_pairs={{0,31},{1,0},{2,1},{3,2},{4,3},{5,4},{6,5},{7,6},{8,7},{9,8},{10,9... | collective-permute-start | bytes 147464 | tf_op jit(solution)/shard_map/ppermute | solution.py:401
  68.9 2.6 %all-to-all-done.1.refs_0_ = f32[32,16,128]{2,1,0:T(8,128)S(1)} async-done(((f32[32,16,128]{2,1,0:T(8,128)}), f32[32,16,128]{2,1,0:T(8,128)S(1)}, u32[]{:S(2)}, u32[]{:S(2)}) %all-to-all-start.1) | async-done | bytes 262176 | tf_op jit(solution)/shard_map/all_to_all | solution.py:410
  71.6 2.7 %shard_map.57.x2 = f32[128,128]{1,0:T(8,128)S(1)} custom-call(f32[32,16,128]{2,1,0:T(8,128)S(1)} %all-to-all-done.1.refs_0_, f32[128,128]{1,0:T(8,128)S(1)} %get-tuple-element.43.refs_1_, f32[128,128]{1,0:T(8,128)S(1)} %get-tuple-element.44.refs_2_, f32[32,128]{1,0:T(8,128)S(1)} %get-tuple-element.45.refs_3_), custom_call_target="tpu_custom_call" | custom-call | flops 2147483648 | tf_op jit(solution)/shard_map/pallas_call | solution.py:24
  74.3 1.6 %shard_map.58 = f32[1,4,64,128]{3,2,1,0:T(8,128)} custom-call(f32[128,128]{1,0:T(8,128)S(1)} %shard_map.57.x2, f32[32,128]{1,0:T(8,128)S(1)} %collective-permute-done.9.lo2, f32[96,128]{1,0:T(8,128)S(1)} %collective-permute-done.10.lo1, f32[32,128]{1,0:T(8,128)S(1)} %get-tuple-element.42.block, f32[96,128]{1,0:T(8,128)S(1)} %collective-permute-done.11.hi1, ...), custom_call_target="tpu_custom_call" | custom-call | tf_op jit(solution)/shard_map/pallas_call | solution.py:24
  (19 shorter events, 0.6 us)
Async XLA Ops:
  1.7 11.9 %collective-permute-start = (f32[4,64,128]{2,1,0:T(8,128)S(1)}, f32[4,64,128]{2,1,0:T(8,128)S(1)}, u32[]{:S(2)}, u32[]{:S(2)}) collective-permute-start(f32[4,64,128]{2,1,0:T(8,128)S(1)} %get-tuple-element.28), channel_id=1, source_target_pairs={{0,1},{1,2},{2,3},{3,4},{4,5},{5,6},{6,7},{7,8},{8,9},{9,10},{10,1... | collective-permute-start | bytes 393224 | tf_op jit(solution)/shard_map/ppermute | solution.py:401
  3.4 10.2 %collective-permute-start.1 = (f32[4,64,128]{2,1,0:T(8,128)S(1)}, f32[4,64,128]{2,1,0:T(8,128)S(1)}, u32[]{:S(2)}, u32[]{:S(2)}) collective-permute-start(f32[4,64,128]{2,1,0:T(8,128)S(1)} %get-tuple-element.29), channel_id=1, source_target_pairs={{0,31},{1,0},{2,1},{3,2},{4,3},{5,4},{6,5},{7,6},{8,7},{9,8},{10,9... | collective-permute-start | bytes 393224 | tf_op jit(solution)/shard_map/ppermute | solution.py:401
  15.2 20.6 %all-to-all-start = ((f32[32,16,128]{2,1,0:T(8,128)}), f32[32,16,128]{2,1,0:T(8,128)S(1)}, u32[]{:S(2)}, u32[]{:S(2)}) async-start(f32[32,16,128]{2,1,0:T(8,128)} %shard_map.52), calls=%async_computation | async-start | bytes 524288 | tf_op jit(solution)/shard_map/all_to_all | solution.py:410
  23.3 15.3 %collective-permute-start.5 = (f32[64,128]{1,0:T(8,128)S(1)}, f32[64,128]{1,0:T(8,128)S(1)}, u32[]{:S(2)}, u32[]{:S(2)}) collective-permute-start(f32[64,128]{1,0:T(8,128)S(1)} %get-tuple-element.30.block), channel_id=1, source_target_pairs={{0,30},{1,31},{2,0},{3,1},{4,2},{5,3},{6,4},{7,5},{8,6},{9,7},{10,... | collective-permute-start | bytes 98312 | tf_op jit(solution)/shard_map/ppermute | solution.py:401
  28.8 9.8 %collective-permute-start.2 = (f32[64,128]{1,0:T(8,128)S(1)}, f32[64,128]{1,0:T(8,128)S(1)}, u32[]{:S(2)}, u32[]{:S(2)}) collective-permute-start(f32[64,128]{1,0:T(8,128)S(1)} %get-tuple-element.30.block), channel_id=1, source_target_pairs={{0,2},{1,3},{2,4},{3,5},{4,6},{5,7},{6,8},{7,9},{8,10},{9,11},{10,... | collective-permute-start | bytes 98312 | tf_op jit(solution)/shard_map/ppermute | solution.py:401
  28.8 9.8 %collective-permute-start.3 = (f32[128,128]{1,0:T(8,128)S(1)}, f32[128,128]{1,0:T(8,128)S(1)}, u32[]{:S(2)}, u32[]{:S(2)}) collective-permute-start(f32[128,128]{1,0:T(8,128)S(1)} %get-tuple-element.34), channel_id=1, source_target_pairs={{0,1},{1,2},{2,3},{3,4},{4,5},{5,6},{6,7},{7,8},{8,9},{9,10},{10,1... | collective-permute-start | bytes 196616 | tf_op jit(solution)/shard_map/ppermute | solution.py:401
  29.4 9.2 %copy-start = (f32[1,2,4,64,128]{4,3,2,1,0:T(8,128)S(1)}, f32[1,2,4,64,128]{4,3,2,1,0:T(8,128)}, u32[]{:S(2)}) copy-start(f32[1,2,4,64,128]{4,3,2,1,0:T(8,128)} %src.3) | copy-start | bytes 786436
  29.4 9.2 %collective-permute-start.4 = (f32[128,128]{1,0:T(8,128)S(1)}, f32[128,128]{1,0:T(8,128)S(1)}, u32[]{:S(2)}, u32[]{:S(2)}) collective-permute-start(f32[128,128]{1,0:T(8,128)S(1)} %get-tuple-element.35), channel_id=1, source_target_pairs={{0,31},{1,0},{2,1},{3,2},{4,3},{5,4},{6,5},{7,6},{8,7},{9,8},{10,9... | collective-permute-start | bytes 196616 | tf_op jit(solution)/shard_map/ppermute | solution.py:401
  40.3 8.1 %collective-permute-start.6 = (f32[4,64,128]{2,1,0:T(8,128)S(1)}, f32[4,64,128]{2,1,0:T(8,128)S(1)}, u32[]{:S(2)}, u32[]{:S(2)}) collective-permute-start(f32[4,64,128]{2,1,0:T(8,128)S(1)} %get-tuple-element.39), channel_id=1, source_target_pairs={{0,32},{1,33},{2,34},{3,35},{4,36},{5,37},{6,38},{7,39},{8,40},{9,... | collective-permute-start | bytes 393224 | tf_op jit(solution)/shard_map/ppermute | solution.py:401
  40.3 8.0 %collective-permute-start.7 = (f32[2,64,128]{2,1,0:T(8,128)S(1)}, f32[2,64,128]{2,1,0:T(8,128)S(1)}, u32[]{:S(2)}, u32[]{:S(2)}) collective-permute-start(f32[2,64,128]{2,1,0:T(8,128)S(1)} %get-tuple-element.40), channel_id=1, source_target_pairs={{0,33},{1,34},{2,35},{3,36},{4,37},{5,38},{6,39},{7,40},{8,41},{9,... | collective-permute-start | bytes 196616 | tf_op jit(solution)/shard_map/ppermute | solution.py:401
  40.9 7.5 %collective-permute-start.8 = (f32[2,64,128]{2,1,0:T(8,128)S(1)}, f32[2,64,128]{2,1,0:T(8,128)S(1)}, u32[]{:S(2)}, u32[]{:S(2)}) collective-permute-start(f32[2,64,128]{2,1,0:T(8,128)S(1)} %get-tuple-element.41), channel_id=1, source_target_pairs={{0,63},{1,32},{2,33},{3,34},{4,35},{5,36},{6,37},{7,38},{8,39},{9,... | collective-permute-start | bytes 196616 | tf_op jit(solution)/shard_map/ppermute | solution.py:401
  50.0 21.6 %all-to-all-start.1 = ((f32[32,16,128]{2,1,0:T(8,128)}), f32[32,16,128]{2,1,0:T(8,128)S(1)}, u32[]{:S(2)}, u32[]{:S(2)}) async-start(f32[32,16,128]{2,1,0:T(8,128)} %shard_map.56), calls=%async_computation.1 | async-start | bytes 524288 | tf_op jit(solution)/shard_map/all_to_all | solution.py:410
  58.0 16.2 %collective-permute-start.12 = (f32[32,128]{1,0:T(8,128)S(1)}, f32[32,128]{1,0:T(8,128)S(1)}, u32[]{:S(2)}, u32[]{:S(2)}) collective-permute-start(f32[32,128]{1,0:T(8,128)S(1)} %get-tuple-element.42.block), channel_id=1, source_target_pairs={{0,30},{1,31},{2,0},{3,1},{4,2},{5,3},{6,4},{7,5},{8,6},{9,7},{10,... | collective-permute-start | bytes 49160 | tf_op jit(solution)/shard_map/ppermute | solution.py:401
  63.6 10.7 %collective-permute-start.9 = (f32[32,128]{1,0:T(8,128)S(1)}, f32[32,128]{1,0:T(8,128)S(1)}, u32[]{:S(2)}, u32[]{:S(2)}) collective-permute-start(f32[32,128]{1,0:T(8,128)S(1)} %get-tuple-element.42.block), channel_id=1, source_target_pairs={{0,2},{1,3},{2,4},{3,5},{4,6},{5,7},{6,8},{7,9},{8,10},{9,11},{10,... | collective-permute-start | bytes 49160 | tf_op jit(solution)/shard_map/ppermute | solution.py:401
  63.6 10.7 %collective-permute-start.10 = (f32[96,128]{1,0:T(8,128)S(1)}, f32[96,128]{1,0:T(8,128)S(1)}, u32[]{:S(2)}, u32[]{:S(2)}) collective-permute-start(f32[96,128]{1,0:T(8,128)S(1)} %get-tuple-element.46), channel_id=1, source_target_pairs={{0,1},{1,2},{2,3},{3,4},{4,5},{5,6},{6,7},{7,8},{8,9},{9,10},{10,1... | collective-permute-start | bytes 147464 | tf_op jit(solution)/shard_map/ppermute | solution.py:401
  64.1 10.1 %collective-permute-start.11 = (f32[96,128]{1,0:T(8,128)S(1)}, f32[96,128]{1,0:T(8,128)S(1)}, u32[]{:S(2)}, u32[]{:S(2)}) collective-permute-start(f32[96,128]{1,0:T(8,128)S(1)} %get-tuple-element.47), channel_id=1, source_target_pairs={{0,31},{1,0},{2,1},{3,2},{4,3},{5,4},{6,5},{7,6},{8,7},{9,8},{10,9... | collective-permute-start | bytes 147464 | tf_op jit(solution)/shard_map/ppermute | solution.py:401
  71.6 2.7 %copy-start.1 = (f32[1,4,64,128]{3,2,1,0:T(8,128)S(1)}, f32[1,4,64,128]{3,2,1,0:T(8,128)}, u32[]{:S(2)}) copy-start(f32[1,4,64,128]{3,2,1,0:T(8,128)} %start.1) | copy-start | bytes 393220

commit v6 on v4

--- a/solution.py
+++ b/solution.py
@@ -31,8 +31,14 @@
     )(*args)
 
 
-def dot(a, b):
-    return jnp.dot(a, b, precision=lax.Precision.HIGHEST, preferred_element_type=F32)
+def dot(a, pick):
+    high = a.astype(jnp.bfloat16)
+    rest = a - high.astype(F32)
+    middle = rest.astype(jnp.bfloat16)
+    low = (rest - middle.astype(F32)).astype(jnp.bfloat16)
+    rows = a.shape[0]
+    out = jnp.dot(jnp.concatenate([high, middle, low], 0), pick, preferred_element_type=F32)
+    return (out[2 * rows :] + out[rows : 2 * rows]) + out[:rows]
 
 
 def iota(shape, axis):
@@ -41,16 +47,19 @@
 
 def picks(test, scale):
     i, j = iota((128, 128), 0), iota((128, 128), 1)
-    return jnp.where(test(i, j), jnp.float32(scale), jnp.float32(0.0))
-
-
-def around_plane(c, below, above):
+    return jnp.where(test(i, j), jnp.float32(scale), jnp.float32(0.0)).astype(jnp.bfloat16)
+
+
+def inside_plane(c):
     row, lane = iota(c.shape, 0), iota(c.shape, 1)
-    total = below + above
-    total = total + jnp.where(lane > 0, pltpu.roll(c, 1, 1), 0.0)
+    total = jnp.where(lane > 0, pltpu.roll(c, 1, 1), 0.0)
     total = total + jnp.where(lane < NX - 1, pltpu.roll(c, NX - 1, 1), 0.0)
     total = total + jnp.where(row > 0, pltpu.roll(c, 1, 0), 0.0)
     return total + jnp.where(row < NY - 1, pltpu.roll(c, NY - 1, 0), 0.0)
+
+
+def around_plane(c, below, above):
+    return inside_plane(c) + (below + above)
 
 
 def around_block(c, below, above):
@@ -113,7 +122,54 @@
     return jnp.concatenate(v, 0)
 
 
-def pack_body(u, src, cap, b_out, up, dn, cap_out, u_in, src_in, sems):
+def row_pairs(ref, start, count):
+    return ref[pl.ds(start, count, stride=2), :] + ref[pl.ds(start + 1, count, stride=2), :]
+
+
+def block_sweep(y, w, below, above):
+    return 1.2 * y + 0.5 * w * around_block(y, below, above)
+
+
+def plane_picks():
+    return (
+        picks(lambda i, j: (i >> 1) == j, 0.125),
+        picks(lambda i, j: (i >> 1) + 64 == j, 0.125),
+    )
+
+
+def local_down(b, cap, w, y, x, rs, lo_pick, hi_pick, first):
+    for p in range(DEPTH):
+        y[p] = w[p] * b(p)
+    zero = jnp.zeros((NY, NX), F32)
+    for p in range(DEPTH):
+        below = y[p - 1] if p > 0 else zero
+        above = y[p + 1] if p < 3 else zero
+        x[p] = 1.2 * y[p] + w[p] * around_plane(y[p], below, above)
+    for half in range(2):
+        total = None
+        for p in (2 * half, 2 * half + 1):
+            below = x[p - 1] if p > 0 else zero
+            above = x[p + 1] if p < 3 else zero
+            r = b(p) - (cap[p] + 6.0) * x[p] + around_plane(x[p], below, above)
+            total = r if total is None else total + r
+        rs[pl.ds(64 * half, 64), :] = total
+        if first:
+            rs[pl.ds(128 + 64 * half, 64), :] = cap[2 * half] + cap[2 * half + 1]
+    low, high = row_pairs(rs, 0, 32), row_pairs(rs, 64, 32)
+    if first:
+        low = jnp.concatenate([low, row_pairs(rs, 128, 32)], 0)
+        high = jnp.concatenate([high, row_pairs(rs, 192, 32)], 0)
+    return dot(low, lo_pick) + dot(high, hi_pick)
+
+
+def fill_edges(up, dn, y, x):
+    for edge, p, q in ((up, 3, 2), (dn, 0, 1)):
+        edge[pl.ds(0, 64), :] = y[p]
+        edge[pl.ds(64, 64), :] = x[p]
+        edge[pl.ds(128, 64), :] = x[q]
+
+
+def pack_body(u, src, cap, w, y, x, block, up, dn, cap_out, u_in, src_in, rs, sems):
     copies = [
         pltpu.make_async_copy(cap, cap_out, sems.at[0]),
         pltpu.make_async_copy(u.at[0], u_in, sems.at[1]),
@@ -121,92 +177,88 @@
     ]
     for copy in copies:
         copy.start()
+    lo_pick, hi_pick = plane_picks()
     for copy in copies:
         copy.wait()
     for p in range(DEPTH):
-        c = cap_out[p]
-        b = c * u_in[p] + src_in[p]
-        b_out[p] = b
-        ends, i = (dn, p) if p < 2 else (up, p - 2)
-        ends[i] = b
-        ends[i + 2] = c
-
-
-def row_pairs(ref, start, count):
-    return ref[pl.ds(start, count, stride=2), :] + ref[pl.ds(start + 1, count, stride=2), :]
-
-
-def block_sweep(y, w, below, above):
-    return 1.2 * y + 0.5 * w * around_block(y, below, above)
-
-
-def fine_down(first, b_own, cap, lo, hi, w, w1, c1, xs, send, up, dn, block, ys, rs):
+        w[p] = OMEGA / (cap_out[p] + 6.0)
+        u_in[p] = cap_out[p] * u_in[p] + src_in[p]
+    blocks = local_down(lambda p: u_in[p], cap_out, w, y, x, rs, lo_pick, hi_pick, True)
+    block[...] = blocks
+    fill_edges(up, dn, y, x)
     lane = iota((32, 128), 1)
-    lo_pick = picks(lambda i, j: (i >> 1) == j, 0.125)
-    hi_pick = picks(lambda i, j: (i >> 1) + 64 == j, 0.125)
-
-    def b(p):
-        return lo[p + 2] if p < 0 else (b_own[p] if p < DEPTH else hi[p - DEPTH])
-
-    def c(p):
-        return lo[p + 4] if p < 0 else (cap[p] if p < DEPTH else hi[p - 2])
-
+    b1, c1 = blocks[:32], blocks[32:]
+    up[pl.ds(192, 32), :] = jnp.where(lane < 64, pltpu.roll(b1, 64, 1), c1)
+    dn[pl.ds(192, 32), :] = jnp.where(lane < 64, b1, pltpu.roll(c1, 64, 1))
+    up[pl.ds(224, 64), :] = w[3]
+    dn[pl.ds(224, 64), :] = w[0]
+
+
+def finish_down(first, w, y, x, b1, c1, lo, hi, wx, yx, xs, pair, send, rs, lo_pick, hi_pick):
+    s = lax.axis_index("space")
+    lane = iota((32, 128), 1)
+
+    def edge(ref, there):
+        return [
+            jnp.where(there, ref[pl.ds(start, 64), :], 0.0)
+            for start in ((0, 64, 128, 224) if first else (0, 64, 128))
+        ]
+
+    sides = []
+    for ref, there, i, p in ((lo, s > 0, 0, 0), (hi, s < SLABS - 1, 5, 3)):
+        ye, xe, xs_far, *we = edge(ref, there)
+        if first:
+            wx[i] = we[0]
+        yx[i] = ye
+        near = w[p] * ye
+        far = wx[i] * y[p]
+        x_near, x_far = x[p] + near, xe + far
+        j = 1 if p == 0 else 6
+        xs[j] = x_far
+        xs[0 if p == 0 else 7] = xs_far
+        xs[p + 2] = x_near
+        own = (near - OMEGA * ye) + inside_plane(near) + x_far
+        beside = (far - OMEGA * y[p]) + inside_plane(far) + x_near
+        sides.append((own, jnp.where(there, beside, 0.0)))
+    for p in range(DEPTH):
+        yx[p + 1] = y[p]
+        if first:
+            wx[p + 1] = w[p]
+    xs[3] = x[1]
+    xs[4] = x[2]
+    for k, v in enumerate((sides[0][0], sides[1][1], sides[1][0], sides[0][1])):
+        rs[pl.ds(64 * k, 64), :] = v
+    low = jnp.concatenate([row_pairs(rs, 0, 32), row_pairs(rs, 64, 32)], 0)
+    high = jnp.concatenate([row_pairs(rs, 128, 32), row_pairs(rs, 192, 32)], 0)
+    terms = dot(low, lo_pick) + dot(high, hi_pick)
+    lo_block, hi_block = lo[pl.ds(192, 32), :], hi[pl.ds(192, 32), :]
     if first:
-        s = lax.axis_index("space")
-        for p in range(-2, 6):
-            v = OMEGA / (c(p) + 6.0)
-            if p < 0:
-                v = jnp.where(s > 0, v, 0.0)
-            if p >= DEPTH:
-                v = jnp.where(s < SLABS - 1, v, 0.0)
-            w[p + 2] = v
-    for p in range(-2, 6):
-        ys[p + 2] = w[p + 2] * b(p)
-    for p in range(-1, 5):
-        i = p + 2
-        xs[p + 1] = 1.2 * ys[i] + w[i] * around_plane(ys[i], ys[i - 1], ys[i + 1])
-    for half in range(2):
-        total = None
-        for p in (2 * half, 2 * half + 1):
-            i = p + 1
-            r = b(p) - (cap[p] + 6.0) * xs[i] + around_plane(xs[i], xs[i - 1], xs[i + 1])
-            total = r if total is None else total + r
-        rs[pl.ds(64 * half, 64), :] = total
-    if first:
-        for k, p in enumerate((0, 2, 4, -2)):
-            rs[pl.ds(128 + 64 * k, 64), :] = c(p) + c(p + 1)
-    low, high = [row_pairs(rs, 0, 32)], [row_pairs(rs, 64, 32)]
-    if first:
-        low += [row_pairs(rs, 128, 32), row_pairs(rs, 256, 32)]
-        high += [row_pairs(rs, 192, 32), row_pairs(rs, 320, 32)]
-    blocks = dot(jnp.concatenate(low, 0), lo_pick) + dot(jnp.concatenate(high, 0), hi_pick)
-    b1 = blocks[:32]
-    if first:
-        c1[0], c1[1] = blocks[32:64], blocks[64:]
-        wide = OMEGA / (blocks[64:] + 3.0)
-        w1[0] = jnp.where((lane >= 64) & (s > 0), wide, 0.0)
-        w1[1] = OMEGA / (blocks[32:64] + 3.0)
-        w1[2] = jnp.where((lane < 64) & (s < SLABS - 1), wide, 0.0)
-    rows = 64 if first else 32
-    block[...] = blocks[:rows]
-    up[pl.ds(0, rows), :] = blocks[:rows]
-    dn[pl.ds(0, rows), :] = blocks[:rows]
-    up[pl.ds(rows, 64), :] = xs[3]
-    dn[pl.ds(rows, 64), :] = xs[2]
-
+        pair[pl.ds(64, 32), :] = c1
+        pair[pl.ds(96, 32), :] = jnp.where(lane < 64, pltpu.roll(hi_block, 64, 1), lo_block)
+        lo_block = pltpu.roll(lo_block, 64, 1)
+    own = b1 + terms[:32]
+    pair[pl.ds(0, 32), :] = own
+    pair[pl.ds(32, 32), :] = jnp.where(lane < 64, hi_block, lo_block) + terms[32:]
+    return own
+
+
+def share(b1, c1, c_mix, send, rs):
+    s = lax.axis_index("space")
+    lane = iota((32, 128), 1)
     zero = jnp.zeros((32, 128), F32)
-    y = w1[1] * b1
+    own, beside = c1 + 3.0, c_mix + 3.0
+    w_own, w_mix = OMEGA / own, OMEGA / beside
+    y = w_own * b1
     x = [
-        block_sweep(zero, w1[0], zero, y),
-        block_sweep(y, w1[1], zero, zero),
-        block_sweep(zero, w1[2], y, zero),
+        block_sweep(zero, jnp.where((lane >= 64) & (s > 0), w_mix, 0.0), zero, y),
+        block_sweep(y, w_own, zero, zero),
+        block_sweep(zero, jnp.where((lane < 64) & (s < SLABS - 1), w_mix, 0.0), y, zero),
     ]
-    own, beside = c1[0] + 3.0, c1[1] + 3.0
     r = [
         0.5 * around_block(x[0], zero, x[1]) - beside * x[0],
         b1 - own * x[1] + 0.5 * around_block(x[1], x[0], x[2]),
         0.5 * around_block(x[2], x[1], zero) - beside * x[2],
-        c1[0],
+        c1,
     ]
     for k in range(4):
         rs[pl.ds(32 * k, 32), :] = r[k]
@@ -219,12 +271,19 @@
         send[peer] = message
 
 
-def first_down_body(b_own, cap, lo, hi, *rest):
-    fine_down(True, b_own, cap, lo, hi, *rest)
-
-
-def next_down_body(*refs):
-    fine_down(False, *refs)
+def first_down_body(w, y, x, block, lo, hi, wx, yx, xs, pair, send, rs):
+    b1, c1 = block[pl.ds(0, 32), :], block[pl.ds(32, 32), :]
+    own = finish_down(True, w, y, x, b1, c1, lo, hi, wx, yx, xs, pair, send, rs, *plane_picks())
+    share(own, c1, pair[pl.ds(96, 32), :], send, rs)
+
+
+def next_down_body(b, lo, hi, cap, w, wx, old, yx, xs, pair, send, y, x, rs):
+    lo_pick, hi_pick = plane_picks()
+    b1 = local_down(lambda p: b[p], cap, w, y, x, rs, lo_pick, hi_pick, False)
+    own = finish_down(
+        False, w, y, x, b1, None, lo, hi, wx, yx, xs, pair, send, rs, lo_pick, hi_pick
+    )
+    share(own, old[pl.ds(64, 32), :], old[pl.ds(96, 32), :], send, rs)
 
 
 def spread(v):
@@ -294,16 +353,27 @@
     low_levels(False, *refs)
 
 
-def fine_up(x2, near, first, b_own, lo, hi, w, xs, w1, work, out):
+def fine_up(x2, lo2, pair, hi2, first, wx, yx, xs, w1, work, out):
     f1, y1, xa, xb, f0, x0, x9 = work
     s = lax.axis_index("space")
-    lo2, lo1, block, hi1, hi2 = near
-    for j, ref in enumerate(near):
-        if first:
-            v = OMEGA / (ref[pl.ds(32, 32), :] + 3.0)
+    lane = iota((32, 128), 1)
+
+    def blocks(start):
+        mixed = [ref[pl.ds(start + 32, 32), :] for ref in (lo2, pair, hi2)]
+        return (
+            lo2[pl.ds(start, 32), :],
+            jnp.where(lane < 64, mixed[0], mixed[1]),
+            pair[pl.ds(start, 32), :],
+            jnp.where(lane < 64, mixed[1], mixed[2]),
+            hi2[pl.ds(start, 32), :],
+        )
+
+    if first:
+        for j, c in enumerate(blocks(64)):
             z = s + (j - 2)
-            w1[j] = jnp.where((z >= 0) & (z < SLABS), v, 0.0)
-        y1[j] = w1[j] * ref[pl.ds(0, 32), :]
+            w1[j] = jnp.where((z >= 0) & (z < SLABS), OMEGA / (c + 3.0), 0.0)
+    for j, b in enumerate(blocks(0)):
+        y1[j] = w1[j] * b
     zero = jnp.zeros((32, 128), F32)
     group = iota((16, 128), 1) >> 5
     parts = []
@@ -332,45 +402,37 @@
     for q, v in enumerate((high[:32], low[:32], high[32:], low[32:])):
         f0[pl.ds(64 * q, 32, stride=2), :] = v
         f0[pl.ds(64 * q + 1, 32, stride=2), :] = v
-    rows = 64 if first else 32
-    far_below = jnp.where(s > 0, lo1[pl.ds(rows, 64), :], 0.0)
-    far_above = jnp.where(s < SLABS - 1, hi1[pl.ds(rows, 64), :], 0.0)
     for i in range(8):
-        v = far_below if i == 0 else (far_above if i == 7 else xs[i - 1])
-        x0[i] = v + f0[pl.ds(64 * (i // 2), 64), :]
-    for p in range(-1, 5):
-        i = p + 2
-        b = lo[1] if p < 0 else (b_own[p] if p < DEPTH else hi[0])
-        c = x0[i]
-        x9[p + 1] = 0.2 * c + w[i] * (b + around_plane(c, x0[i - 1], x0[i + 1]))
+        x0[i] = xs[i] + f0[pl.ds(64 * (i // 2), 64), :]
+    for i in range(6):
+        c = x0[i + 1]
+        x9[i] = 0.2 * c + yx[i] + wx[i] * around_plane(c, x0[i], x0[i + 2])
     for p in range(DEPTH):
         c = x9[p + 1]
-        u = 0.2 * c + w[p + 2] * (b_own[p] + around_plane(c, x9[p], x9[p + 2]))
-        out(p, u)
+        out(p, 0.2 * c + yx[p + 1] + wx[p + 1] * around_plane(c, x9[p], x9[p + 2]))
 
 
 def first_up_body(
-    x2, lo2, lo1, block, hi1, hi2, b_own, lo, hi, w, xs, cap, src, u_out, b_out, up, dn, w1, *work
+    x2, lo2, pair, hi2, wx, yx, xs, w, cap, src, u_out, b_out, up, dn, w1, y, x, rs, *work
 ):
     def out(p, u):
         u_out[0, p] = u
-        b = cap[p] * u + src[0, 1, p]
-        b_out[p] = b
-        ends, i = (dn, p) if p < 2 else (up, p - 2)
-        ends[i] = b
-
-    near = (lo2, lo1, block, hi1, hi2)
-    fine_up(x2, near, True, b_own, lo, hi, w, xs, w1, work, out)
-
-
-def next_up_body(x2, lo2, lo1, block, hi1, hi2, b_own, lo, hi, w, xs, w1, start, u_out, *work):
+        b_out[p] = cap[p] * u + src[0, 1, p]
+
+    fine_up(x2, lo2, pair, hi2, True, wx, yx, xs, w1, work, out)
+    block = local_down(lambda p: b_out[p], cap, w, y, x, rs, *plane_picks(), False)
+    fill_edges(up, dn, y, x)
+    up[pl.ds(192, 32), :] = block
+    dn[pl.ds(192, 32), :] = block
+
+
+def next_up_body(x2, lo2, pair, hi2, wx, yx, xs, w1, start, u_out, *work):
     keep = lax.axis_index("tm") == 0
 
     def out(p, u):
         u_out[0, p] = jnp.where(keep, start[0, p], u)
 
-    near = (lo2, lo1, block, hi1, hi2)
-    fine_up(x2, near, False, b_own, lo, hi, w, xs, w1, work, out)
+    fine_up(x2, lo2, pair, hi2, False, wx, yx, xs, w1, work, out)
 
 
 LOW_WORK = [(64, 128)]
@@ -384,7 +446,7 @@
     (8, NY, NX),
     (6, NY, NX),
 ]
-DOWN_WORK = [(8, NY, NX), (384, 128)]
+EDGE_SUMS = (256, 128)
 PLANE = (NY, NX)
 PLANE4 = (DEPTH, NY, NX)
 MESSAGE = f32(SLABS, 16, 128)
@@ -398,39 +460,29 @@
     return lax.ppermute(x, ("tm", "space"), pairs)
 
 
-def exchanged(send, up, dn, block):
-    lo1, hi1 = moved(up, 0, 1), moved(dn, 0, -1)
-    lo2, hi2 = moved(block, 0, 2), moved(block, 0, -2)
+def exchanged(send, pair):
     got = lax.all_to_all(send, "space", 0, 0, tiled=True)
-    return got, lo2, lo1, block, hi1, hi2
+    return got, moved(pair, 0, 2), pair, moved(pair, 0, -2)
 
 
 def shards(u0, src, cap):
-    b, up, dn, cap = call(
+    slab = f32(*PLANE4)
+    w, y, x, block, up, dn, cap_in = call(
         pack_body,
-        (f32(4, *PLANE),) * 4,
-        [PLANE4, PLANE4],
-        *(u0, src, cap),
+        (slab, slab, slab, f32(64, 128), f32(288, 128), f32(288, 128), slab),
+        [PLANE4, PLANE4, EDGE_SUMS],
+        *(pltpu.with_memory_space_constraint(v, pltpu.HBM) for v in (u0, src, cap)),
         space=pl.BlockSpec(memory_space=pltpu.HBM),
         sems=[pltpu.SemaphoreType.DMA((3,))],
     )
     lo, hi = moved(up, 0, 1), moved(dn, 0, -1)
-    w, w1, c1, xs, send, up, dn, block = call(
+    wx, yx, xs, pair, send = call(
         first_down_body,
-        (
-            f32(8, *PLANE),
-            f32(3, 32, 128),
-            f32(2, 32, 128),
-            f32(6, *PLANE),
-            MESSAGE,
-            f32(128, 128),
-            f32(128, 128),
-            f32(64, 128),
-        ),
-        DOWN_WORK,
-        *(b, cap, lo, hi),
-    )
-    got, *near = exchanged(send, up, dn, block)
+        (f32(6, *PLANE), f32(6, *PLANE), f32(8, *PLANE), f32(128, 128), MESSAGE),
+        [EDGE_SUMS],
+        *(w, y, x, block, lo, hi),
+    )
+    got, *near = exchanged(send, pair)
     w2, d2, w3, x2 = call(
         first_low_body,
         (f32(128, 128), f32(128, 128), f32(32, 128), f32(128, 128)),
@@ -438,23 +490,23 @@
         got,
         flops=LOW_FLOPS,
     )
-    fpoint, b, up, dn, v1 = call(
+    fpoint, b, up, dn, w1 = call(
         first_up_body,
-        (f32(1, *PLANE4), f32(*PLANE4), f32(2, *PLANE), f32(2, *PLANE), f32(5, 32, 128)),
-        WORK,
-        *(x2, *near, b, lo, hi, w, xs, cap, src),
+        (f32(1, *PLANE4), slab, f32(224, 128), f32(224, 128), f32(5, 32, 128)),
+        [PLANE4, PLANE4, EDGE_SUMS, *WORK],
+        *(x2, *near, wx, yx, xs, w, cap_in, src),
     )
     b, lo, hi = moved(b, 1, 0), moved(up, 1, 1), moved(dn, 1, -1)
-    xs, send, up, dn, block = call(
+    yx, xs, pair, send = call(
         next_down_body,
-        (f32(6, *PLANE), MESSAGE, f32(96, 128), f32(96, 128), f32(32, 128)),
-        DOWN_WORK,
-        *(b, cap, lo, hi, w, w1, c1),
-    )
-    got, *near = exchanged(send, up, dn, block)
+        (f32(6, *PLANE), f32(8, *PLANE), f32(64, 128), MESSAGE),
+        [PLANE4, PLANE4, EDGE_SUMS],
+        *(b, lo, hi, cap_in, w, wx, pair),
+    )
+    got, *near = exchanged(send, pair)
     (x2,) = call(next_low_body, (f32(128, 128),), LOW_WORK, *(got, w2, d2, w3), flops=LOW_FLOPS)
     (updated,) = call(
-        next_up_body, (f32(1, *PLANE4),), WORK, *(x2, *near, b, lo, hi, w, xs, v1, u0)
+        next_up_body, (f32(1, *PLANE4),), WORK, *(x2, *near, wx, yx, xs, w1, u0)
     )
     return fpoint, updated
 

time: 78.6 us -> 77.5 us (0.986)
  waiting for transfers between devices: 10.1 us -> 22.1 us
  starting transfers between devices: 52 us -> 41.3 us
  local copies, waits for them, and re-layouts: 2.76 us -> 0.01 us
    ppermute x13 -> x9, starting transfers between devices: 36 us -> 25.3 us  [moved(): return lax.ppermute(x, ('tm', 'space'), pairs)]
    all_to_all x2, waiting for transfers between devices: 4.26 us -> 14.8 us  [exchanged(): got = lax.all_to_all(send, 'space', 0, 0, tiled=True)]
    unnamed x10 -> x4, local copies, waits for them, and re-layouts: 2.76 us -> 0.01 us
    ppermute x13 -> x9, waiting for transfers between devices: 5.82 us -> 7.21 us  [moved(): return lax.ppermute(x, ('tm', 'space'), pairs)]
  transfers between devices with their start and end apart: 15 -> 11, of which waited for: 5 -> 4; matrix products, arithmetic and copies ran while one was open for 0% -> 0% of each run, Pallas kernels for 7% -> 7%
where the time goes in v6:
time: 77.5 us; the launch traced here: 77.2 us
  starting transfers between devices  41.3 us (53%)
  waiting for transfers between devices  22.1 us (29%)
  Pallas kernels  13.1 us (17%)
    ppermute x9, starting transfers between devices, moved(): return lax.ppermute(x, ('tm', 'space'), pairs)  25.3 us
    all_to_all x2, starting transfers between devices, exchanged(): got = lax.all_to_all(send, 'space', 0, 0, tiled=True)  16 us
    all_to_all x2, waiting for transfers between devices, exchanged(): got = lax.all_to_all(send, 'space', 0, 0, tiled=True)  14.8 us
    pallas_call x7, Pallas kernels, call(): pl.pallas_call(body, out_shape=outs, in_specs=[space] * len(args), out_sp...  13.1 us
    ppermute x9, waiting for transfers between devices, moved(): return lax.ppermute(x, ('tm', 'space'), pairs)  7.21 us
  transfers between devices with their start and end apart: 11, of which 4 were waited for; matrix products, arithmetic and copies ran while one was open for 0% of the time, Pallas kernels for 7%

profile of v6, /device:TPU:4, one launch (start us, length us, event | category | flops | bytes accessed | tf_op | source)
XLA Modules:
  0.0 77.2 jit_solution(14935296298684856299)
XLA Ops:
  0.6 1.5 %shard_map.50 = (f32[4,64,128]{2,1,0:T(8,128)S(1)}, f32[4,64,128]{2,1,0:T(8,128)S(1)}, f32[4,64,128]{2,1,0:T(8,128)S(1)}, f32[64,128]{1,0:T(8,128)S(1)}, f32[288...) custom-call(f32[1,4,64,128]{3,2,1,0:T(8,128)} %start.1, f32[1,2,4,64,128]{4,3,2,1,0:T(8,128)} %src.3, ...), custom_call_target="tpu_custom_call" | custom-call | tf_op jit(solution)/shard_map/pallas_call | solution.py:23
  2.2 1.7 %collective-permute-start = (f32[288,128]{1,0:T(8,128)S(1)}, f32[288,128]{1,0:T(8,128)S(1)}, u32[]{:S(2)}, u32[]{:S(2)}) collective-permute-start(f32[288,128]{1,0:T(8,128)S(1)} %get-tuple-element.31), channel_id=1, source_target_pairs={{0,1},{1,2},{2,3},{3,4},{4,5},{5,6},{6,7},{7,8},{8,9},{9,10},{10,1... | collective-permute-start | bytes 442376 | tf_op jit(solution)/shard_map/ppermute | solution.py:460
  3.8 6.8 %collective-permute-start.1 = (f32[288,128]{1,0:T(8,128)S(1)}, f32[288,128]{1,0:T(8,128)S(1)}, u32[]{:S(2)}, u32[]{:S(2)}) collective-permute-start(f32[288,128]{1,0:T(8,128)S(1)} %get-tuple-element.32), channel_id=1, source_target_pairs={{0,31},{1,0},{2,1},{3,2},{4,3},{5,4},{6,5},{7,6},{8,7},{9,8},{10,9... | collective-permute-start | bytes 442376 | tf_op jit(solution)/shard_map/ppermute | solution.py:460
  10.6 3.8 %collective-permute-done.lo = f32[288,128]{1,0:T(8,128)S(1)} collective-permute-done((f32[288,128]{1,0:T(8,128)S(1)}, f32[288,128]{1,0:T(8,128)S(1)}, u32[]{:S(2)}, u32[]{:S(2)}) %collective-permute-start) | collective-permute-done | bytes 147488 | tf_op jit(solution)/shard_map/ppermute | solution.py:460
  14.4 0.0 collective-permute-done.1.hi
  14.4 1.4 %shard_map.51 = (f32[6,64,128]{2,1,0:T(8,128)S(1)}, f32[6,64,128]{2,1,0:T(8,128)S(1)}, f32[8,64,128]{2,1,0:T(8,128)S(1)}, f32[128,128]{1,0:T(8,128)S(1)}, f32[32,16,128]{2,1,0:T(8,128)}) custom-call(f32[4,64,128]{2,1,0:T(8,128)S(1)} %get-tuple-element.27.w, f32[4,64,128]{2,1,0:T(8,128)S(1)} %get-tuple-element.28.y, f32[4,64,128]{2,1,0:T(8,128)S(1)} %get-tuple-element.29.x, ...), custom_call_target="tpu_custom_call" | custom-call | tf_op jit(solution)/shard_map/pallas_call | solution.py:23
  15.8 8.0 %all-to-all-start = ((f32[32,16,128]{2,1,0:T(8,128)}), f32[32,16,128]{2,1,0:T(8,128)S(1)}, u32[]{:S(2)}, u32[]{:S(2)}) async-start(f32[32,16,128]{2,1,0:T(8,128)} %get-tuple-element.33), calls=%async_computation | async-start | bytes 524288 | tf_op jit(solution)/shard_map/all_to_all | solution.py:464
  23.8 0.0 copy-start
  23.8 5.6 %collective-permute-start.3 = (f32[128,128]{1,0:T(8,128)S(1)}, f32[128,128]{1,0:T(8,128)S(1)}, u32[]{:S(2)}, u32[]{:S(2)}) collective-permute-start(f32[128,128]{1,0:T(8,128)S(1)} %get-tuple-element.35.pair.old), channel_id=1, source_target_pairs={{0,30},{1,31},{2,0},{3,1},{4,2},{5,3},{6,4},{7,5},{8,6},{9,7},{10,... | collective-permute-start | bytes 196616 | tf_op jit(solution)/shard_map/ppermute | solution.py:460
  29.3 0.0 collective-permute-start.2
  29.3 7.0 %all-to-all-done.got = f32[32,16,128]{2,1,0:T(8,128)S(1)} async-done(((f32[32,16,128]{2,1,0:T(8,128)}), f32[32,16,128]{2,1,0:T(8,128)S(1)}, u32[]{:S(2)}, u32[]{:S(2)}) %all-to-all-start) | async-done | bytes 262176 | tf_op jit(solution)/shard_map/all_to_all | solution.py:464
  36.4 2.7 %shard_map.52 = (f32[128,128]{1,0:T(8,128)S(1)}, f32[128,128]{1,0:T(8,128)S(1)}, f32[32,128]{1,0:T(8,128)S(1)}, f32[128,128]{1,0:T(8,128)S(1)}) custom-call(f32[32,16,128]{2,1,0:T(8,128)S(1)} %all-to-all-done.got), custom_call_target="tpu_custom_call" | custom-call | flops 2147483648 | tf_op jit(solution)/shard_map/pallas_call | solution.py:23
  39.1 0.0 collective-permute-done.2.lo2
  39.2 1.8 %shard_map.53 = (f32[1,4,64,128]{3,2,1,0:T(8,128)}, f32[4,64,128]{2,1,0:T(8,128)S(1)}, f32[224,128]{1,0:T(8,128)S(1)}, f32[224,128]{1,0:T(8,128)S(1)}, f32[5,32,128]{2,1,0:T(8,128)S(1)}) custom-call(f32[128,128]{1,0:T(8,128)S(1)} %get-tuple-element.34.x2, f32[128,128]{1,0:T(8,128)S(1)} %collective-permute-done.2.lo2, ...), custom_call_target="tpu_custom_call" | custom-call | tf_op jit(solution)/shard_map/pallas_call | solution.py:23
  40.9 0.5 collective-permute-start.5
  41.4 5.2 %collective-permute-start.6 = (f32[224,128]{1,0:T(8,128)S(1)}, f32[224,128]{1,0:T(8,128)S(1)}, u32[]{:S(2)}, u32[]{:S(2)}) collective-permute-start(f32[224,128]{1,0:T(8,128)S(1)} %get-tuple-element.43), channel_id=1, source_target_pairs={{0,63},{1,32},{2,33},{3,34},{4,35},{5,36},{6,37},{7,38},{8,39},{9,... | collective-permute-start | bytes 344072 | tf_op jit(solution)/shard_map/ppermute | solution.py:460
  46.6 3.4 %collective-permute-done.5.lo = f32[224,128]{1,0:T(8,128)S(1)} collective-permute-done((f32[224,128]{1,0:T(8,128)S(1)}, f32[224,128]{1,0:T(8,128)S(1)}, u32[]{:S(2)}, u32[]{:S(2)}) %collective-permute-start.5) | collective-permute-done | bytes 114720 | tf_op jit(solution)/shard_map/ppermute | solution.py:460
  50.0 0.0 collective-permute-done.6.hi
  50.0 1.5 %shard_map.54 = (f32[6,64,128]{2,1,0:T(8,128)S(1)}, f32[8,64,128]{2,1,0:T(8,128)S(1)}, f32[64,128]{1,0:T(8,128)S(1)}, f32[32,16,128]{2,1,0:T(8,128)}) custom-call(f32[4,64,128]{2,1,0:T(8,128)S(1)} %collective-permute-done.4.b, f32[224,128]{1,0:T(8,128)S(1)} %collective-permute-done.5.lo, f32[224,128]{1,0:T(8,128)S(1)} %collective-permute-done.6.hi, ...), custom_call_target="tpu_custom_call" | custom-call | tf_op jit(solution)/shard_map/pallas_call | solution.py:23
  51.6 8.0 %all-to-all-start.1 = ((f32[32,16,128]{2,1,0:T(8,128)}), f32[32,16,128]{2,1,0:T(8,128)S(1)}, u32[]{:S(2)}, u32[]{:S(2)}) async-start(f32[32,16,128]{2,1,0:T(8,128)} %get-tuple-element.44), calls=%async_computation.1 | async-start | bytes 524288 | tf_op jit(solution)/shard_map/all_to_all | solution.py:464
  59.6 5.6 %collective-permute-start.8 = (f32[64,128]{1,0:T(8,128)S(1)}, f32[64,128]{1,0:T(8,128)S(1)}, u32[]{:S(2)}, u32[]{:S(2)}) collective-permute-start(f32[64,128]{1,0:T(8,128)S(1)} %get-tuple-element.48.pair), channel_id=1, source_target_pairs={{0,30},{1,31},{2,0},{3,1},{4,2},{5,3},{6,4},{7,5},{8,6},{9,7},{10,... | collective-permute-start | bytes 98312 | tf_op jit(solution)/shard_map/ppermute | solution.py:460
  65.2 7.8 %all-to-all-done.1.refs_0_ = f32[32,16,128]{2,1,0:T(8,128)S(1)} async-done(((f32[32,16,128]{2,1,0:T(8,128)}), f32[32,16,128]{2,1,0:T(8,128)S(1)}, u32[]{:S(2)}, u32[]{:S(2)}) %all-to-all-start.1) | async-done | bytes 262176 | tf_op jit(solution)/shard_map/all_to_all | solution.py:464
  73.0 2.6 %shard_map.55.x2 = f32[128,128]{1,0:T(8,128)S(1)} custom-call(f32[32,16,128]{2,1,0:T(8,128)S(1)} %all-to-all-done.1.refs_0_, f32[128,128]{1,0:T(8,128)S(1)} %get-tuple-element.45.refs_1_, f32[128,128]{1,0:T(8,128)S(1)} %get-tuple-element.46.refs_2_, f32[32,128]{1,0:T(8,128)S(1)} %get-tuple-element.47.refs_3_), custom_call_target="tpu_custom_call" | custom-call | flops 2147483648 | tf_op jit(solution)/shard_map/pallas_call | solution.py:23
  75.6 1.6 %shard_map.56 = f32[1,4,64,128]{3,2,1,0:T(8,128)} custom-call(f32[128,128]{1,0:T(8,128)S(1)} %shard_map.55.x2, f32[64,128]{1,0:T(8,128)S(1)} %collective-permute-done.7.lo2, f32[64,128]{1,0:T(8,128)S(1)} %get-tuple-element.48.pair, f32[64,128]{1,0:T(8,128)S(1)} %collective-permute-done.8.hi2, f32[6,64,128]{2,1,0:T(8,128)S(1)} %get-tuple-element.36.wx, ...), custom_call_target="tpu_custom_call" | custom-call | tf_op jit(solution)/shard_map/pallas_call | solution.py:23
  (9 shorter events, 0.0 us)
Async XLA Ops:
  2.2 12.2 %collective-permute-start = (f32[288,128]{1,0:T(8,128)S(1)}, f32[288,128]{1,0:T(8,128)S(1)}, u32[]{:S(2)}, u32[]{:S(2)}) collective-permute-start(f32[288,128]{1,0:T(8,128)S(1)} %get-tuple-element.31), channel_id=1, source_target_pairs={{0,1},{1,2},{2,3},{3,4},{4,5},{5,6},{6,7},{7,8},{8,9},{9,10},{10,1... | collective-permute-start | bytes 442376 | tf_op jit(solution)/shard_map/ppermute | solution.py:460
  3.8 10.6 %collective-permute-start.1 = (f32[288,128]{1,0:T(8,128)S(1)}, f32[288,128]{1,0:T(8,128)S(1)}, u32[]{:S(2)}, u32[]{:S(2)}) collective-permute-start(f32[288,128]{1,0:T(8,128)S(1)} %get-tuple-element.32), channel_id=1, source_target_pairs={{0,31},{1,0},{2,1},{3,2},{4,3},{5,4},{6,5},{7,6},{8,7},{9,8},{10,9... | collective-permute-start | bytes 442376 | tf_op jit(solution)/shard_map/ppermute | solution.py:460
  15.8 20.6 %all-to-all-start = ((f32[32,16,128]{2,1,0:T(8,128)}), f32[32,16,128]{2,1,0:T(8,128)S(1)}, u32[]{:S(2)}, u32[]{:S(2)}) async-start(f32[32,16,128]{2,1,0:T(8,128)} %get-tuple-element.33), calls=%async_computation | async-start | bytes 524288 | tf_op jit(solution)/shard_map/all_to_all | solution.py:464
  23.8 15.4 %copy-start = (f32[1,2,4,64,128]{4,3,2,1,0:T(8,128)S(1)}, f32[1,2,4,64,128]{4,3,2,1,0:T(8,128)}, u32[]{:S(2)}) copy-start(f32[1,2,4,64,128]{4,3,2,1,0:T(8,128)} %src.3) | copy-start | bytes 786436
  23.8 15.3 %collective-permute-start.3 = (f32[128,128]{1,0:T(8,128)S(1)}, f32[128,128]{1,0:T(8,128)S(1)}, u32[]{:S(2)}, u32[]{:S(2)}) collective-permute-start(f32[128,128]{1,0:T(8,128)S(1)} %get-tuple-element.35.pair.old), channel_id=1, source_target_pairs={{0,30},{1,31},{2,0},{3,1},{4,2},{5,3},{6,4},{7,5},{8,6},{9,7},{10,... | collective-permute-start | bytes 196616 | tf_op jit(solution)/shard_map/ppermute | solution.py:460
  29.3 9.8 %collective-permute-start.2 = (f32[128,128]{1,0:T(8,128)S(1)}, f32[128,128]{1,0:T(8,128)S(1)}, u32[]{:S(2)}, u32[]{:S(2)}) collective-permute-start(f32[128,128]{1,0:T(8,128)S(1)} %get-tuple-element.35.pair.old), channel_id=1, source_target_pairs={{0,2},{1,3},{2,4},{3,5},{4,6},{5,7},{6,8},{7,9},{8,10},{9,11},{10,... | collective-permute-start | bytes 196616 | tf_op jit(solution)/shard_map/ppermute | solution.py:460
  40.9 9.1 %collective-permute-start.4 = (f32[4,64,128]{2,1,0:T(8,128)S(1)}, f32[4,64,128]{2,1,0:T(8,128)S(1)}, u32[]{:S(2)}, u32[]{:S(2)}) collective-permute-start(f32[4,64,128]{2,1,0:T(8,128)S(1)} %get-tuple-element.41), channel_id=1, source_target_pairs={{0,32},{1,33},{2,34},{3,35},{4,36},{5,37},{6,38},{7,39},{8,40},{9,... | collective-permute-start | bytes 393224 | tf_op jit(solution)/shard_map/ppermute | solution.py:460
  40.9 9.1 %collective-permute-start.5 = (f32[224,128]{1,0:T(8,128)S(1)}, f32[224,128]{1,0:T(8,128)S(1)}, u32[]{:S(2)}, u32[]{:S(2)}) collective-permute-start(f32[224,128]{1,0:T(8,128)S(1)} %get-tuple-element.42), channel_id=1, source_target_pairs={{0,33},{1,34},{2,35},{3,36},{4,37},{5,38},{6,39},{7,40},{8,41},{9,... | collective-permute-start | bytes 344072 | tf_op jit(solution)/shard_map/ppermute | solution.py:460
  41.4 8.6 %collective-permute-start.6 = (f32[224,128]{1,0:T(8,128)S(1)}, f32[224,128]{1,0:T(8,128)S(1)}, u32[]{:S(2)}, u32[]{:S(2)}) collective-permute-start(f32[224,128]{1,0:T(8,128)S(1)} %get-tuple-element.43), channel_id=1, source_target_pairs={{0,63},{1,32},{2,33},{3,34},{4,35},{5,36},{6,37},{7,38},{8,39},{9,... | collective-permute-start | bytes 344072 | tf_op jit(solution)/shard_map/ppermute | solution.py:460
  51.6 21.4 %all-to-all-start.1 = ((f32[32,16,128]{2,1,0:T(8,128)}), f32[32,16,128]{2,1,0:T(8,128)S(1)}, u32[]{:S(2)}, u32[]{:S(2)}) async-start(f32[32,16,128]{2,1,0:T(8,128)} %get-tuple-element.44), calls=%async_computation.1 | async-start | bytes 524288 | tf_op jit(solution)/shard_map/all_to_all | solution.py:464
  59.6 16.0 %collective-permute-start.8 = (f32[64,128]{1,0:T(8,128)S(1)}, f32[64,128]{1,0:T(8,128)S(1)}, u32[]{:S(2)}, u32[]{:S(2)}) collective-permute-start(f32[64,128]{1,0:T(8,128)S(1)} %get-tuple-element.48.pair), channel_id=1, source_target_pairs={{0,30},{1,31},{2,0},{3,1},{4,2},{5,3},{6,4},{7,5},{8,6},{9,7},{10,... | collective-permute-start | bytes 98312 | tf_op jit(solution)/shard_map/ppermute | solution.py:460
  65.2 10.4 %collective-permute-start.7 = (f32[64,128]{1,0:T(8,128)S(1)}, f32[64,128]{1,0:T(8,128)S(1)}, u32[]{:S(2)}, u32[]{:S(2)}) collective-permute-start(f32[64,128]{1,0:T(8,128)S(1)} %get-tuple-element.48.pair), channel_id=1, source_target_pairs={{0,2},{1,3},{2,4},{3,5},{4,6},{5,7},{6,8},{7,9},{8,10},{9,11},{10,... | collective-permute-start | bytes 98312 | tf_op jit(solution)/shard_map/ppermute | solution.py:460
  73.0 2.6 %copy-start.1 = (f32[1,4,64,128]{3,2,1,0:T(8,128)S(1)}, f32[1,4,64,128]{3,2,1,0:T(8,128)}, u32[]{:S(2)}) copy-start(f32[1,4,64,128]{3,2,1,0:T(8,128)} %start.1) | copy-start | bytes 393220

commit v7 on v6

--- a/solution.py
+++ b/solution.py
@@ -194,7 +194,8 @@
     dn[pl.ds(224, 64), :] = w[0]
 
 
-def finish_down(first, w, y, x, b1, c1, lo, hi, wx, yx, xs, pair, send, rs, lo_pick, hi_pick):
+def finish_down(first, w, y, x, b1, c1, lo, hi, wx, yx, xs, pair, rs):
+    lo_pick, hi_pick = plane_picks()
     s = lax.axis_index("space")
     lane = iota((32, 128), 1)
 
@@ -273,17 +274,44 @@
 
 def first_down_body(w, y, x, block, lo, hi, wx, yx, xs, pair, send, rs):
     b1, c1 = block[pl.ds(0, 32), :], block[pl.ds(32, 32), :]
-    own = finish_down(True, w, y, x, b1, c1, lo, hi, wx, yx, xs, pair, send, rs, *plane_picks())
+    own = finish_down(True, w, y, x, b1, c1, lo, hi, wx, yx, xs, pair, rs)
     share(own, c1, pair[pl.ds(96, 32), :], send, rs)
 
 
-def next_down_body(b, lo, hi, cap, w, wx, old, yx, xs, pair, send, y, x, rs):
+def next_down_body(y, x, block, lo, hi, w, wx, yx, xs, pair, rs):
+    finish_down(False, w, y, x, block[...], None, lo, hi, wx, yx, xs, pair, rs)
+
+
+def wide_share(block, y, x, wx, w1, c1, send, rs):
+    lane = iota((32, 128), 1)
+    zero = jnp.zeros((32, 128), F32)
+    for k, (i, p) in enumerate(((0, 0), (5, 3))):
+        far = wx[i] * y[p]
+        rs[pl.ds(64 * k, 64), :] = far
+        rs[pl.ds(128 + 64 * k, 64), :] = (far - OMEGA * y[p]) + inside_plane(far) + x[p]
     lo_pick, hi_pick = plane_picks()
-    b1 = local_down(lambda p: b[p], cap, w, y, x, rs, lo_pick, hi_pick, False)
-    own = finish_down(
-        False, w, y, x, b1, None, lo, hi, wx, yx, xs, pair, send, rs, lo_pick, hi_pick
-    )
-    share(own, old[pl.ds(64, 32), :], old[pl.ds(96, 32), :], send, rs)
+    low = jnp.concatenate([row_pairs(rs, 0, 32), row_pairs(rs, 192, 32)], 0)
+    high = jnp.concatenate([row_pairs(rs, 64, 32), row_pairs(rs, 128, 32)], 0)
+    terms = dot(low, lo_pick) + dot(high, hi_pick)
+    mix = terms[32:]
+    b = [jnp.where(lane >= 64, mix, 0.0), block + terms[:32], jnp.where(lane < 64, mix, 0.0)]
+    v = [zero] + [w1[j + 1] * b[j] for j in range(3)] + [zero]
+    v = [zero] + [block_sweep(v[j], w1[j], v[j - 1], v[j + 1]) for j in (1, 2, 3)] + [zero]
+    r = [0.5 * around_block(zero, zero, v[1])]
+    for j in (1, 2, 3):
+        r.append(b[j - 1] - (c1[j] + 3.0) * v[j] + 0.5 * around_block(v[j], v[j - 1], v[j + 1]))
+    r.append(0.5 * around_block(zero, v[3], zero))
+    for k in range(5):
+        rs[pl.ds(32 * k, 32), :] = r[k]
+    low = dot(row_pairs(rs, 0, 80), picks(lambda i, j: ((i & 63) >> 1) == (j & 31), 0.125))
+    group = iota((16, 128), 1) >> 5
+    message = low[:16]
+    for k in (1, 2, 3):
+        message = jnp.where(group == k, low[16 * k : 16 * k + 16], message)
+    last = jnp.where(group[:8] == 0, low[64:72], low[72:80])
+    for peer in range(SLABS):
+        send[peer, pl.ds(0, 16), :] = message
+        send[peer, pl.ds(16, 8), :] = last
 
 
 def spread(v):
@@ -312,16 +340,21 @@
 
 def low_levels(first, got, w2, d2, w3, x2, t3):
     group = iota((16, 128), 1) >> 5
+    narrow = iota((8, 128), 1) >> 5
+    reach = 1 if first else 2
     parts, caps = [], []
     for zl in range(8):
         total, cap = None, None
         for zh in range(4):
             z = 8 * zh + zl
-            v = jnp.where(group == 1, got[z], 0.0)
-            if z + 1 < SLABS:
-                v = jnp.where(group == 0, got[z + 1], v)
-            if z > 0:
-                v = jnp.where(group == 2, got[z - 1], v)
+            v = jnp.zeros((16, 128), F32)
+            for k in range(3 if first else 4):
+                if 0 <= z + reach - k < SLABS:
+                    v = jnp.where(group == k, got[z + reach - k, pl.ds(0, 16), :], v)
+            if not first and z >= 2:
+                last = got[z - 2, pl.ds(16, 8), :]
+                halves = [jnp.where(narrow == k, last, 0.0) for k in range(2)]
+                v = v + jnp.concatenate(halves, 0)
             v = spread(v)
             total = v if total is None else jnp.where(group == zh, v, total)
             if first:
@@ -349,11 +382,11 @@
     low_levels(True, got, w2, d2, w3, x2, t3)
 
 
-def next_low_body(*refs):
-    low_levels(False, *refs)
-
-
-def fine_up(x2, lo2, pair, hi2, first, wx, yx, xs, w1, work, out):
+def next_low_body(got, w2, d2, w3, after, x2, t3):
+    low_levels(False, got, w2, d2, w3, x2, t3)
+
+
+def fine_up(x2, lo2, pair, hi2, c1, wx, yx, xs, w1, work, out):
     f1, y1, xa, xb, f0, x0, x9 = work
     s = lax.axis_index("space")
     lane = iota((32, 128), 1)
@@ -368,8 +401,9 @@
             hi2[pl.ds(start, 32), :],
         )
 
-    if first:
+    if c1 is not None:
         for j, c in enumerate(blocks(64)):
+            c1[j] = c
             z = s + (j - 2)
             w1[j] = jnp.where((z >= 0) & (z < SLABS), OMEGA / (c + 3.0), 0.0)
     for j, b in enumerate(blocks(0)):
@@ -413,26 +447,28 @@
 
 
 def first_up_body(
-    x2, lo2, pair, hi2, wx, yx, xs, w, cap, src, u_out, b_out, up, dn, w1, y, x, rs, *work
+    x2, lo2, pair, hi2, wx, yx, xs, w, cap, src, u_out, y, x, block, up, dn, w1, send, *work
 ):
+    b_out, c1, rs, *work = work
+
     def out(p, u):
         u_out[0, p] = u
         b_out[p] = cap[p] * u + src[0, 1, p]
 
-    fine_up(x2, lo2, pair, hi2, True, wx, yx, xs, w1, work, out)
-    block = local_down(lambda p: b_out[p], cap, w, y, x, rs, *plane_picks(), False)
+    fine_up(x2, lo2, pair, hi2, c1, wx, yx, xs, w1, work, out)
+    own = local_down(lambda p: b_out[p], cap, w, y, x, rs, *plane_picks(), False)
+    wide_share(own, y, x, wx, w1, c1, send, rs)
+    block[...] = own
     fill_edges(up, dn, y, x)
-    up[pl.ds(192, 32), :] = block
-    dn[pl.ds(192, 32), :] = block
-
-
-def next_up_body(x2, lo2, pair, hi2, wx, yx, xs, w1, start, u_out, *work):
-    keep = lax.axis_index("tm") == 0
-
+    up[pl.ds(192, 32), :] = own
+    dn[pl.ds(192, 32), :] = own
+
+
+def next_up_body(x2, lo2, pair, hi2, wx, yx, xs, w1, u_out, *work):
     def out(p, u):
-        u_out[0, p] = jnp.where(keep, start[0, p], u)
-
-    fine_up(x2, lo2, pair, hi2, False, wx, yx, xs, w1, work, out)
+        u_out[0, p] = u
+
+    fine_up(x2, lo2, pair, hi2, None, wx, yx, xs, w1, work, out)
 
 
 LOW_WORK = [(64, 128)]
@@ -450,6 +486,7 @@
 PLANE = (NY, NX)
 PLANE4 = (DEPTH, NY, NX)
 MESSAGE = f32(SLABS, 16, 128)
+WIDE_MESSAGE = f32(SLABS, 24, 128)
 
 
 def moved(x, spans, slabs):
@@ -460,9 +497,12 @@
     return lax.ppermute(x, ("tm", "space"), pairs)
 
 
-def exchanged(send, pair):
-    got = lax.all_to_all(send, "space", 0, 0, tiled=True)
-    return got, moved(pair, 0, 2), pair, moved(pair, 0, -2)
+def gathered(send):
+    return lax.all_to_all(send, "space", 0, 0, tiled=True)
+
+
+def near(pair):
+    return moved(pair, 0, 2), pair, moved(pair, 0, -2)
 
 
 def shards(u0, src, cap):
@@ -482,7 +522,7 @@
         [EDGE_SUMS],
         *(w, y, x, block, lo, hi),
     )
-    got, *near = exchanged(send, pair)
+    got = gathered(send)
     w2, d2, w3, x2 = call(
         first_low_body,
         (f32(128, 128), f32(128, 128), f32(32, 128), f32(128, 128)),
@@ -490,24 +530,34 @@
         got,
         flops=LOW_FLOPS,
     )
-    fpoint, b, up, dn, w1 = call(
+    fpoint, y, x, block, up, dn, w1, send = call(
         first_up_body,
-        (f32(1, *PLANE4), slab, f32(224, 128), f32(224, 128), f32(5, 32, 128)),
-        [PLANE4, PLANE4, EDGE_SUMS, *WORK],
-        *(x2, *near, wx, yx, xs, w, cap_in, src),
-    )
-    b, lo, hi = moved(b, 1, 0), moved(up, 1, 1), moved(dn, 1, -1)
-    yx, xs, pair, send = call(
+        (
+            f32(1, *PLANE4),
+            slab,
+            slab,
+            f32(32, 128),
+            f32(224, 128),
+            f32(224, 128),
+            f32(5, 32, 128),
+            WIDE_MESSAGE,
+        ),
+        [PLANE4, (5, 32, 128), EDGE_SUMS, *WORK],
+        *(x2, *near(pair), wx, yx, xs, w, cap_in, src),
+    )
+    got = gathered(send)
+    lo, hi = moved(up, 0, 1), moved(dn, 0, -1)
+    yx, xs, pair = call(
         next_down_body,
-        (f32(6, *PLANE), f32(8, *PLANE), f32(64, 128), MESSAGE),
-        [PLANE4, PLANE4, EDGE_SUMS],
-        *(b, lo, hi, cap_in, w, wx, pair),
-    )
-    got, *near = exchanged(send, pair)
-    (x2,) = call(next_low_body, (f32(128, 128),), LOW_WORK, *(got, w2, d2, w3), flops=LOW_FLOPS)
-    (updated,) = call(
-        next_up_body, (f32(1, *PLANE4),), WORK, *(x2, *near, wx, yx, xs, w1, u0)
-    )
+        (f32(6, *PLANE), f32(8, *PLANE), f32(64, 128)),
+        [EDGE_SUMS],
+        *(y, x, block, lo, hi, w, wx),
+    )
+    (x2,) = call(
+        next_low_body, (f32(128, 128),), LOW_WORK, *(got, w2, d2, w3, pair), flops=LOW_FLOPS
+    )
+    (u,) = call(next_up_body, (f32(1, *PLANE4),), WORK, *(x2, *near(pair), wx, yx, xs, w1))
+    updated = jnp.where(lax.axis_index("tm") == 0, u0, moved(u, 1, 0))
     return fpoint, updated
 
 

time: 77.5 us -> 73.8 us (0.952)
  starting transfers between devices: 41.3 us -> 37.2 us
  Pallas kernels: 13.1 us -> 11.9 us
    ppermute x9, waiting for transfers between devices: 7.21 us -> 15.7 us  [moved(): return lax.ppermute(x, ('tm', 'space'), pairs)]
    all_to_all x2, waiting for transfers between devices: 14.8 us -> 7.05 us  [gathered(): return lax.all_to_all(send, 'space', 0, 0, tiled=True)]
    all_to_all x2, starting transfers between devices: 16 us -> 11.9 us  [gathered(): return lax.all_to_all(send, 'space', 0, 0, tiled=True)]
    pallas_call x7, Pallas kernels: 13.1 us -> 11.9 us  [call(): pl.pallas_call(body, out_shape=outs, in_specs=[space] * len(args), out_sp...]
  transfers between devices with their start and end apart: 11 -> 11, of which waited for: 4 -> 4; matrix products, arithmetic and copies ran while one was open for 0% -> 0% of each run, Pallas kernels for 7% -> 8%
where the time goes in v7:
time: 73.8 us; the launch traced here: 73.3 us
  starting transfers between devices  37.2 us (50%)
  waiting for transfers between devices  22.8 us (31%)
  Pallas kernels  11.9 us (16%)
  between operations  0.77 us (1%)
    ppermute x9, starting transfers between devices, moved(): return lax.ppermute(x, ('tm', 'space'), pairs)  25.3 us
    ppermute x9, waiting for transfers between devices, moved(): return lax.ppermute(x, ('tm', 'space'), pairs)  15.7 us
    pallas_call x7, Pallas kernels, call(): pl.pallas_call(body, out_shape=outs, in_specs=[space] * len(args), out_sp...  11.9 us
    all_to_all x2, starting transfers between devices, gathered(): return lax.all_to_all(send, 'space', 0, 0, tiled=True)  11.9 us
    all_to_all x2, waiting for transfers between devices, gathered(): return lax.all_to_all(send, 'space', 0, 0, tiled=True)  7.05 us
  transfers between devices with their start and end apart: 11, of which 4 were waited for; matrix products, arithmetic and copies ran while one was open for 0% of the time, Pallas kernels for 8%

profile of v7, /device:TPU:4, one launch (start us, length us, event | category | flops | bytes accessed | tf_op | source)
XLA Modules:
  0.0 73.3 jit_solution(5723277903730059992)
XLA Ops:
  0.6 1.5 %shard_map.50 = (f32[4,64,128]{2,1,0:T(8,128)S(1)}, f32[4,64,128]{2,1,0:T(8,128)S(1)}, f32[4,64,128]{2,1,0:T(8,128)S(1)}, f32[64,128]{1,0:T(8,128)S(1)}, f32[288...) custom-call(f32[1,4,64,128]{3,2,1,0:T(8,128)} %u.1, f32[1,2,4,64,128]{4,3,2,1,0:T(8,128)} %src.3, ...), custom_call_target="tpu_custom_call" | custom-call | tf_op jit(solution)/shard_map/pallas_call | solution.py:23
  2.2 1.7 %collective-permute-start = (f32[288,128]{1,0:T(8,128)S(1)}, f32[288,128]{1,0:T(8,128)S(1)}, u32[]{:S(2)}, u32[]{:S(2)}) collective-permute-start(f32[288,128]{1,0:T(8,128)S(1)} %get-tuple-element.33), channel_id=1, source_target_pairs={{0,1},{1,2},{2,3},{3,4},{4,5},{5,6},{6,7},{7,8},{8,9},{9,10},{10,1... | collective-permute-start | bytes 442376 | tf_op jit(solution)/shard_map/ppermute | solution.py:497
  3.8 6.8 %collective-permute-start.1 = (f32[288,128]{1,0:T(8,128)S(1)}, f32[288,128]{1,0:T(8,128)S(1)}, u32[]{:S(2)}, u32[]{:S(2)}) collective-permute-start(f32[288,128]{1,0:T(8,128)S(1)} %get-tuple-element.34), channel_id=1, source_target_pairs={{0,31},{1,0},{2,1},{3,2},{4,3},{5,4},{6,5},{7,6},{8,7},{9,8},{10,9... | collective-permute-start | bytes 442376 | tf_op jit(solution)/shard_map/ppermute | solution.py:497
  10.6 3.8 %collective-permute-done.lo = f32[288,128]{1,0:T(8,128)S(1)} collective-permute-done((f32[288,128]{1,0:T(8,128)S(1)}, f32[288,128]{1,0:T(8,128)S(1)}, u32[]{:S(2)}, u32[]{:S(2)}) %collective-permute-start) | collective-permute-done | bytes 147488 | tf_op jit(solution)/shard_map/ppermute | solution.py:497
  14.4 1.4 %shard_map.51 = (f32[6,64,128]{2,1,0:T(8,128)S(1)}, f32[6,64,128]{2,1,0:T(8,128)S(1)}, f32[8,64,128]{2,1,0:T(8,128)S(1)}, f32[128,128]{1,0:T(8,128)S(1)}, f32[32,16,128]{2,1,0:T(8,128)}) custom-call(f32[4,64,128]{2,1,0:T(8,128)S(1)} %get-tuple-element.29.w, f32[4,64,128]{2,1,0:T(8,128)S(1)} %get-tuple-element.30.y, f32[4,64,128]{2,1,0:T(8,128)S(1)} %get-tuple-element.31.x, ...), custom_call_target="tpu_custom_call" | custom-call | tf_op jit(solution)/shard_map/pallas_call | solution.py:23
  15.8 8.0 %all-to-all-start = ((f32[32,16,128]{2,1,0:T(8,128)}), f32[32,16,128]{2,1,0:T(8,128)S(1)}, u32[]{:S(2)}, u32[]{:S(2)}) async-start(f32[32,16,128]{2,1,0:T(8,128)} %get-tuple-element.35), calls=%async_computation | async-start | bytes 524288 | tf_op jit(solution)/shard_map/all_to_all | solution.py:501
  23.8 0.0 copy-start
  23.8 3.4 %collective-permute-start.2 = (f32[128,128]{1,0:T(8,128)S(1)}, f32[128,128]{1,0:T(8,128)S(1)}, u32[]{:S(2)}, u32[]{:S(2)}) collective-permute-start(f32[128,128]{1,0:T(8,128)S(1)} %get-tuple-element.37.pair), channel_id=1, source_target_pairs={{0,2},{1,3},{2,4},{3,5},{4,6},{5,7},{6,8},{7,9},{8,10},{9,11},{10,... | collective-permute-start | bytes 196616 | tf_op jit(solution)/shard_map/ppermute | solution.py:497
  27.1 2.3 %collective-permute-start.3 = (f32[128,128]{1,0:T(8,128)S(1)}, f32[128,128]{1,0:T(8,128)S(1)}, u32[]{:S(2)}, u32[]{:S(2)}) collective-permute-start(f32[128,128]{1,0:T(8,128)S(1)} %get-tuple-element.37.pair), channel_id=1, source_target_pairs={{0,30},{1,31},{2,0},{3,1},{4,2},{5,3},{6,4},{7,5},{8,6},{9,7},{10,... | collective-permute-start | bytes 196616 | tf_op jit(solution)/shard_map/ppermute | solution.py:497
  29.5 7.0 %all-to-all-done.got = f32[32,16,128]{2,1,0:T(8,128)S(1)} async-done(((f32[32,16,128]{2,1,0:T(8,128)}), f32[32,16,128]{2,1,0:T(8,128)S(1)}, u32[]{:S(2)}, u32[]{:S(2)}) %all-to-all-start) | async-done | bytes 262176 | tf_op jit(solution)/shard_map/all_to_all | solution.py:501
  36.5 2.7 %shard_map.52 = (f32[128,128]{1,0:T(8,128)S(1)}, f32[128,128]{1,0:T(8,128)S(1)}, f32[32,128]{1,0:T(8,128)S(1)}, f32[128,128]{1,0:T(8,128)S(1)}) custom-call(f32[32,16,128]{2,1,0:T(8,128)S(1)} %all-to-all-done.got), custom_call_target="tpu_custom_call" | custom-call | flops 2147483648 | tf_op jit(solution)/shard_map/pallas_call | solution.py:23
  39.3 2.5 %shard_map.53 = (f32[1,4,64,128]{3,2,1,0:T(8,128)}, f32[4,64,128]{2,1,0:T(8,128)S(1)}, f32[4,64,128]{2,1,0:T(8,128)S(1)}, f32[32,128]{1,0:T(8,128)S(1)}, f32[224...) custom-call(f32[128,128]{1,0:T(8,128)S(1)} %get-tuple-element.36.x2, ...), custom_call_target="tpu_custom_call" | custom-call | tf_op jit(solution)/shard_map/pallas_call | solution.py:23
  41.8 3.9 %all-to-all-start.1 = ((f32[32,24,128]{2,1,0:T(8,128)}), f32[32,24,128]{2,1,0:T(8,128)S(1)}, u32[]{:S(2)}, u32[]{:S(2)}) async-start(f32[32,24,128]{2,1,0:T(8,128)} %get-tuple-element.43), calls=%async_computation.1 | async-start | bytes 786432 | tf_op jit(solution)/shard_map/all_to_all | solution.py:501
  45.7 1.8 %collective-permute-start.4 = (f32[224,128]{1,0:T(8,128)S(1)}, f32[224,128]{1,0:T(8,128)S(1)}, u32[]{:S(2)}, u32[]{:S(2)}) collective-permute-start(f32[224,128]{1,0:T(8,128)S(1)} %get-tuple-element.50), channel_id=1, source_target_pairs={{0,1},{1,2},{2,3},{3,4},{4,5},{5,6},{6,7},{7,8},{8,9},{9,10},{10,1... | collective-permute-start | bytes 344072 | tf_op jit(solution)/shard_map/ppermute | solution.py:497
  47.4 3.7 %collective-permute-start.5 = (f32[224,128]{1,0:T(8,128)S(1)}, f32[224,128]{1,0:T(8,128)S(1)}, u32[]{:S(2)}, u32[]{:S(2)}) collective-permute-start(f32[224,128]{1,0:T(8,128)S(1)} %get-tuple-element.51), channel_id=1, source_target_pairs={{0,31},{1,0},{2,1},{3,2},{4,3},{5,4},{6,5},{7,6},{8,7},{9,8},{10,9... | collective-permute-start | bytes 344072 | tf_op jit(solution)/shard_map/ppermute | solution.py:497
  51.1 7.6 %collective-permute-done.4.lo = f32[224,128]{1,0:T(8,128)S(1)} collective-permute-done((f32[224,128]{1,0:T(8,128)S(1)}, f32[224,128]{1,0:T(8,128)S(1)}, u32[]{:S(2)}, u32[]{:S(2)}) %collective-permute-start.4) | collective-permute-done | bytes 114720 | tf_op jit(solution)/shard_map/ppermute | solution.py:497
  58.6 0.3 shard_map.54
  59.0 0.1 collective-permute-start.6
  59.0 5.6 %collective-permute-start.7 = (f32[64,128]{1,0:T(8,128)S(1)}, f32[64,128]{1,0:T(8,128)S(1)}, u32[]{:S(2)}, u32[]{:S(2)}) collective-permute-start(f32[64,128]{1,0:T(8,128)S(1)} %get-tuple-element.52.after.pair), channel_id=1, source_target_pairs={{0,30},{1,31},{2,0},{3,1},{4,2},{5,3},{6,4},{7,5},{8,6},{9,7},{10,... | collective-permute-start | bytes 98312 | tf_op jit(solution)/shard_map/ppermute | solution.py:497
  64.7 2.6 %shard_map.55.x2 = f32[128,128]{1,0:T(8,128)S(1)} custom-call(f32[32,24,128]{2,1,0:T(8,128)S(1)} %all-to-all-done.1.got, f32[128,128]{1,0:T(8,128)S(1)} %get-tuple-element.44.w2, f32[128,128]{1,0:T(8,128)S(1)} %get-tuple-element.45.d2, f32[32,128]{1,0:T(8,128)S(1)} %get-tuple-element.46.w3, f32[64,128]{1,0:T(8,128)S(1)} %get-tuple-element.52.after.pair), custom_call_target="tpu_custom_call" | custom-call | flops 2147483648 | tf_op jit(solution)/shard_map/pallas_call | solution.py:23
  67.3 0.9 %shard_map.56 = f32[1,4,64,128]{3,2,1,0:T(8,128)S(1)} custom-call(f32[128,128]{1,0:T(8,128)S(1)} %shard_map.55.x2, f32[64,128]{1,0:T(8,128)S(1)} %collective-permute-done.6.lo2, f32[64,128]{1,0:T(8,128)S(1)} %get-tuple-element.52.after.pair, f32[64,128]{1,0:T(8,128)S(1)} %collective-permute-done.7.hi2, f32[6,64,128]{2,1,0:T(8,128)S(1)} %get-tuple-element.38.wx, ...), custom_call_target="tpu_custom_call" | custom-call | tf_op jit(solution)/shard_map/pallas_call | solution.py:23
  68.3 0.0 collective-permute-start.8
  68.3 4.4 %collective-permute-done.8 = f32[1,4,64,128]{3,2,1,0:T(8,128)S(1)} collective-permute-done((f32[1,4,64,128]{3,2,1,0:T(8,128)S(1)}, f32[1,4,64,128]{3,2,1,0:T(8,128)S(1)}, u32[]{:S(2)}, u32[]{:S(2)}) %collective-permute-start.8) | collective-permute-done | bytes 131104 | tf_op jit(solution)/shard_map/ppermute | solution.py:497
  72.7 0.7 broadcast_select_fusion
  (10 shorter events, 0.0 us)
Async XLA Ops:
  2.2 12.2 %collective-permute-start = (f32[288,128]{1,0:T(8,128)S(1)}, f32[288,128]{1,0:T(8,128)S(1)}, u32[]{:S(2)}, u32[]{:S(2)}) collective-permute-start(f32[288,128]{1,0:T(8,128)S(1)} %get-tuple-element.33), channel_id=1, source_target_pairs={{0,1},{1,2},{2,3},{3,4},{4,5},{5,6},{6,7},{7,8},{8,9},{9,10},{10,1... | collective-permute-start | bytes 442376 | tf_op jit(solution)/shard_map/ppermute | solution.py:497
  3.8 10.6 %collective-permute-start.1 = (f32[288,128]{1,0:T(8,128)S(1)}, f32[288,128]{1,0:T(8,128)S(1)}, u32[]{:S(2)}, u32[]{:S(2)}) collective-permute-start(f32[288,128]{1,0:T(8,128)S(1)} %get-tuple-element.34), channel_id=1, source_target_pairs={{0,31},{1,0},{2,1},{3,2},{4,3},{5,4},{6,5},{7,6},{8,7},{9,8},{10,9... | collective-permute-start | bytes 442376 | tf_op jit(solution)/shard_map/ppermute | solution.py:497
  15.8 20.8 %all-to-all-start = ((f32[32,16,128]{2,1,0:T(8,128)}), f32[32,16,128]{2,1,0:T(8,128)S(1)}, u32[]{:S(2)}, u32[]{:S(2)}) async-start(f32[32,16,128]{2,1,0:T(8,128)} %get-tuple-element.35), calls=%async_computation | async-start | bytes 524288 | tf_op jit(solution)/shard_map/all_to_all | solution.py:501
  23.8 15.5 %copy-start = (f32[1,2,4,64,128]{4,3,2,1,0:T(8,128)S(1)}, f32[1,2,4,64,128]{4,3,2,1,0:T(8,128)}, u32[]{:S(2)}) copy-start(f32[1,2,4,64,128]{4,3,2,1,0:T(8,128)} %src.3) | copy-start | bytes 786436
  23.8 15.5 %collective-permute-start.2 = (f32[128,128]{1,0:T(8,128)S(1)}, f32[128,128]{1,0:T(8,128)S(1)}, u32[]{:S(2)}, u32[]{:S(2)}) collective-permute-start(f32[128,128]{1,0:T(8,128)S(1)} %get-tuple-element.37.pair), channel_id=1, source_target_pairs={{0,2},{1,3},{2,4},{3,5},{4,6},{5,7},{6,8},{7,9},{8,10},{9,11},{10,... | collective-permute-start | bytes 196616 | tf_op jit(solution)/shard_map/ppermute | solution.py:497
  27.1 12.1 %collective-permute-start.3 = (f32[128,128]{1,0:T(8,128)S(1)}, f32[128,128]{1,0:T(8,128)S(1)}, u32[]{:S(2)}, u32[]{:S(2)}) collective-permute-start(f32[128,128]{1,0:T(8,128)S(1)} %get-tuple-element.37.pair), channel_id=1, source_target_pairs={{0,30},{1,31},{2,0},{3,1},{4,2},{5,3},{6,4},{7,5},{8,6},{9,7},{10,... | collective-permute-start | bytes 196616 | tf_op jit(solution)/shard_map/ppermute | solution.py:497
  41.8 22.9 %all-to-all-start.1 = ((f32[32,24,128]{2,1,0:T(8,128)}), f32[32,24,128]{2,1,0:T(8,128)S(1)}, u32[]{:S(2)}, u32[]{:S(2)}) async-start(f32[32,24,128]{2,1,0:T(8,128)} %get-tuple-element.43), calls=%async_computation.1 | async-start | bytes 786432 | tf_op jit(solution)/shard_map/all_to_all | solution.py:501
  45.7 13.0 %collective-permute-start.4 = (f32[224,128]{1,0:T(8,128)S(1)}, f32[224,128]{1,0:T(8,128)S(1)}, u32[]{:S(2)}, u32[]{:S(2)}) collective-permute-start(f32[224,128]{1,0:T(8,128)S(1)} %get-tuple-element.50), channel_id=1, source_target_pairs={{0,1},{1,2},{2,3},{3,4},{4,5},{5,6},{6,7},{7,8},{8,9},{9,10},{10,1... | collective-permute-start | bytes 344072 | tf_op jit(solution)/shard_map/ppermute | solution.py:497
  47.4 11.2 %collective-permute-start.5 = (f32[224,128]{1,0:T(8,128)S(1)}, f32[224,128]{1,0:T(8,128)S(1)}, u32[]{:S(2)}, u32[]{:S(2)}) collective-permute-start(f32[224,128]{1,0:T(8,128)S(1)} %get-tuple-element.51), channel_id=1, source_target_pairs={{0,31},{1,0},{2,1},{3,2},{4,3},{5,4},{6,5},{7,6},{8,7},{9,8},{10,9... | collective-permute-start | bytes 344072 | tf_op jit(solution)/shard_map/ppermute | solution.py:497
  59.0 8.3 %collective-permute-start.6 = (f32[64,128]{1,0:T(8,128)S(1)}, f32[64,128]{1,0:T(8,128)S(1)}, u32[]{:S(2)}, u32[]{:S(2)}) collective-permute-start(f32[64,128]{1,0:T(8,128)S(1)} %get-tuple-element.52.after.pair), channel_id=1, source_target_pairs={{0,2},{1,3},{2,4},{3,5},{4,6},{5,7},{6,8},{7,9},{8,10},{9,11},{10,... | collective-permute-start | bytes 98312 | tf_op jit(solution)/shard_map/ppermute | solution.py:497
  59.0 8.3 %collective-permute-start.7 = (f32[64,128]{1,0:T(8,128)S(1)}, f32[64,128]{1,0:T(8,128)S(1)}, u32[]{:S(2)}, u32[]{:S(2)}) collective-permute-start(f32[64,128]{1,0:T(8,128)S(1)} %get-tuple-element.52.after.pair), channel_id=1, source_target_pairs={{0,30},{1,31},{2,0},{3,1},{4,2},{5,3},{6,4},{7,5},{8,6},{9,7},{10,... | collective-permute-start | bytes 98312 | tf_op jit(solution)/shard_map/ppermute | solution.py:497
  67.3 5.4 %copy-start.1 = (f32[1,4,64,128]{3,2,1,0:T(8,128)S(1)}, f32[1,4,64,128]{3,2,1,0:T(8,128)}, u32[]{:S(2)}) copy-start(f32[1,4,64,128]{3,2,1,0:T(8,128)} %u.1) | copy-start | bytes 393220
  68.3 4.4 %collective-permute-start.8 = (f32[1,4,64,128]{3,2,1,0:T(8,128)S(1)}, f32[1,4,64,128]{3,2,1,0:T(8,128)S(1)}, u32[]{:S(2)}, u32[]{:S(2)}) collective-permute-start(f32[1,4,64,128]{3,2,1,0:T(8,128)S(1)} %shard_map.56), channel_id=1, source_target_pairs={{0,32},{1,33},{2,34},{3,35},{4,36},{5,37},{6,38},{7,39},{8,40},{9,... | collective-permute-start | bytes 393224 | tf_op jit(solution)/shard_map/ppermute | solution.py:497

commit v8 on v7

--- a/solution.py
+++ b/solution.py
@@ -4,6 +4,7 @@
 from jax.experimental import pallas as pl
 from jax.experimental.pallas import tpu as pltpu
 from jax.sharding import PartitionSpec as P
+
 
 COARSE_SWEEPS = 24
 NY, NX = 64, 128
@@ -85,16 +86,25 @@
     return total + jnp.where(y < 15, pltpu.roll(v, 127, 0), 0.0)
 
 
+def rolled(v, k, j):
+    return pltpu.roll(v[k % 4], (j - 16 * (k // 4)) % 128, 1) if (k // 4 or j) else v[k]
+
+
+CENTRE = [(k, 0) for k in range(4)]
+FIRST = [(k, j) for k in range(4) for j in (-1, 0, 1)] + [(-1, 0), (4, 0)]
+
+
 def coarsest(b3, w3):
     lane, row = iota((8, 128), 1), iota((8, 128), 0)
     x = lane & 15
-    steps = []
+    used = lane < 64
+    base, own = [], []
     for k in range(4):
-        w = w3[8 * k : 8 * k + 8]
+        w = jnp.where(used, w3[8 * k : 8 * k + 8], 0.0)
         wh = 0.125 * w
-        steps.append(
+        own.append(w * b3[8 * k : 8 * k + 8])
+        base.append(
             (
-                w * b3[8 * k : 8 * k + 8],
                 wh,
                 jnp.where(x > 0, wh, 0.0),
                 jnp.where(x < 15, wh, 0.0),
@@ -102,23 +112,38 @@
                 jnp.where(row < 7, wh, 0.0),
             )
         )
-    inside = lane < 64
-
-    def sweep(_, v):
-        below = jnp.where(inside, pltpu.roll(v[3], 16, 1), 0.0)
-        above = jnp.where(inside, pltpu.roll(v[0], 112, 1), 0.0)
-        line = (below, *v, above)
-        new = []
-        for k in range(4):
-            wb, wh, left, right, up, down = steps[k]
-            c = v[k]
-            t = (0.2 * c + wb) + wh * (line[k] + line[k + 2])
-            s = up * pltpu.roll(c, 1, 0) + down * pltpu.roll(c, 7, 0)
-            e = left * pltpu.roll(c, 1, 1) + right * pltpu.roll(c, 127, 1)
-            new.append((t + s) + e)
-        return tuple(new)
-
-    v = lax.fori_loop(0, COARSE_SWEEPS - 1, sweep, tuple(s[0] for s in steps), unroll=True)
+    terms = list(zip(*base))
+    steps = {
+        (k, j): (rolled(own, k, j), *(rolled(t, k, j) for t in terms)) for k, j in FIRST
+    }
+
+    def sweep(v, k, j):
+        wb, wh, left, right, up, down = steps[k, j]
+        c = v[k, j]
+        t = (0.2 * c + wb) + wh * (v[k - 1, j] + v[k + 1, j])
+        s = up * pltpu.roll(c, 1, 0) + down * pltpu.roll(c, 7, 0)
+        return (t + s) + (left * v[k, j + 1] + right * v[k, j - 1])
+
+    def copies(v, reach):
+        return {
+            (k, j): rolled(v, k, j)
+            for k in range(-reach, 4 + reach)
+            for j in range(-reach, reach + 1)
+            if max(0, -k, k - 3) + abs(j) <= reach
+        }
+
+    def one(v):
+        v = copies(v, 1)
+        return [sweep(v, k, j) for k, j in CENTRE]
+
+    def two(_, v):
+        v = copies(v, 2)
+        v = {(k, j): sweep(v, k, j) for k, j in FIRST}
+        return tuple(sweep(v, k, j) for k, j in CENTRE)
+
+    pairs, rest = divmod(COARSE_SWEEPS - 1, 2)
+    v = one(own) if rest else own
+    v = lax.fori_loop(0, pairs, two, tuple(v), unroll=True)
     return jnp.concatenate(v, 0)
 
 
@@ -546,7 +571,8 @@
         *(x2, *near(pair), wx, yx, xs, w, cap_in, src),
     )
     got = gathered(send)
-    lo, hi = moved(up, 0, 1), moved(dn, 0, -1)
+    lo = moved(up, 0, 1)
+    hi = moved(dn, 0, -1)
     yx, xs, pair = call(
         next_down_body,
         (f32(6, *PLANE), f32(8, *PLANE), f32(64, 128)),

time: 73.8 us -> 73.4 us (level)
  Pallas kernels: 11.9 us -> 10.8 us
    pallas_call x7, Pallas kernels: 11.9 us -> 10.8 us  [call(): pl.pallas_call(body, out_shape=outs, in_specs=[space] * len(args), out_sp...]
  transfers between devices with their start and end apart: 11 -> 11, of which waited for: 4 -> 4; matrix products, arithmetic and copies ran while one was open for 0% -> 0% of each run, Pallas kernels for 8% -> 6%
where the time goes in v8:
time: 73.4 us; the launch traced here: 72.9 us
  starting transfers between devices  37.3 us (51%)
  waiting for transfers between devices  23.4 us (32%)
  Pallas kernels  10.8 us (15%)
  between operations  0.77 us (1%)
    ppermute x9, starting transfers between devices, moved(): return lax.ppermute(x, ('tm', 'space'), pairs)  25.3 us
    ppermute x9, waiting for transfers between devices, moved(): return lax.ppermute(x, ('tm', 'space'), pairs)  16.4 us
    all_to_all x2, starting transfers between devices, gathered(): return lax.all_to_all(send, 'space', 0, 0, tiled=True)  11.9 us
    pallas_call x7, Pallas kernels, call(): pl.pallas_call(body, out_shape=outs, in_specs=[space] * len(args), out_sp...  10.8 us
    all_to_all x2, waiting for transfers between devices, gathered(): return lax.all_to_all(send, 'space', 0, 0, tiled=True)  7.05 us
  transfers between devices with their start and end apart: 11, of which 4 were waited for; matrix products, arithmetic and copies ran while one was open for 0% of the time, Pallas kernels for 6%

profile of v8, /device:TPU:4, one launch (start us, length us, event | category | flops | bytes accessed | tf_op | source)
XLA Modules:
  0.0 72.9 jit_solution(15508859126262929032)
XLA Ops:
  0.6 1.5 %shard_map.50 = (f32[4,64,128]{2,1,0:T(8,128)S(1)}, f32[4,64,128]{2,1,0:T(8,128)S(1)}, f32[4,64,128]{2,1,0:T(8,128)S(1)}, f32[64,128]{1,0:T(8,128)S(1)}, f32[288...) custom-call(f32[1,4,64,128]{3,2,1,0:T(8,128)} %u.1, f32[1,2,4,64,128]{4,3,2,1,0:T(8,128)} %src.3, ...), custom_call_target="tpu_custom_call" | custom-call | tf_op jit(solution)/shard_map/pallas_call | solution.py:24
  2.2 1.7 %collective-permute-start = (f32[288,128]{1,0:T(8,128)S(1)}, f32[288,128]{1,0:T(8,128)S(1)}, u32[]{:S(2)}, u32[]{:S(2)}) collective-permute-start(f32[288,128]{1,0:T(8,128)S(1)} %get-tuple-element.33), channel_id=1, source_target_pairs={{0,1},{1,2},{2,3},{3,4},{4,5},{5,6},{6,7},{7,8},{8,9},{9,10},{10,1... | collective-permute-start | bytes 442376 | tf_op jit(solution)/shard_map/ppermute | solution.py:522
  3.8 6.8 %collective-permute-start.1 = (f32[288,128]{1,0:T(8,128)S(1)}, f32[288,128]{1,0:T(8,128)S(1)}, u32[]{:S(2)}, u32[]{:S(2)}) collective-permute-start(f32[288,128]{1,0:T(8,128)S(1)} %get-tuple-element.34), channel_id=1, source_target_pairs={{0,31},{1,0},{2,1},{3,2},{4,3},{5,4},{6,5},{7,6},{8,7},{9,8},{10,9... | collective-permute-start | bytes 442376 | tf_op jit(solution)/shard_map/ppermute | solution.py:522
  10.6 3.8 %collective-permute-done.lo = f32[288,128]{1,0:T(8,128)S(1)} collective-permute-done((f32[288,128]{1,0:T(8,128)S(1)}, f32[288,128]{1,0:T(8,128)S(1)}, u32[]{:S(2)}, u32[]{:S(2)}) %collective-permute-start) | collective-permute-done | bytes 147488 | tf_op jit(solution)/shard_map/ppermute | solution.py:522
  14.4 1.4 %shard_map.51 = (f32[6,64,128]{2,1,0:T(8,128)S(1)}, f32[6,64,128]{2,1,0:T(8,128)S(1)}, f32[8,64,128]{2,1,0:T(8,128)S(1)}, f32[128,128]{1,0:T(8,128)S(1)}, f32[32,16,128]{2,1,0:T(8,128)}) custom-call(f32[4,64,128]{2,1,0:T(8,128)S(1)} %get-tuple-element.29.w, f32[4,64,128]{2,1,0:T(8,128)S(1)} %get-tuple-element.30.y, f32[4,64,128]{2,1,0:T(8,128)S(1)} %get-tuple-element.31.x, ...), custom_call_target="tpu_custom_call" | custom-call | tf_op jit(solution)/shard_map/pallas_call | solution.py:24
  15.8 8.0 %all-to-all-start = ((f32[32,16,128]{2,1,0:T(8,128)}), f32[32,16,128]{2,1,0:T(8,128)S(1)}, u32[]{:S(2)}, u32[]{:S(2)}) async-start(f32[32,16,128]{2,1,0:T(8,128)} %get-tuple-element.35), calls=%async_computation | async-start | bytes 524288 | tf_op jit(solution)/shard_map/all_to_all | solution.py:526
  23.8 0.0 copy-start
  23.8 3.4 %collective-permute-start.2 = (f32[128,128]{1,0:T(8,128)S(1)}, f32[128,128]{1,0:T(8,128)S(1)}, u32[]{:S(2)}, u32[]{:S(2)}) collective-permute-start(f32[128,128]{1,0:T(8,128)S(1)} %get-tuple-element.37.pair), channel_id=1, source_target_pairs={{0,2},{1,3},{2,4},{3,5},{4,6},{5,7},{6,8},{7,9},{8,10},{9,11},{10,... | collective-permute-start | bytes 196616 | tf_op jit(solution)/shard_map/ppermute | solution.py:522
  27.1 2.3 %collective-permute-start.3 = (f32[128,128]{1,0:T(8,128)S(1)}, f32[128,128]{1,0:T(8,128)S(1)}, u32[]{:S(2)}, u32[]{:S(2)}) collective-permute-start(f32[128,128]{1,0:T(8,128)S(1)} %get-tuple-element.37.pair), channel_id=1, source_target_pairs={{0,30},{1,31},{2,0},{3,1},{4,2},{5,3},{6,4},{7,5},{8,6},{9,7},{10,... | collective-permute-start | bytes 196616 | tf_op jit(solution)/shard_map/ppermute | solution.py:522
  29.5 7.0 %all-to-all-done.got = f32[32,16,128]{2,1,0:T(8,128)S(1)} async-done(((f32[32,16,128]{2,1,0:T(8,128)}), f32[32,16,128]{2,1,0:T(8,128)S(1)}, u32[]{:S(2)}, u32[]{:S(2)}) %all-to-all-start) | async-done | bytes 262176 | tf_op jit(solution)/shard_map/all_to_all | solution.py:526
  36.5 2.2 %shard_map.52 = (f32[128,128]{1,0:T(8,128)S(1)}, f32[128,128]{1,0:T(8,128)S(1)}, f32[32,128]{1,0:T(8,128)S(1)}, f32[128,128]{1,0:T(8,128)S(1)}) custom-call(f32[32,16,128]{2,1,0:T(8,128)S(1)} %all-to-all-done.got), custom_call_target="tpu_custom_call" | custom-call | flops 2147483648 | tf_op jit(solution)/shard_map/pallas_call | solution.py:24
  38.8 2.5 %shard_map.53 = (f32[1,4,64,128]{3,2,1,0:T(8,128)}, f32[4,64,128]{2,1,0:T(8,128)S(1)}, f32[4,64,128]{2,1,0:T(8,128)S(1)}, f32[32,128]{1,0:T(8,128)S(1)}, f32[224...) custom-call(f32[128,128]{1,0:T(8,128)S(1)} %get-tuple-element.36.x2, ...), custom_call_target="tpu_custom_call" | custom-call | tf_op jit(solution)/shard_map/pallas_call | solution.py:24
  41.2 3.9 %all-to-all-start.1 = ((f32[32,24,128]{2,1,0:T(8,128)}), f32[32,24,128]{2,1,0:T(8,128)S(1)}, u32[]{:S(2)}, u32[]{:S(2)}) async-start(f32[32,24,128]{2,1,0:T(8,128)} %get-tuple-element.43), calls=%async_computation.1 | async-start | bytes 786432 | tf_op jit(solution)/shard_map/all_to_all | solution.py:526
  45.1 1.9 %collective-permute-start.4 = (f32[224,128]{1,0:T(8,128)S(1)}, f32[224,128]{1,0:T(8,128)S(1)}, u32[]{:S(2)}, u32[]{:S(2)}) collective-permute-start(f32[224,128]{1,0:T(8,128)S(1)} %get-tuple-element.50), channel_id=1, source_target_pairs={{0,1},{1,2},{2,3},{3,4},{4,5},{5,6},{6,7},{7,8},{8,9},{9,10},{10,1... | collective-permute-start | bytes 344072 | tf_op jit(solution)/shard_map/ppermute | solution.py:522
  47.0 3.6 %collective-permute-start.5 = (f32[224,128]{1,0:T(8,128)S(1)}, f32[224,128]{1,0:T(8,128)S(1)}, u32[]{:S(2)}, u32[]{:S(2)}) collective-permute-start(f32[224,128]{1,0:T(8,128)S(1)} %get-tuple-element.51), channel_id=1, source_target_pairs={{0,31},{1,0},{2,1},{3,2},{4,3},{5,4},{6,5},{7,6},{8,7},{9,8},{10,9... | collective-permute-start | bytes 344072 | tf_op jit(solution)/shard_map/ppermute | solution.py:522
  50.6 8.2 %collective-permute-done.4.lo = f32[224,128]{1,0:T(8,128)S(1)} collective-permute-done((f32[224,128]{1,0:T(8,128)S(1)}, f32[224,128]{1,0:T(8,128)S(1)}, u32[]{:S(2)}, u32[]{:S(2)}) %collective-permute-start.4) | collective-permute-done | bytes 114720 | tf_op jit(solution)/shard_map/ppermute | solution.py:522
  58.8 0.3 shard_map.54
  59.1 0.1 collective-permute-start.6
  59.2 5.6 %collective-permute-start.7 = (f32[64,128]{1,0:T(8,128)S(1)}, f32[64,128]{1,0:T(8,128)S(1)}, u32[]{:S(2)}, u32[]{:S(2)}) collective-permute-start(f32[64,128]{1,0:T(8,128)S(1)} %get-tuple-element.52.after.pair), channel_id=1, source_target_pairs={{0,30},{1,31},{2,0},{3,1},{4,2},{5,3},{6,4},{7,5},{8,6},{9,7},{10,... | collective-permute-start | bytes 98312 | tf_op jit(solution)/shard_map/ppermute | solution.py:522
  64.8 2.0 %shard_map.55.x2 = f32[128,128]{1,0:T(8,128)S(1)} custom-call(f32[32,24,128]{2,1,0:T(8,128)S(1)} %all-to-all-done.1.got, f32[128,128]{1,0:T(8,128)S(1)} %get-tuple-element.44.w2, f32[128,128]{1,0:T(8,128)S(1)} %get-tuple-element.45.d2, f32[32,128]{1,0:T(8,128)S(1)} %get-tuple-element.46.w3, f32[64,128]{1,0:T(8,128)S(1)} %get-tuple-element.52.after.pair), custom_call_target="tpu_custom_call" | custom-call | flops 2147483648 | tf_op jit(solution)/shard_map/pallas_call | solution.py:24
  66.9 0.9 %shard_map.56 = f32[1,4,64,128]{3,2,1,0:T(8,128)S(1)} custom-call(f32[128,128]{1,0:T(8,128)S(1)} %shard_map.55.x2, f32[64,128]{1,0:T(8,128)S(1)} %collective-permute-done.6.lo2, f32[64,128]{1,0:T(8,128)S(1)} %get-tuple-element.52.after.pair, f32[64,128]{1,0:T(8,128)S(1)} %collective-permute-done.7.hi2, f32[6,64,128]{2,1,0:T(8,128)S(1)} %get-tuple-element.38.wx, ...), custom_call_target="tpu_custom_call" | custom-call | tf_op jit(solution)/shard_map/pallas_call | solution.py:24
  67.9 0.0 collective-permute-start.8
  67.9 4.4 %collective-permute-done.8 = f32[1,4,64,128]{3,2,1,0:T(8,128)S(1)} collective-permute-done((f32[1,4,64,128]{3,2,1,0:T(8,128)S(1)}, f32[1,4,64,128]{3,2,1,0:T(8,128)S(1)}, u32[]{:S(2)}, u32[]{:S(2)}) %collective-permute-start.8) | collective-permute-done | bytes 131104 | tf_op jit(solution)/shard_map/ppermute | solution.py:522
  72.3 0.7 broadcast_select_fusion
  (10 shorter events, 0.0 us)
Async XLA Ops:
  2.2 12.2 %collective-permute-start = (f32[288,128]{1,0:T(8,128)S(1)}, f32[288,128]{1,0:T(8,128)S(1)}, u32[]{:S(2)}, u32[]{:S(2)}) collective-permute-start(f32[288,128]{1,0:T(8,128)S(1)} %get-tuple-element.33), channel_id=1, source_target_pairs={{0,1},{1,2},{2,3},{3,4},{4,5},{5,6},{6,7},{7,8},{8,9},{9,10},{10,1... | collective-permute-start | bytes 442376 | tf_op jit(solution)/shard_map/ppermute | solution.py:522
  3.8 10.6 %collective-permute-start.1 = (f32[288,128]{1,0:T(8,128)S(1)}, f32[288,128]{1,0:T(8,128)S(1)}, u32[]{:S(2)}, u32[]{:S(2)}) collective-permute-start(f32[288,128]{1,0:T(8,128)S(1)} %get-tuple-element.34), channel_id=1, source_target_pairs={{0,31},{1,0},{2,1},{3,2},{4,3},{5,4},{6,5},{7,6},{8,7},{9,8},{10,9... | collective-permute-start | bytes 442376 | tf_op jit(solution)/shard_map/ppermute | solution.py:522
  15.8 20.8 %all-to-all-start = ((f32[32,16,128]{2,1,0:T(8,128)}), f32[32,16,128]{2,1,0:T(8,128)S(1)}, u32[]{:S(2)}, u32[]{:S(2)}) async-start(f32[32,16,128]{2,1,0:T(8,128)} %get-tuple-element.35), calls=%async_computation | async-start | bytes 524288 | tf_op jit(solution)/shard_map/all_to_all | solution.py:526
  23.8 15.0 %copy-start = (f32[1,2,4,64,128]{4,3,2,1,0:T(8,128)S(1)}, f32[1,2,4,64,128]{4,3,2,1,0:T(8,128)}, u32[]{:S(2)}) copy-start(f32[1,2,4,64,128]{4,3,2,1,0:T(8,128)} %src.3) | copy-start | bytes 786436
  23.8 15.0 %collective-permute-start.2 = (f32[128,128]{1,0:T(8,128)S(1)}, f32[128,128]{1,0:T(8,128)S(1)}, u32[]{:S(2)}, u32[]{:S(2)}) collective-permute-start(f32[128,128]{1,0:T(8,128)S(1)} %get-tuple-element.37.pair), channel_id=1, source_target_pairs={{0,2},{1,3},{2,4},{3,5},{4,6},{5,7},{6,8},{7,9},{8,10},{9,11},{10,... | collective-permute-start | bytes 196616 | tf_op jit(solution)/shard_map/ppermute | solution.py:522
  27.1 11.6 %collective-permute-start.3 = (f32[128,128]{1,0:T(8,128)S(1)}, f32[128,128]{1,0:T(8,128)S(1)}, u32[]{:S(2)}, u32[]{:S(2)}) collective-permute-start(f32[128,128]{1,0:T(8,128)S(1)} %get-tuple-element.37.pair), channel_id=1, source_target_pairs={{0,30},{1,31},{2,0},{3,1},{4,2},{5,3},{6,4},{7,5},{8,6},{9,7},{10,... | collective-permute-start | bytes 196616 | tf_op jit(solution)/shard_map/ppermute | solution.py:522
  41.2 23.6 %all-to-all-start.1 = ((f32[32,24,128]{2,1,0:T(8,128)}), f32[32,24,128]{2,1,0:T(8,128)S(1)}, u32[]{:S(2)}, u32[]{:S(2)}) async-start(f32[32,24,128]{2,1,0:T(8,128)} %get-tuple-element.43), calls=%async_computation.1 | async-start | bytes 786432 | tf_op jit(solution)/shard_map/all_to_all | solution.py:526
  45.1 13.7 %collective-permute-start.4 = (f32[224,128]{1,0:T(8,128)S(1)}, f32[224,128]{1,0:T(8,128)S(1)}, u32[]{:S(2)}, u32[]{:S(2)}) collective-permute-start(f32[224,128]{1,0:T(8,128)S(1)} %get-tuple-element.50), channel_id=1, source_target_pairs={{0,1},{1,2},{2,3},{3,4},{4,5},{5,6},{6,7},{7,8},{8,9},{9,10},{10,1... | collective-permute-start | bytes 344072 | tf_op jit(solution)/shard_map/ppermute | solution.py:522
  47.0 11.8 %collective-permute-start.5 = (f32[224,128]{1,0:T(8,128)S(1)}, f32[224,128]{1,0:T(8,128)S(1)}, u32[]{:S(2)}, u32[]{:S(2)}) collective-permute-start(f32[224,128]{1,0:T(8,128)S(1)} %get-tuple-element.51), channel_id=1, source_target_pairs={{0,31},{1,0},{2,1},{3,2},{4,3},{5,4},{6,5},{7,6},{8,7},{9,8},{10,9... | collective-permute-start | bytes 344072 | tf_op jit(solution)/shard_map/ppermute | solution.py:522
  59.1 7.8 %collective-permute-start.6 = (f32[64,128]{1,0:T(8,128)S(1)}, f32[64,128]{1,0:T(8,128)S(1)}, u32[]{:S(2)}, u32[]{:S(2)}) collective-permute-start(f32[64,128]{1,0:T(8,128)S(1)} %get-tuple-element.52.after.pair), channel_id=1, source_target_pairs={{0,2},{1,3},{2,4},{3,5},{4,6},{5,7},{6,8},{7,9},{8,10},{9,11},{10,... | collective-permute-start | bytes 98312 | tf_op jit(solution)/shard_map/ppermute | solution.py:522
  59.2 7.7 %collective-permute-start.7 = (f32[64,128]{1,0:T(8,128)S(1)}, f32[64,128]{1,0:T(8,128)S(1)}, u32[]{:S(2)}, u32[]{:S(2)}) collective-permute-start(f32[64,128]{1,0:T(8,128)S(1)} %get-tuple-element.52.after.pair), channel_id=1, source_target_pairs={{0,30},{1,31},{2,0},{3,1},{4,2},{5,3},{6,4},{7,5},{8,6},{9,7},{10,... | collective-permute-start | bytes 98312 | tf_op jit(solution)/shard_map/ppermute | solution.py:522
  66.9 5.4 %copy-start.1 = (f32[1,4,64,128]{3,2,1,0:T(8,128)S(1)}, f32[1,4,64,128]{3,2,1,0:T(8,128)}, u32[]{:S(2)}) copy-start(f32[1,4,64,128]{3,2,1,0:T(8,128)} %u.1) | copy-start | bytes 393220
  67.9 4.4 %collective-permute-start.8 = (f32[1,4,64,128]{3,2,1,0:T(8,128)S(1)}, f32[1,4,64,128]{3,2,1,0:T(8,128)S(1)}, u32[]{:S(2)}, u32[]{:S(2)}) collective-permute-start(f32[1,4,64,128]{3,2,1,0:T(8,128)S(1)} %shard_map.56), channel_id=1, source_target_pairs={{0,32},{1,33},{2,34},{3,35},{4,36},{5,37},{6,38},{7,39},{8,40},{9,... | collective-permute-start | bytes 393224 | tf_op jit(solution)/shard_map/ppermute | solution.py:522

commit v9 on v8

--- a/solution.py
+++ b/solution.py
@@ -32,23 +32,26 @@
     )(*args)
 
 
-def dot(a, pick):
-    high = a.astype(jnp.bfloat16)
-    rest = a - high.astype(F32)
-    middle = rest.astype(jnp.bfloat16)
-    low = (rest - middle.astype(F32)).astype(jnp.bfloat16)
-    rows = a.shape[0]
-    out = jnp.dot(jnp.concatenate([high, middle, low], 0), pick, preferred_element_type=F32)
-    return (out[2 * rows :] + out[rows : 2 * rows]) + out[:rows]
+def lanes_of(v, lane):
+    return jnp.take_along_axis(v, lane, axis=1, mode="promise_in_bounds")
 
 
 def iota(shape, axis):
     return lax.broadcasted_iota(jnp.int32, shape, axis)
 
 
-def picks(test, scale):
-    i, j = iota((128, 128), 0), iota((128, 128), 1)
-    return jnp.where(test(i, j), jnp.float32(scale), jnp.float32(0.0)).astype(jnp.bfloat16)
+def halves(low, high):
+    lane = iota(low.shape, 1)
+    at = (lane & 63) * 2
+    low = lanes_of(low, at) + lanes_of(low, at + 1)
+    high = lanes_of(high, at) + lanes_of(high, at + 1)
+    return 0.125 * jnp.where(lane < 64, low, high)
+
+
+def quarters(v):
+    at = (iota(v.shape, 1) & 31) * 2
+    low = lanes_of(v, at) + lanes_of(v, at + 1)
+    return 0.125 * (low + (lanes_of(v, at + 64) + lanes_of(v, at + 65)))
 
 
 def inside_plane(c):
@@ -87,7 +90,7 @@
 
 
 def rolled(v, k, j):
-    return pltpu.roll(v[k % 4], (j - 16 * (k // 4)) % 128, 1) if (k // 4 or j) else v[k]
+    return pltpu.roll(v[k % 4], (2 * j - 32 * (k // 4)) % 128, 1) if (k // 4 or j) else v[k]
 
 
 CENTRE = [(k, 0) for k in range(4)]
@@ -96,16 +99,16 @@
 
 def coarsest(b3, w3):
     lane, row = iota((8, 128), 1), iota((8, 128), 0)
-    x = lane & 15
-    used = lane < 64
+    x = (lane & 31) >> 1
     base, own = [], []
     for k in range(4):
-        w = jnp.where(used, w3[8 * k : 8 * k + 8], 0.0)
+        w = w3[8 * k : 8 * k + 8]
         wh = 0.125 * w
         own.append(w * b3[8 * k : 8 * k + 8])
         base.append(
             (
-                wh,
+                jnp.where(lane >= 32, wh, 0.0) if k == 0 else wh,
+                jnp.where(lane < 96, wh, 0.0) if k == 3 else wh,
                 jnp.where(x > 0, wh, 0.0),
                 jnp.where(x < 15, wh, 0.0),
                 jnp.where(row > 0, wh, 0.0),
@@ -118,9 +121,9 @@
     }
 
     def sweep(v, k, j):
-        wb, wh, left, right, up, down = steps[k, j]
+        wb, below, above, left, right, up, down = steps[k, j]
         c = v[k, j]
-        t = (0.2 * c + wb) + wh * (v[k - 1, j] + v[k + 1, j])
+        t = (0.2 * c + wb) + (below * v[k - 1, j] + above * v[k + 1, j])
         s = up * pltpu.roll(c, 1, 0) + down * pltpu.roll(c, 7, 0)
         return (t + s) + (left * v[k, j + 1] + right * v[k, j - 1])
 
@@ -155,14 +158,7 @@
     return 1.2 * y + 0.5 * w * around_block(y, below, above)
 
 
-def plane_picks():
-    return (
-        picks(lambda i, j: (i >> 1) == j, 0.125),
-        picks(lambda i, j: (i >> 1) + 64 == j, 0.125),
-    )
-
-
-def local_down(b, cap, w, y, x, rs, lo_pick, hi_pick, first):
+def local_down(b, cap, w, y, x, rs, first):
     for p in range(DEPTH):
         y[p] = w[p] * b(p)
     zero = jnp.zeros((NY, NX), F32)
@@ -184,7 +180,7 @@
     if first:
         low = jnp.concatenate([low, row_pairs(rs, 128, 32)], 0)
         high = jnp.concatenate([high, row_pairs(rs, 192, 32)], 0)
-    return dot(low, lo_pick) + dot(high, hi_pick)
+    return halves(low, high)
 
 
 def fill_edges(up, dn, y, x):
@@ -202,13 +198,12 @@
     ]
     for copy in copies:
         copy.start()
-    lo_pick, hi_pick = plane_picks()
     for copy in copies:
         copy.wait()
     for p in range(DEPTH):
         w[p] = OMEGA / (cap_out[p] + 6.0)
         u_in[p] = cap_out[p] * u_in[p] + src_in[p]
-    blocks = local_down(lambda p: u_in[p], cap_out, w, y, x, rs, lo_pick, hi_pick, True)
+    blocks = local_down(lambda p: u_in[p], cap_out, w, y, x, rs, True)
     block[...] = blocks
     fill_edges(up, dn, y, x)
     lane = iota((32, 128), 1)
@@ -220,7 +215,6 @@
 
 
 def finish_down(first, w, y, x, b1, c1, lo, hi, wx, yx, xs, pair, rs):
-    lo_pick, hi_pick = plane_picks()
     s = lax.axis_index("space")
     lane = iota((32, 128), 1)
 
@@ -256,7 +250,7 @@
         rs[pl.ds(64 * k, 64), :] = v
     low = jnp.concatenate([row_pairs(rs, 0, 32), row_pairs(rs, 64, 32)], 0)
     high = jnp.concatenate([row_pairs(rs, 128, 32), row_pairs(rs, 192, 32)], 0)
-    terms = dot(low, lo_pick) + dot(high, hi_pick)
+    terms = halves(low, high)
     lo_block, hi_block = lo[pl.ds(192, 32), :], hi[pl.ds(192, 32), :]
     if first:
         pair[pl.ds(64, 32), :] = c1
@@ -288,7 +282,7 @@
     ]
     for k in range(4):
         rs[pl.ds(32 * k, 32), :] = r[k]
-    low = dot(row_pairs(rs, 0, 64), picks(lambda i, j: ((i & 63) >> 1) == (j & 31), 0.125))
+    low = quarters(row_pairs(rs, 0, 64))
     group = iota((16, 128), 1) >> 5
     message = low[48:]
     for k in range(3):
@@ -314,10 +308,9 @@
         far = wx[i] * y[p]
         rs[pl.ds(64 * k, 64), :] = far
         rs[pl.ds(128 + 64 * k, 64), :] = (far - OMEGA * y[p]) + inside_plane(far) + x[p]
-    lo_pick, hi_pick = plane_picks()
     low = jnp.concatenate([row_pairs(rs, 0, 32), row_pairs(rs, 192, 32)], 0)
     high = jnp.concatenate([row_pairs(rs, 64, 32), row_pairs(rs, 128, 32)], 0)
-    terms = dot(low, lo_pick) + dot(high, hi_pick)
+    terms = halves(low, high)
     mix = terms[32:]
     b = [jnp.where(lane >= 64, mix, 0.0), block + terms[:32], jnp.where(lane < 64, mix, 0.0)]
     v = [zero] + [w1[j + 1] * b[j] for j in range(3)] + [zero]
@@ -328,15 +321,19 @@
     r.append(0.5 * around_block(zero, v[3], zero))
     for k in range(5):
         rs[pl.ds(32 * k, 32), :] = r[k]
-    low = dot(row_pairs(rs, 0, 80), picks(lambda i, j: ((i & 63) >> 1) == (j & 31), 0.125))
+    low = quarters(row_pairs(rs, 0, 80))
     group = iota((16, 128), 1) >> 5
     message = low[:16]
     for k in (1, 2, 3):
         message = jnp.where(group == k, low[16 * k : 16 * k + 16], message)
-    last = jnp.where(group[:8] == 0, low[64:72], low[72:80])
+    pieces = [message[4 * k : 4 * k + 4] for k in range(4)]
+    last = low[64:68]
+    for k in (1, 2, 3):
+        last = jnp.where(group[:4] == k, low[64 + 4 * k : 68 + 4 * k], last)
+    pieces.append(last)
     for peer in range(SLABS):
-        send[peer, pl.ds(0, 16), :] = message
-        send[peer, pl.ds(16, 8), :] = last
+        for k in range(5):
+            send[5 * peer + k] = pieces[k]
 
 
 def spread(v):
@@ -347,13 +344,13 @@
 def to_coarsest(v, t3):
     for k in range(4):
         t3[pl.ds(16 * k, 16), :] = v[32 * k : 32 * k + 16] + v[32 * k + 16 : 32 * k + 32]
-    pick = picks(lambda i, j: (j < 64) & ((i >> 5) == (j >> 4)) & (((i & 31) >> 1) == (j & 15)), 0.125)
-    return dot(row_pairs(t3, 0, 32), pick)
+    v = row_pairs(t3, 0, 32)
+    return 0.125 * (v + pltpu.roll(v, 127, 1))
 
 
 def from_coarsest(v, t3):
-    pick = picks(lambda i, j: (i < 64) & ((j >> 5) == (i >> 4)) & (((j & 31) >> 1) == (i & 15)), 1.0)
-    v = dot(v, pick)
+    v = jnp.where((iota(v.shape, 1) & 1) == 0, v, 0.0)
+    v = v + pltpu.roll(v, 1, 1)
     t3[pl.ds(0, 32, stride=2), :] = v
     t3[pl.ds(1, 32, stride=2), :] = v
     parts = []
@@ -363,9 +360,15 @@
     return jnp.concatenate(parts, 0)
 
 
-def low_levels(first, got, w2, d2, w3, x2, t3):
+def low_levels(first, got, w2, d2, w3, x2, t3, joined=None):
     group = iota((16, 128), 1) >> 5
-    narrow = iota((8, 128), 1) >> 5
+    quarter = iota((16, 128), 0) >> 2
+    if not first:
+        for z in range(SLABS):
+            for k in range(4):
+                joined[z, pl.ds(4 * k, 4), :] = got[5 * z + k]
+                joined[z, pl.ds(16 + 4 * k, 4), :] = got[5 * z + 4]
+    rows = got if first else joined
     reach = 1 if first else 2
     parts, caps = [], []
     for zl in range(8):
@@ -375,11 +378,9 @@
             v = jnp.zeros((16, 128), F32)
             for k in range(3 if first else 4):
                 if 0 <= z + reach - k < SLABS:
-                    v = jnp.where(group == k, got[z + reach - k, pl.ds(0, 16), :], v)
+                    v = jnp.where(group == k, rows[z + reach - k, pl.ds(0, 16), :], v)
             if not first and z >= 2:
-                last = got[z - 2, pl.ds(16, 8), :]
-                halves = [jnp.where(narrow == k, last, 0.0) for k in range(2)]
-                v = v + jnp.concatenate(halves, 0)
+                v = v + jnp.where(group == quarter, rows[z - 2, pl.ds(16, 16), :], 0.0)
             v = spread(v)
             total = v if total is None else jnp.where(group == zh, v, total)
             if first:
@@ -407,8 +408,8 @@
     low_levels(True, got, w2, d2, w3, x2, t3)
 
 
-def next_low_body(got, w2, d2, w3, after, x2, t3):
-    low_levels(False, got, w2, d2, w3, x2, t3)
+def next_low_body(got, w2, d2, w3, after, x2, t3, joined):
+    low_levels(False, got, w2, d2, w3, x2, t3, joined)
 
 
 def fine_up(x2, lo2, pair, hi2, c1, wx, yx, xs, w1, work, out):
@@ -434,16 +435,14 @@
     for j, b in enumerate(blocks(0)):
         y1[j] = w1[j] * b
     zero = jnp.zeros((32, 128), F32)
-    group = iota((16, 128), 1) >> 5
-    parts = []
+    lane = iota((16, 128), 1)
     for j in range(5):
         z = s + (j - 2)
         v = x2[pl.ds(pl.multiple_of((z & 7) * 16, 16), 16), :]
-        parts.append(spread(jnp.where(group == (z >> 3), v, 0.0)))
-    pick = picks(lambda i, j: i == ((j & 63) >> 1), 1.0)
-    v = dot(jnp.concatenate(parts, 0), pick)
-    f1[pl.ds(0, 80, stride=2), :] = v
-    f1[pl.ds(1, 80, stride=2), :] = v
+        v = lanes_of(v, ((lane & 63) >> 1) + ((z >> 3) & 3) * 32)
+        v = jnp.where((z >= 0) & (z < SLABS), v, 0.0)
+        f1[pl.ds(32 * j, 16, stride=2), :] = v
+        f1[pl.ds(32 * j + 1, 16, stride=2), :] = v
     for j in range(5):
         below = y1[j - 1] if j > 0 else zero
         above = y1[j + 1] if j < 4 else zero
@@ -456,9 +455,14 @@
             t = around_block(c, old[j - 1], old[j + 1])
             new[j] = 0.2 * c + y1[j] + 0.5 * w1[j] * t
     one, two, three = xa[1], xa[2], xa[3]
-    low = dot(jnp.concatenate([two, three], 0), picks(lambda i, j: i == (j >> 1), 1.0))
-    high = dot(jnp.concatenate([one, two], 0), picks(lambda i, j: i == (j >> 1) + 64, 1.0))
-    for q, v in enumerate((high[:32], low[:32], high[32:], low[32:])):
+    half = iota((32, 128), 1) >> 1
+    wide = (
+        lanes_of(one, half + 64),
+        lanes_of(two, half),
+        lanes_of(two, half + 64),
+        lanes_of(three, half),
+    )
+    for q, v in enumerate(wide):
         f0[pl.ds(64 * q, 32, stride=2), :] = v
         f0[pl.ds(64 * q + 1, 32, stride=2), :] = v
     for i in range(8):
@@ -481,7 +485,7 @@
         b_out[p] = cap[p] * u + src[0, 1, p]
 
     fine_up(x2, lo2, pair, hi2, c1, wx, yx, xs, w1, work, out)
-    own = local_down(lambda p: b_out[p], cap, w, y, x, rs, *plane_picks(), False)
+    own = local_down(lambda p: b_out[p], cap, w, y, x, rs, False)
     wide_share(own, y, x, wx, w1, c1, send, rs)
     block[...] = own
     fill_edges(up, dn, y, x)
@@ -511,7 +515,7 @@
 PLANE = (NY, NX)
 PLANE4 = (DEPTH, NY, NX)
 MESSAGE = f32(SLABS, 16, 128)
-WIDE_MESSAGE = f32(SLABS, 24, 128)
+WIDE_MESSAGE = f32(SLABS * 5, 4, 128)
 
 
 def moved(x, spans, slabs):
@@ -580,7 +584,11 @@
         *(y, x, block, lo, hi, w, wx),
     )
     (x2,) = call(
-        next_low_body, (f32(128, 128),), LOW_WORK, *(got, w2, d2, w3, pair), flops=LOW_FLOPS
+        next_low_body,
+        (f32(128, 128),),
+        [*LOW_WORK, (SLABS, 32, 128)],
+        *(got, w2, d2, w3, pair),
+        flops=LOW_FLOPS,
     )
     (u,) = call(next_up_body, (f32(1, *PLANE4),), WORK, *(x2, *near(pair), wx, yx, xs, w1))
     updated = jnp.where(lax.axis_index("tm") == 0, u0, moved(u, 1, 0))

time: 73.4 us -> 71.1 us (0.969)
  waiting for transfers between devices: 23.4 us -> 21.9 us
  Pallas kernels: 10.8 us -> 9.83 us
    ppermute x9, waiting for transfers between devices: 16.4 us -> 14.9 us  [moved(): return lax.ppermute(x, ('tm', 'space'), pairs)]
    pallas_call x7, Pallas kernels: 10.8 us -> 9.83 us  [call(): pl.pallas_call(body, out_shape=outs, in_specs=[space] * len(args), out_sp...]
where the time goes in v9:
time: 71.1 us; the launch traced here: 70.6 us
  starting transfers between devices  37.4 us (53%)
  waiting for transfers between devices  21.9 us (31%)
  Pallas kernels  9.83 us (14%)
  between operations  0.77 us (1%)
    ppermute x9, starting transfers between devices, moved(): return lax.ppermute(x, ('tm', 'space'), pairs)  25.3 us
    ppermute x9, waiting for transfers between devices, moved(): return lax.ppermute(x, ('tm', 'space'), pairs)  14.9 us
    all_to_all x2, starting transfers between devices, gathered(): return lax.all_to_all(send, 'space', 0, 0, tiled=True)  12 us
    pallas_call x7, Pallas kernels, call(): pl.pallas_call(body, out_shape=outs, in_specs=[space] * len(args), out_sp...  9.83 us
    all_to_all x2, waiting for transfers between devices, gathered(): return lax.all_to_all(send, 'space', 0, 0, tiled=True)  7.05 us
  transfers between devices with their start and end apart: 11, of which 4 were waited for; matrix products, arithmetic and copies ran while one was open for 0% of the time, Pallas kernels for 6%

profile of v9, /device:TPU:4, one launch (start us, length us, event | category | flops | bytes accessed | tf_op | source)
XLA Modules:
  0.0 70.6 jit_solution(17565391367988235696)
XLA Ops:
  0.6 1.5 %shard_map.50 = (f32[4,64,128]{2,1,0:T(8,128)S(1)}, f32[4,64,128]{2,1,0:T(8,128)S(1)}, f32[4,64,128]{2,1,0:T(8,128)S(1)}, f32[64,128]{1,0:T(8,128)S(1)}, f32[288...) custom-call(f32[1,4,64,128]{3,2,1,0:T(8,128)} %u.1, f32[1,2,4,64,128]{4,3,2,1,0:T(8,128)} %src.3, ...), custom_call_target="tpu_custom_call" | custom-call | tf_op jit(solution)/shard_map/pallas_call | solution.py:24
  2.1 1.7 %collective-permute-start = (f32[288,128]{1,0:T(8,128)S(1)}, f32[288,128]{1,0:T(8,128)S(1)}, u32[]{:S(2)}, u32[]{:S(2)}) collective-permute-start(f32[288,128]{1,0:T(8,128)S(1)} %get-tuple-element.33), channel_id=1, source_target_pairs={{0,1},{1,2},{2,3},{3,4},{4,5},{5,6},{6,7},{7,8},{8,9},{9,10},{10,1... | collective-permute-start | bytes 442376 | tf_op jit(solution)/shard_map/ppermute | solution.py:526
  3.7 6.8 %collective-permute-start.1 = (f32[288,128]{1,0:T(8,128)S(1)}, f32[288,128]{1,0:T(8,128)S(1)}, u32[]{:S(2)}, u32[]{:S(2)}) collective-permute-start(f32[288,128]{1,0:T(8,128)S(1)} %get-tuple-element.34), channel_id=1, source_target_pairs={{0,31},{1,0},{2,1},{3,2},{4,3},{5,4},{6,5},{7,6},{8,7},{9,8},{10,9... | collective-permute-start | bytes 442376 | tf_op jit(solution)/shard_map/ppermute | solution.py:526
  10.6 3.8 %collective-permute-done.lo = f32[288,128]{1,0:T(8,128)S(1)} collective-permute-done((f32[288,128]{1,0:T(8,128)S(1)}, f32[288,128]{1,0:T(8,128)S(1)}, u32[]{:S(2)}, u32[]{:S(2)}) %collective-permute-start) | collective-permute-done | bytes 147488 | tf_op jit(solution)/shard_map/ppermute | solution.py:526
  14.3 1.2 %shard_map.51 = (f32[6,64,128]{2,1,0:T(8,128)S(1)}, f32[6,64,128]{2,1,0:T(8,128)S(1)}, f32[8,64,128]{2,1,0:T(8,128)S(1)}, f32[128,128]{1,0:T(8,128)S(1)}, f32[32,16,128]{2,1,0:T(8,128)}) custom-call(f32[4,64,128]{2,1,0:T(8,128)S(1)} %get-tuple-element.29.w, f32[4,64,128]{2,1,0:T(8,128)S(1)} %get-tuple-element.30.y, f32[4,64,128]{2,1,0:T(8,128)S(1)} %get-tuple-element.31.x, ...), custom_call_target="tpu_custom_call" | custom-call | tf_op jit(solution)/shard_map/pallas_call | solution.py:24
  15.6 8.0 %all-to-all-start = ((f32[32,16,128]{2,1,0:T(8,128)}), f32[32,16,128]{2,1,0:T(8,128)S(1)}, u32[]{:S(2)}, u32[]{:S(2)}) async-start(f32[32,16,128]{2,1,0:T(8,128)} %get-tuple-element.35), calls=%async_computation | async-start | bytes 524288 | tf_op jit(solution)/shard_map/all_to_all | solution.py:530
  23.6 0.0 copy-start
  23.6 3.4 %collective-permute-start.2 = (f32[128,128]{1,0:T(8,128)S(1)}, f32[128,128]{1,0:T(8,128)S(1)}, u32[]{:S(2)}, u32[]{:S(2)}) collective-permute-start(f32[128,128]{1,0:T(8,128)S(1)} %get-tuple-element.37.pair), channel_id=1, source_target_pairs={{0,2},{1,3},{2,4},{3,5},{4,6},{5,7},{6,8},{7,9},{8,10},{9,11},{10,... | collective-permute-start | bytes 196616 | tf_op jit(solution)/shard_map/ppermute | solution.py:526
  27.0 2.3 %collective-permute-start.3 = (f32[128,128]{1,0:T(8,128)S(1)}, f32[128,128]{1,0:T(8,128)S(1)}, u32[]{:S(2)}, u32[]{:S(2)}) collective-permute-start(f32[128,128]{1,0:T(8,128)S(1)} %get-tuple-element.37.pair), channel_id=1, source_target_pairs={{0,30},{1,31},{2,0},{3,1},{4,2},{5,3},{6,4},{7,5},{8,6},{9,7},{10,... | collective-permute-start | bytes 196616 | tf_op jit(solution)/shard_map/ppermute | solution.py:526
  29.3 7.0 %all-to-all-done.got = f32[32,16,128]{2,1,0:T(8,128)S(1)} async-done(((f32[32,16,128]{2,1,0:T(8,128)}), f32[32,16,128]{2,1,0:T(8,128)S(1)}, u32[]{:S(2)}, u32[]{:S(2)}) %all-to-all-start) | async-done | bytes 262176 | tf_op jit(solution)/shard_map/all_to_all | solution.py:530
  36.3 2.1 %shard_map.52 = (f32[128,128]{1,0:T(8,128)S(1)}, f32[128,128]{1,0:T(8,128)S(1)}, f32[32,128]{1,0:T(8,128)S(1)}, f32[128,128]{1,0:T(8,128)S(1)}) custom-call(f32[32,16,128]{2,1,0:T(8,128)S(1)} %all-to-all-done.got), custom_call_target="tpu_custom_call" | custom-call | flops 2147483648 | tf_op jit(solution)/shard_map/pallas_call | solution.py:24
  38.5 2.1 %shard_map.53 = (f32[1,4,64,128]{3,2,1,0:T(8,128)}, f32[4,64,128]{2,1,0:T(8,128)S(1)}, f32[4,64,128]{2,1,0:T(8,128)S(1)}, f32[32,128]{1,0:T(8,128)S(1)}, f32[224...) custom-call(f32[128,128]{1,0:T(8,128)S(1)} %get-tuple-element.36.x2, ...), custom_call_target="tpu_custom_call" | custom-call | tf_op jit(solution)/shard_map/pallas_call | solution.py:24
  40.6 4.0 %all-to-all-start.1 = ((f32[160,4,128]{2,1,0:T(4,128)}), f32[160,4,128]{2,1,0:T(4,128)S(1)}, u32[]{:S(2)}, u32[]{:S(2)}) async-start(f32[160,4,128]{2,1,0:T(4,128)} %get-tuple-element.43), calls=%async_computation.1 | async-start | bytes 655360 | tf_op jit(solution)/shard_map/all_to_all | solution.py:530
  44.6 1.9 %collective-permute-start.4 = (f32[224,128]{1,0:T(8,128)S(1)}, f32[224,128]{1,0:T(8,128)S(1)}, u32[]{:S(2)}, u32[]{:S(2)}) collective-permute-start(f32[224,128]{1,0:T(8,128)S(1)} %get-tuple-element.50), channel_id=1, source_target_pairs={{0,1},{1,2},{2,3},{3,4},{4,5},{5,6},{6,7},{7,8},{8,9},{9,10},{10,1... | collective-permute-start | bytes 344072 | tf_op jit(solution)/shard_map/ppermute | solution.py:526
  46.5 3.6 %collective-permute-start.5 = (f32[224,128]{1,0:T(8,128)S(1)}, f32[224,128]{1,0:T(8,128)S(1)}, u32[]{:S(2)}, u32[]{:S(2)}) collective-permute-start(f32[224,128]{1,0:T(8,128)S(1)} %get-tuple-element.51), channel_id=1, source_target_pairs={{0,31},{1,0},{2,1},{3,2},{4,3},{5,4},{6,5},{7,6},{8,7},{9,8},{10,9... | collective-permute-start | bytes 344072 | tf_op jit(solution)/shard_map/ppermute | solution.py:526
  50.0 6.7 %collective-permute-done.4.lo = f32[224,128]{1,0:T(8,128)S(1)} collective-permute-done((f32[224,128]{1,0:T(8,128)S(1)}, f32[224,128]{1,0:T(8,128)S(1)}, u32[]{:S(2)}, u32[]{:S(2)}) %collective-permute-start.4) | collective-permute-done | bytes 114720 | tf_op jit(solution)/shard_map/ppermute | solution.py:526
  56.8 0.3 shard_map.54
  57.1 0.1 collective-permute-start.6
  57.1 5.6 %collective-permute-start.7 = (f32[64,128]{1,0:T(8,128)S(1)}, f32[64,128]{1,0:T(8,128)S(1)}, u32[]{:S(2)}, u32[]{:S(2)}) collective-permute-start(f32[64,128]{1,0:T(8,128)S(1)} %get-tuple-element.52.after.pair), channel_id=1, source_target_pairs={{0,30},{1,31},{2,0},{3,1},{4,2},{5,3},{6,4},{7,5},{8,6},{9,7},{10,... | collective-permute-start | bytes 98312 | tf_op jit(solution)/shard_map/ppermute | solution.py:526
  62.8 2.0 %shard_map.55.x2 = f32[128,128]{1,0:T(8,128)S(1)} custom-call(f32[160,4,128]{2,1,0:T(4,128)S(1)} %all-to-all-done.1.got, f32[128,128]{1,0:T(8,128)S(1)} %get-tuple-element.44.w2, f32[128,128]{1,0:T(8,128)S(1)} %get-tuple-element.45.d2, f32[32,128]{1,0:T(8,128)S(1)} %get-tuple-element.46.w3, f32[64,128]{1,0:T(8,128)S(1)} %get-tuple-element.52.after.pair), custom_call_target="tpu_custom_call" | custom-call | flops 2147483648 | tf_op jit(solution)/shard_map/pallas_call | solution.py:24
  64.8 0.7 shard_map.56
  65.5 0.0 collective-permute-start.8
  65.5 4.4 %collective-permute-done.8 = f32[1,4,64,128]{3,2,1,0:T(8,128)S(1)} collective-permute-done((f32[1,4,64,128]{3,2,1,0:T(8,128)S(1)}, f32[1,4,64,128]{3,2,1,0:T(8,128)S(1)}, u32[]{:S(2)}, u32[]{:S(2)}) %collective-permute-start.8) | collective-permute-done | bytes 131104 | tf_op jit(solution)/shard_map/ppermute | solution.py:526
  69.9 0.7 broadcast_select_fusion
  (10 shorter events, 0.0 us)
Async XLA Ops:
  2.1 12.2 %collective-permute-start = (f32[288,128]{1,0:T(8,128)S(1)}, f32[288,128]{1,0:T(8,128)S(1)}, u32[]{:S(2)}, u32[]{:S(2)}) collective-permute-start(f32[288,128]{1,0:T(8,128)S(1)} %get-tuple-element.33), channel_id=1, source_target_pairs={{0,1},{1,2},{2,3},{3,4},{4,5},{5,6},{6,7},{7,8},{8,9},{9,10},{10,1... | collective-permute-start | bytes 442376 | tf_op jit(solution)/shard_map/ppermute | solution.py:526
  3.7 10.6 %collective-permute-start.1 = (f32[288,128]{1,0:T(8,128)S(1)}, f32[288,128]{1,0:T(8,128)S(1)}, u32[]{:S(2)}, u32[]{:S(2)}) collective-permute-start(f32[288,128]{1,0:T(8,128)S(1)} %get-tuple-element.34), channel_id=1, source_target_pairs={{0,31},{1,0},{2,1},{3,2},{4,3},{5,4},{6,5},{7,6},{8,7},{9,8},{10,9... | collective-permute-start | bytes 442376 | tf_op jit(solution)/shard_map/ppermute | solution.py:526
  15.6 20.8 %all-to-all-start = ((f32[32,16,128]{2,1,0:T(8,128)}), f32[32,16,128]{2,1,0:T(8,128)S(1)}, u32[]{:S(2)}, u32[]{:S(2)}) async-start(f32[32,16,128]{2,1,0:T(8,128)} %get-tuple-element.35), calls=%async_computation | async-start | bytes 524288 | tf_op jit(solution)/shard_map/all_to_all | solution.py:530
  23.6 14.9 %copy-start = (f32[1,2,4,64,128]{4,3,2,1,0:T(8,128)S(1)}, f32[1,2,4,64,128]{4,3,2,1,0:T(8,128)}, u32[]{:S(2)}) copy-start(f32[1,2,4,64,128]{4,3,2,1,0:T(8,128)} %src.3) | copy-start | bytes 786436
  23.6 14.8 %collective-permute-start.2 = (f32[128,128]{1,0:T(8,128)S(1)}, f32[128,128]{1,0:T(8,128)S(1)}, u32[]{:S(2)}, u32[]{:S(2)}) collective-permute-start(f32[128,128]{1,0:T(8,128)S(1)} %get-tuple-element.37.pair), channel_id=1, source_target_pairs={{0,2},{1,3},{2,4},{3,5},{4,6},{5,7},{6,8},{7,9},{8,10},{9,11},{10,... | collective-permute-start | bytes 196616 | tf_op jit(solution)/shard_map/ppermute | solution.py:526
  27.0 11.5 %collective-permute-start.3 = (f32[128,128]{1,0:T(8,128)S(1)}, f32[128,128]{1,0:T(8,128)S(1)}, u32[]{:S(2)}, u32[]{:S(2)}) collective-permute-start(f32[128,128]{1,0:T(8,128)S(1)} %get-tuple-element.37.pair), channel_id=1, source_target_pairs={{0,30},{1,31},{2,0},{3,1},{4,2},{5,3},{6,4},{7,5},{8,6},{9,7},{10,... | collective-permute-start | bytes 196616 | tf_op jit(solution)/shard_map/ppermute | solution.py:526
  40.6 22.2 %all-to-all-start.1 = ((f32[160,4,128]{2,1,0:T(4,128)}), f32[160,4,128]{2,1,0:T(4,128)S(1)}, u32[]{:S(2)}, u32[]{:S(2)}) async-start(f32[160,4,128]{2,1,0:T(4,128)} %get-tuple-element.43), calls=%async_computation.1 | async-start | bytes 655360 | tf_op jit(solution)/shard_map/all_to_all | solution.py:530
  44.6 12.2 %collective-permute-start.4 = (f32[224,128]{1,0:T(8,128)S(1)}, f32[224,128]{1,0:T(8,128)S(1)}, u32[]{:S(2)}, u32[]{:S(2)}) collective-permute-start(f32[224,128]{1,0:T(8,128)S(1)} %get-tuple-element.50), channel_id=1, source_target_pairs={{0,1},{1,2},{2,3},{3,4},{4,5},{5,6},{6,7},{7,8},{8,9},{9,10},{10,1... | collective-permute-start | bytes 344072 | tf_op jit(solution)/shard_map/ppermute | solution.py:526
  46.5 10.3 %collective-permute-start.5 = (f32[224,128]{1,0:T(8,128)S(1)}, f32[224,128]{1,0:T(8,128)S(1)}, u32[]{:S(2)}, u32[]{:S(2)}) collective-permute-start(f32[224,128]{1,0:T(8,128)S(1)} %get-tuple-element.51), channel_id=1, source_target_pairs={{0,31},{1,0},{2,1},{3,2},{4,3},{5,4},{6,5},{7,6},{8,7},{9,8},{10,9... | collective-permute-start | bytes 344072 | tf_op jit(solution)/shard_map/ppermute | solution.py:526
  57.1 7.7 %collective-permute-start.6 = (f32[64,128]{1,0:T(8,128)S(1)}, f32[64,128]{1,0:T(8,128)S(1)}, u32[]{:S(2)}, u32[]{:S(2)}) collective-permute-start(f32[64,128]{1,0:T(8,128)S(1)} %get-tuple-element.52.after.pair), channel_id=1, source_target_pairs={{0,2},{1,3},{2,4},{3,5},{4,6},{5,7},{6,8},{7,9},{8,10},{9,11},{10,... | collective-permute-start | bytes 98312 | tf_op jit(solution)/shard_map/ppermute | solution.py:526
  57.1 7.7 %collective-permute-start.7 = (f32[64,128]{1,0:T(8,128)S(1)}, f32[64,128]{1,0:T(8,128)S(1)}, u32[]{:S(2)}, u32[]{:S(2)}) collective-permute-start(f32[64,128]{1,0:T(8,128)S(1)} %get-tuple-element.52.after.pair), channel_id=1, source_target_pairs={{0,30},{1,31},{2,0},{3,1},{4,2},{5,3},{6,4},{7,5},{8,6},{9,7},{10,... | collective-permute-start | bytes 98312 | tf_op jit(solution)/shard_map/ppermute | solution.py:526
  64.8 5.1 %copy-start.1 = (f32[1,4,64,128]{3,2,1,0:T(8,128)S(1)}, f32[1,4,64,128]{3,2,1,0:T(8,128)}, u32[]{:S(2)}) copy-start(f32[1,4,64,128]{3,2,1,0:T(8,128)} %u.1) | copy-start | bytes 393220
  65.5 4.4 %collective-permute-start.8 = (f32[1,4,64,128]{3,2,1,0:T(8,128)S(1)}, f32[1,4,64,128]{3,2,1,0:T(8,128)S(1)}, u32[]{:S(2)}, u32[]{:S(2)}) collective-permute-start(f32[1,4,64,128]{3,2,1,0:T(8,128)S(1)} %shard_map.56), channel_id=1, source_target_pairs={{0,32},{1,33},{2,34},{3,35},{4,36},{5,37},{6,38},{7,39},{8,40},{9,... | collective-permute-start | bytes 393224 | tf_op jit(solution)/shard_map/ppermute | solution.py:526

commit v10 on v9

--- a/solution.py
+++ b/solution.py
@@ -90,25 +90,25 @@
 
 
 def rolled(v, k, j):
-    return pltpu.roll(v[k % 4], (2 * j - 32 * (k // 4)) % 128, 1) if (k // 4 or j) else v[k]
-
-
-CENTRE = [(k, 0) for k in range(4)]
-FIRST = [(k, j) for k in range(4) for j in (-1, 0, 1)] + [(-1, 0), (4, 0)]
+    return pltpu.roll(v[k % 2], (j - 16 * (k // 2)) % 128, 1) if (k // 2 or j) else v[k]
+
+
+CENTRE = [(k, 0) for k in range(2)]
+FIRST = [(k, j) for k in range(2) for j in (-1, 0, 1)] + [(-1, 0), (2, 0)]
 
 
 def coarsest(b3, w3):
     lane, row = iota((8, 128), 1), iota((8, 128), 0)
-    x = (lane & 31) >> 1
+    x = lane & 15
     base, own = [], []
-    for k in range(4):
+    for k in range(2):
         w = w3[8 * k : 8 * k + 8]
         wh = 0.125 * w
         own.append(w * b3[8 * k : 8 * k + 8])
         base.append(
             (
-                jnp.where(lane >= 32, wh, 0.0) if k == 0 else wh,
-                jnp.where(lane < 96, wh, 0.0) if k == 3 else wh,
+                jnp.where(lane >= 16, wh, 0.0) if k == 0 else wh,
+                jnp.where(lane < 112, wh, 0.0) if k == 1 else wh,
                 jnp.where(x > 0, wh, 0.0),
                 jnp.where(x < 15, wh, 0.0),
                 jnp.where(row > 0, wh, 0.0),
@@ -130,9 +130,9 @@
     def copies(v, reach):
         return {
             (k, j): rolled(v, k, j)
-            for k in range(-reach, 4 + reach)
+            for k in range(-reach, 2 + reach)
             for j in range(-reach, reach + 1)
-            if max(0, -k, k - 3) + abs(j) <= reach
+            if max(0, -k, k - 1) + abs(j) <= reach
         }
 
     def one(v):
@@ -345,12 +345,16 @@
     for k in range(4):
         t3[pl.ds(16 * k, 16), :] = v[32 * k : 32 * k + 16] + v[32 * k + 16 : 32 * k + 32]
     v = row_pairs(t3, 0, 32)
-    return 0.125 * (v + pltpu.roll(v, 127, 1))
+    lane = iota(v.shape, 1)
+    at = (lane & 96) + 2 * (lane & 15)
+    v = 0.125 * (lanes_of(v, at) + lanes_of(v, at + 1))
+    return jnp.where((lane[:16] & 16) == 0, v[:16], v[16:])
 
 
 def from_coarsest(v, t3):
-    v = jnp.where((iota(v.shape, 1) & 1) == 0, v, 0.0)
-    v = v + pltpu.roll(v, 1, 1)
+    lane = iota(v.shape, 1)
+    at = (lane & 96) + ((lane & 31) >> 1)
+    v = jnp.concatenate([lanes_of(v, at), lanes_of(v, at + 16)], 0)
     t3[pl.ds(0, 32, stride=2), :] = v
     t3[pl.ds(1, 32, stride=2), :] = v
     parts = []
@@ -530,8 +534,15 @@
     return lax.all_to_all(send, "space", 0, 0, tiled=True)
 
 
+def both(up, dn, reach):
+    lo = moved(up, 0, reach)
+    hi = moved(dn, 0, -reach)
+    return lo, hi
+
+
 def near(pair):
-    return moved(pair, 0, 2), pair, moved(pair, 0, -2)
+    lo, hi = both(pair, pair, 2)
+    return lo, pair, hi
 
 
 def shards(u0, src, cap):
@@ -544,7 +555,7 @@
         space=pl.BlockSpec(memory_space=pltpu.HBM),
         sems=[pltpu.SemaphoreType.DMA((3,))],
     )
-    lo, hi = moved(up, 0, 1), moved(dn, 0, -1)
+    lo, hi = both(up, dn, 1)
     wx, yx, xs, pair, send = call(
         first_down_body,
         (f32(6, *PLANE), f32(6, *PLANE), f32(8, *PLANE), f32(128, 128), MESSAGE),
@@ -554,7 +565,7 @@
     got = gathered(send)
     w2, d2, w3, x2 = call(
         first_low_body,
-        (f32(128, 128), f32(128, 128), f32(32, 128), f32(128, 128)),
+        (f32(128, 128), f32(128, 128), f32(16, 128), f32(128, 128)),
         LOW_WORK,
         got,
         flops=LOW_FLOPS,
@@ -575,8 +586,7 @@
         *(x2, *near(pair), wx, yx, xs, w, cap_in, src),
     )
     got = gathered(send)
-    lo = moved(up, 0, 1)
-    hi = moved(dn, 0, -1)
+    lo, hi = both(up, dn, 1)
     yx, xs, pair = call(
         next_down_body,
         (f32(6, *PLANE), f32(8, *PLANE), f32(64, 128)),

time: 71.1 us -> 71.1 us (level)
  no operation moved by 1% of the time
where the time goes in v10:
time: 71.1 us; the launch traced here: 70.4 us
  starting transfers between devices  37.5 us (53%)
  waiting for transfers between devices  21.9 us (31%)
  Pallas kernels  9.6 us (14%)
  between operations  0.76 us (1%)
    ppermute x9, starting transfers between devices, moved(): return lax.ppermute(x, ('tm', 'space'), pairs)  25.3 us
    ppermute x9, waiting for transfers between devices, moved(): return lax.ppermute(x, ('tm', 'space'), pairs)  14.9 us
    all_to_all x2, starting transfers between devices, gathered(): return lax.all_to_all(send, 'space', 0, 0, tiled=True)  12.1 us
    pallas_call x7, Pallas kernels, call(): pl.pallas_call(body, out_shape=outs, in_specs=[space] * len(args), out_sp...  9.6 us
    all_to_all x2, waiting for transfers between devices, gathered(): return lax.all_to_all(send, 'space', 0, 0, tiled=True)  7.05 us
  transfers between devices with their start and end apart: 11, of which 4 were waited for; matrix products, arithmetic and copies ran while one was open for 0% of the time, Pallas kernels for 6%

profile of v10, /device:TPU:4, one launch (start us, length us, event | category | flops | bytes accessed | tf_op | source)
XLA Modules:
  0.0 70.4 jit_solution(6762860282030174891)
XLA Ops:
  0.6 1.5 %shard_map.50 = (f32[4,64,128]{2,1,0:T(8,128)S(1)}, f32[4,64,128]{2,1,0:T(8,128)S(1)}, f32[4,64,128]{2,1,0:T(8,128)S(1)}, f32[64,128]{1,0:T(8,128)S(1)}, f32[288...) custom-call(f32[1,4,64,128]{3,2,1,0:T(8,128)} %u.1, f32[1,2,4,64,128]{4,3,2,1,0:T(8,128)} %src.3, ...), custom_call_target="tpu_custom_call" | custom-call | tf_op jit(solution)/shard_map/pallas_call | solution.py:24
  2.1 1.7 %collective-permute-start = (f32[288,128]{1,0:T(8,128)S(1)}, f32[288,128]{1,0:T(8,128)S(1)}, u32[]{:S(2)}, u32[]{:S(2)}) collective-permute-start(f32[288,128]{1,0:T(8,128)S(1)} %get-tuple-element.33), channel_id=1, source_target_pairs={{0,1},{1,2},{2,3},{3,4},{4,5},{5,6},{6,7},{7,8},{8,9},{9,10},{10,1... | collective-permute-start | bytes 442376 | tf_op jit(solution)/shard_map/ppermute | solution.py:530
  3.7 6.8 %collective-permute-start.1 = (f32[288,128]{1,0:T(8,128)S(1)}, f32[288,128]{1,0:T(8,128)S(1)}, u32[]{:S(2)}, u32[]{:S(2)}) collective-permute-start(f32[288,128]{1,0:T(8,128)S(1)} %get-tuple-element.34), channel_id=1, source_target_pairs={{0,31},{1,0},{2,1},{3,2},{4,3},{5,4},{6,5},{7,6},{8,7},{9,8},{10,9... | collective-permute-start | bytes 442376 | tf_op jit(solution)/shard_map/ppermute | solution.py:530
  10.6 3.8 %collective-permute-done.lo = f32[288,128]{1,0:T(8,128)S(1)} collective-permute-done((f32[288,128]{1,0:T(8,128)S(1)}, f32[288,128]{1,0:T(8,128)S(1)}, u32[]{:S(2)}, u32[]{:S(2)}) %collective-permute-start) | collective-permute-done | bytes 147488 | tf_op jit(solution)/shard_map/ppermute | solution.py:530
  14.3 1.2 %shard_map.51 = (f32[6,64,128]{2,1,0:T(8,128)S(1)}, f32[6,64,128]{2,1,0:T(8,128)S(1)}, f32[8,64,128]{2,1,0:T(8,128)S(1)}, f32[128,128]{1,0:T(8,128)S(1)}, f32[32,16,128]{2,1,0:T(8,128)}) custom-call(f32[4,64,128]{2,1,0:T(8,128)S(1)} %get-tuple-element.29.w, f32[4,64,128]{2,1,0:T(8,128)S(1)} %get-tuple-element.30.y, f32[4,64,128]{2,1,0:T(8,128)S(1)} %get-tuple-element.31.x, ...), custom_call_target="tpu_custom_call" | custom-call | tf_op jit(solution)/shard_map/pallas_call | solution.py:24
  15.6 8.0 %all-to-all-start = ((f32[32,16,128]{2,1,0:T(8,128)}), f32[32,16,128]{2,1,0:T(8,128)S(1)}, u32[]{:S(2)}, u32[]{:S(2)}) async-start(f32[32,16,128]{2,1,0:T(8,128)} %get-tuple-element.35), calls=%async_computation | async-start | bytes 524288 | tf_op jit(solution)/shard_map/all_to_all | solution.py:534
  23.6 0.0 copy-start
  23.6 3.4 %collective-permute-start.2 = (f32[128,128]{1,0:T(8,128)S(1)}, f32[128,128]{1,0:T(8,128)S(1)}, u32[]{:S(2)}, u32[]{:S(2)}) collective-permute-start(f32[128,128]{1,0:T(8,128)S(1)} %get-tuple-element.37.pair), channel_id=1, source_target_pairs={{0,2},{1,3},{2,4},{3,5},{4,6},{5,7},{6,8},{7,9},{8,10},{9,11},{10,... | collective-permute-start | bytes 196616 | tf_op jit(solution)/shard_map/ppermute | solution.py:530
  27.0 2.3 %collective-permute-start.3 = (f32[128,128]{1,0:T(8,128)S(1)}, f32[128,128]{1,0:T(8,128)S(1)}, u32[]{:S(2)}, u32[]{:S(2)}) collective-permute-start(f32[128,128]{1,0:T(8,128)S(1)} %get-tuple-element.37.pair), channel_id=1, source_target_pairs={{0,30},{1,31},{2,0},{3,1},{4,2},{5,3},{6,4},{7,5},{8,6},{9,7},{10,... | collective-permute-start | bytes 196616 | tf_op jit(solution)/shard_map/ppermute | solution.py:530
  29.3 7.0 %all-to-all-done.got = f32[32,16,128]{2,1,0:T(8,128)S(1)} async-done(((f32[32,16,128]{2,1,0:T(8,128)}), f32[32,16,128]{2,1,0:T(8,128)S(1)}, u32[]{:S(2)}, u32[]{:S(2)}) %all-to-all-start) | async-done | bytes 262176 | tf_op jit(solution)/shard_map/all_to_all | solution.py:534
  36.3 2.0 %shard_map.52 = (f32[128,128]{1,0:T(8,128)S(1)}, f32[128,128]{1,0:T(8,128)S(1)}, f32[16,128]{1,0:T(8,128)S(1)}, f32[128,128]{1,0:T(8,128)S(1)}) custom-call(f32[32,16,128]{2,1,0:T(8,128)S(1)} %all-to-all-done.got), custom_call_target="tpu_custom_call" | custom-call | flops 2147483648 | tf_op jit(solution)/shard_map/pallas_call | solution.py:24
  38.4 2.1 %shard_map.53 = (f32[1,4,64,128]{3,2,1,0:T(8,128)}, f32[4,64,128]{2,1,0:T(8,128)S(1)}, f32[4,64,128]{2,1,0:T(8,128)S(1)}, f32[32,128]{1,0:T(8,128)S(1)}, f32[224...) custom-call(f32[128,128]{1,0:T(8,128)S(1)} %get-tuple-element.36.x2, ...), custom_call_target="tpu_custom_call" | custom-call | tf_op jit(solution)/shard_map/pallas_call | solution.py:24
  40.5 4.1 %all-to-all-start.1 = ((f32[160,4,128]{2,1,0:T(4,128)}), f32[160,4,128]{2,1,0:T(4,128)S(1)}, u32[]{:S(2)}, u32[]{:S(2)}) async-start(f32[160,4,128]{2,1,0:T(4,128)} %get-tuple-element.43), calls=%async_computation.1 | async-start | bytes 655360 | tf_op jit(solution)/shard_map/all_to_all | solution.py:534
  44.6 1.9 %collective-permute-start.4 = (f32[224,128]{1,0:T(8,128)S(1)}, f32[224,128]{1,0:T(8,128)S(1)}, u32[]{:S(2)}, u32[]{:S(2)}) collective-permute-start(f32[224,128]{1,0:T(8,128)S(1)} %get-tuple-element.50), channel_id=1, source_target_pairs={{0,1},{1,2},{2,3},{3,4},{4,5},{5,6},{6,7},{7,8},{8,9},{9,10},{10,1... | collective-permute-start | bytes 344072 | tf_op jit(solution)/shard_map/ppermute | solution.py:530
  46.5 3.6 %collective-permute-start.5 = (f32[224,128]{1,0:T(8,128)S(1)}, f32[224,128]{1,0:T(8,128)S(1)}, u32[]{:S(2)}, u32[]{:S(2)}) collective-permute-start(f32[224,128]{1,0:T(8,128)S(1)} %get-tuple-element.51), channel_id=1, source_target_pairs={{0,31},{1,0},{2,1},{3,2},{4,3},{5,4},{6,5},{7,6},{8,7},{9,8},{10,9... | collective-permute-start | bytes 344072 | tf_op jit(solution)/shard_map/ppermute | solution.py:530
  50.0 6.7 %collective-permute-done.4.lo = f32[224,128]{1,0:T(8,128)S(1)} collective-permute-done((f32[224,128]{1,0:T(8,128)S(1)}, f32[224,128]{1,0:T(8,128)S(1)}, u32[]{:S(2)}, u32[]{:S(2)}) %collective-permute-start.4) | collective-permute-done | bytes 114720 | tf_op jit(solution)/shard_map/ppermute | solution.py:530
  56.8 0.3 shard_map.54
  57.1 0.1 collective-permute-start.6
  57.1 5.6 %collective-permute-start.7 = (f32[64,128]{1,0:T(8,128)S(1)}, f32[64,128]{1,0:T(8,128)S(1)}, u32[]{:S(2)}, u32[]{:S(2)}) collective-permute-start(f32[64,128]{1,0:T(8,128)S(1)} %get-tuple-element.52.after.pair), channel_id=1, source_target_pairs={{0,30},{1,31},{2,0},{3,1},{4,2},{5,3},{6,4},{7,5},{8,6},{9,7},{10,... | collective-permute-start | bytes 98312 | tf_op jit(solution)/shard_map/ppermute | solution.py:530
  62.8 1.9 %shard_map.55.x2 = f32[128,128]{1,0:T(8,128)S(1)} custom-call(f32[160,4,128]{2,1,0:T(4,128)S(1)} %all-to-all-done.1.got, f32[128,128]{1,0:T(8,128)S(1)} %get-tuple-element.44.w2, f32[128,128]{1,0:T(8,128)S(1)} %get-tuple-element.45.d2, f32[16,128]{1,0:T(8,128)S(1)} %get-tuple-element.46.w3, f32[64,128]{1,0:T(8,128)S(1)} %get-tuple-element.52.after.pair), custom_call_target="tpu_custom_call" | custom-call | flops 2147483648 | tf_op jit(solution)/shard_map/pallas_call | solution.py:24
  64.7 0.7 shard_map.56
  65.4 0.0 collective-permute-start.8
  65.4 4.4 %collective-permute-done.8 = f32[1,4,64,128]{3,2,1,0:T(8,128)S(1)} collective-permute-done((f32[1,4,64,128]{3,2,1,0:T(8,128)S(1)}, f32[1,4,64,128]{3,2,1,0:T(8,128)S(1)}, u32[]{:S(2)}, u32[]{:S(2)}) %collective-permute-start.8) | collective-permute-done | bytes 131104 | tf_op jit(solution)/shard_map/ppermute | solution.py:530
  69.8 0.7 broadcast_select_fusion
  (10 shorter events, 0.0 us)
Async XLA Ops:
  2.1 12.2 %collective-permute-start = (f32[288,128]{1,0:T(8,128)S(1)}, f32[288,128]{1,0:T(8,128)S(1)}, u32[]{:S(2)}, u32[]{:S(2)}) collective-permute-start(f32[288,128]{1,0:T(8,128)S(1)} %get-tuple-element.33), channel_id=1, source_target_pairs={{0,1},{1,2},{2,3},{3,4},{4,5},{5,6},{6,7},{7,8},{8,9},{9,10},{10,1... | collective-permute-start | bytes 442376 | tf_op jit(solution)/shard_map/ppermute | solution.py:530
  3.7 10.6 %collective-permute-start.1 = (f32[288,128]{1,0:T(8,128)S(1)}, f32[288,128]{1,0:T(8,128)S(1)}, u32[]{:S(2)}, u32[]{:S(2)}) collective-permute-start(f32[288,128]{1,0:T(8,128)S(1)} %get-tuple-element.34), channel_id=1, source_target_pairs={{0,31},{1,0},{2,1},{3,2},{4,3},{5,4},{6,5},{7,6},{8,7},{9,8},{10,9... | collective-permute-start | bytes 442376 | tf_op jit(solution)/shard_map/ppermute | solution.py:530
  15.6 20.8 %all-to-all-start = ((f32[32,16,128]{2,1,0:T(8,128)}), f32[32,16,128]{2,1,0:T(8,128)S(1)}, u32[]{:S(2)}, u32[]{:S(2)}) async-start(f32[32,16,128]{2,1,0:T(8,128)} %get-tuple-element.35), calls=%async_computation | async-start | bytes 524288 | tf_op jit(solution)/shard_map/all_to_all | solution.py:534
  23.6 14.8 %copy-start = (f32[1,2,4,64,128]{4,3,2,1,0:T(8,128)S(1)}, f32[1,2,4,64,128]{4,3,2,1,0:T(8,128)}, u32[]{:S(2)}) copy-start(f32[1,2,4,64,128]{4,3,2,1,0:T(8,128)} %src.3) | copy-start | bytes 786436
  23.6 14.7 %collective-permute-start.2 = (f32[128,128]{1,0:T(8,128)S(1)}, f32[128,128]{1,0:T(8,128)S(1)}, u32[]{:S(2)}, u32[]{:S(2)}) collective-permute-start(f32[128,128]{1,0:T(8,128)S(1)} %get-tuple-element.37.pair), channel_id=1, source_target_pairs={{0,2},{1,3},{2,4},{3,5},{4,6},{5,7},{6,8},{7,9},{8,10},{9,11},{10,... | collective-permute-start | bytes 196616 | tf_op jit(solution)/shard_map/ppermute | solution.py:530
  27.0 11.4 %collective-permute-start.3 = (f32[128,128]{1,0:T(8,128)S(1)}, f32[128,128]{1,0:T(8,128)S(1)}, u32[]{:S(2)}, u32[]{:S(2)}) collective-permute-start(f32[128,128]{1,0:T(8,128)S(1)} %get-tuple-element.37.pair), channel_id=1, source_target_pairs={{0,30},{1,31},{2,0},{3,1},{4,2},{5,3},{6,4},{7,5},{8,6},{9,7},{10,... | collective-permute-start | bytes 196616 | tf_op jit(solution)/shard_map/ppermute | solution.py:530
  40.5 22.3 %all-to-all-start.1 = ((f32[160,4,128]{2,1,0:T(4,128)}), f32[160,4,128]{2,1,0:T(4,128)S(1)}, u32[]{:S(2)}, u32[]{:S(2)}) async-start(f32[160,4,128]{2,1,0:T(4,128)} %get-tuple-element.43), calls=%async_computation.1 | async-start | bytes 655360 | tf_op jit(solution)/shard_map/all_to_all | solution.py:534
  44.6 12.2 %collective-permute-start.4 = (f32[224,128]{1,0:T(8,128)S(1)}, f32[224,128]{1,0:T(8,128)S(1)}, u32[]{:S(2)}, u32[]{:S(2)}) collective-permute-start(f32[224,128]{1,0:T(8,128)S(1)} %get-tuple-element.50), channel_id=1, source_target_pairs={{0,1},{1,2},{2,3},{3,4},{4,5},{5,6},{6,7},{7,8},{8,9},{9,10},{10,1... | collective-permute-start | bytes 344072 | tf_op jit(solution)/shard_map/ppermute | solution.py:530
  46.5 10.3 %collective-permute-start.5 = (f32[224,128]{1,0:T(8,128)S(1)}, f32[224,128]{1,0:T(8,128)S(1)}, u32[]{:S(2)}, u32[]{:S(2)}) collective-permute-start(f32[224,128]{1,0:T(8,128)S(1)} %get-tuple-element.51), channel_id=1, source_target_pairs={{0,31},{1,0},{2,1},{3,2},{4,3},{5,4},{6,5},{7,6},{8,7},{9,8},{10,9... | collective-permute-start | bytes 344072 | tf_op jit(solution)/shard_map/ppermute | solution.py:530
  57.1 7.6 %collective-permute-start.6 = (f32[64,128]{1,0:T(8,128)S(1)}, f32[64,128]{1,0:T(8,128)S(1)}, u32[]{:S(2)}, u32[]{:S(2)}) collective-permute-start(f32[64,128]{1,0:T(8,128)S(1)} %get-tuple-element.52.after.pair), channel_id=1, source_target_pairs={{0,2},{1,3},{2,4},{3,5},{4,6},{5,7},{6,8},{7,9},{8,10},{9,11},{10,... | collective-permute-start | bytes 98312 | tf_op jit(solution)/shard_map/ppermute | solution.py:530
  57.1 7.5 %collective-permute-start.7 = (f32[64,128]{1,0:T(8,128)S(1)}, f32[64,128]{1,0:T(8,128)S(1)}, u32[]{:S(2)}, u32[]{:S(2)}) collective-permute-start(f32[64,128]{1,0:T(8,128)S(1)} %get-tuple-element.52.after.pair), channel_id=1, source_target_pairs={{0,30},{1,31},{2,0},{3,1},{4,2},{5,3},{6,4},{7,5},{8,6},{9,7},{10,... | collective-permute-start | bytes 98312 | tf_op jit(solution)/shard_map/ppermute | solution.py:530
  64.7 5.1 %copy-start.1 = (f32[1,4,64,128]{3,2,1,0:T(8,128)S(1)}, f32[1,4,64,128]{3,2,1,0:T(8,128)}, u32[]{:S(2)}) copy-start(f32[1,4,64,128]{3,2,1,0:T(8,128)} %u.1) | copy-start | bytes 393220
  65.4 4.4 %collective-permute-start.8 = (f32[1,4,64,128]{3,2,1,0:T(8,128)S(1)}, f32[1,4,64,128]{3,2,1,0:T(8,128)S(1)}, u32[]{:S(2)}, u32[]{:S(2)}) collective-permute-start(f32[1,4,64,128]{3,2,1,0:T(8,128)S(1)} %shard_map.56), channel_id=1, source_target_pairs={{0,32},{1,33},{2,34},{3,35},{4,36},{5,37},{6,38},{7,39},{8,40},{9,... | collective-permute-start | bytes 393224 | tf_op jit(solution)/shard_map/ppermute | solution.py:530

commit v11 on v10

--- a/solution.py
+++ b/solution.py
@@ -93,11 +93,16 @@
     return pltpu.roll(v[k % 2], (j - 16 * (k // 2)) % 128, 1) if (k // 2 or j) else v[k]
 
 
-CENTRE = [(k, 0) for k in range(2)]
-FIRST = [(k, j) for k in range(2) for j in (-1, 0, 1)] + [(-1, 0), (2, 0)]
-
-
-def coarsest(b3, w3):
+def within(reach):
+    return [
+        (k, j)
+        for k in range(-reach, 2 + reach)
+        for j in range(-reach, reach + 1)
+        if max(0, -k, k - 1) + abs(j) <= reach
+    ]
+
+
+def coarsest(b3, w3, most):
     lane, row = iota((8, 128), 1), iota((8, 128), 0)
     x = lane & 15
     base, own = [], []
@@ -117,7 +122,7 @@
         )
     terms = list(zip(*base))
     steps = {
-        (k, j): (rolled(own, k, j), *(rolled(t, k, j) for t in terms)) for k, j in FIRST
+        (k, j): (rolled(own, k, j), *(rolled(t, k, j) for t in terms)) for k, j in within(most - 1)
     }
 
     def sweep(v, k, j):
@@ -127,26 +132,14 @@
         s = up * pltpu.roll(c, 1, 0) + down * pltpu.roll(c, 7, 0)
         return (t + s) + (left * v[k, j + 1] + right * v[k, j - 1])
 
-    def copies(v, reach):
-        return {
-            (k, j): rolled(v, k, j)
-            for k in range(-reach, 2 + reach)
-            for j in range(-reach, reach + 1)
-            if max(0, -k, k - 1) + abs(j) <= reach
-        }
-
-    def one(v):
-        v = copies(v, 1)
-        return [sweep(v, k, j) for k, j in CENTRE]
-
-    def two(_, v):
-        v = copies(v, 2)
-        v = {(k, j): sweep(v, k, j) for k, j in FIRST}
-        return tuple(sweep(v, k, j) for k, j in CENTRE)
-
-    pairs, rest = divmod(COARSE_SWEEPS - 1, 2)
-    v = one(own) if rest else own
-    v = lax.fori_loop(0, pairs, two, tuple(v), unroll=True)
+    v, remaining = own, COARSE_SWEEPS - 1
+    while remaining:
+        count = min(most, remaining)
+        v = {(k, j): rolled(v, k, j) for k, j in within(count)}
+        for reach in reversed(range(count)):
+            v = {(k, j): sweep(v, k, j) for k, j in within(reach)}
+        v = [v[k, 0] for k in range(2)]
+        remaining -= count
     return jnp.concatenate(v, 0)
 
 
@@ -198,10 +191,12 @@
     ]
     for copy in copies:
         copy.start()
-    for copy in copies:
+    copies[0].wait()
+    for p in range(DEPTH):
+        w[p] = OMEGA / (cap_out[p] + 6.0)
+    for copy in copies[1:]:
         copy.wait()
     for p in range(DEPTH):
-        w[p] = OMEGA / (cap_out[p] + 6.0)
         u_in[p] = cap_out[p] * u_in[p] + src_in[p]
     blocks = local_down(lambda p: u_in[p], cap_out, w, y, x, rs, True)
     block[...] = blocks
@@ -402,7 +397,7 @@
     y = w * b
     x = 1.2 * y + 0.25 * w * around_low(y)
     r = b - d * x + 0.25 * around_low(x)
-    x = x + from_coarsest(coarsest(to_coarsest(r, t3), w3[...]), t3)
+    x = x + from_coarsest(coarsest(to_coarsest(r, t3), w3[...], 2 if first else 3), t3)
     for _ in range(2):
         x = 0.2 * x + y + 0.25 * w * around_low(x)
     x2[...] = x

time: 71.1 us -> 71.1 us (level)
  transfers between devices with their start and end apart: 11 -> 11, of which waited for: 4 -> 5; matrix products, arithmetic and copies ran while one was open for 0% -> 0% of each run, Pallas kernels for 6% -> 6%
where the time goes in v11:
time: 71.1 us; the launch traced here: 70.4 us
  starting transfers between devices  37.4 us (53%)
  waiting for transfers between devices  22 us (31%)
  Pallas kernels  9.59 us (13%)
  between operations  0.74 us (1%)
    ppermute x9, starting transfers between devices, moved(): return lax.ppermute(x, ('tm', 'space'), pairs)  25.3 us
    ppermute x9, waiting for transfers between devices, moved(): return lax.ppermute(x, ('tm', 'space'), pairs)  14.9 us
    all_to_all x2, starting transfers between devices, gathered(): return lax.all_to_all(send, 'space', 0, 0, tiled=True)  12.1 us
    pallas_call x7, Pallas kernels, call(): pl.pallas_call(body, out_shape=outs, in_specs=[space] * len(args), out_sp...  9.59 us
    all_to_all x2, waiting for transfers between devices, gathered(): return lax.all_to_all(send, 'space', 0, 0, tiled=True)  7.05 us
  transfers between devices with their start and end apart: 11, of which 5 were waited for; matrix products, arithmetic and copies ran while one was open for 0% of the time, Pallas kernels for 6%

profile of v11, /device:TPU:4, one launch (start us, length us, event | category | flops | bytes accessed | tf_op | source)
XLA Modules:
  0.0 70.4 jit_solution(13829711302349708823)
XLA Ops:
  0.6 1.5 %shard_map.50 = (f32[4,64,128]{2,1,0:T(8,128)S(1)}, f32[4,64,128]{2,1,0:T(8,128)S(1)}, f32[4,64,128]{2,1,0:T(8,128)S(1)}, f32[64,128]{1,0:T(8,128)S(1)}, f32[288...) custom-call(f32[1,4,64,128]{3,2,1,0:T(8,128)} %u.1, f32[1,2,4,64,128]{4,3,2,1,0:T(8,128)} %src.3, ...), custom_call_target="tpu_custom_call" | custom-call | tf_op jit(solution)/shard_map/pallas_call | solution.py:24
  2.1 1.7 %collective-permute-start = (f32[288,128]{1,0:T(8,128)S(1)}, f32[288,128]{1,0:T(8,128)S(1)}, u32[]{:S(2)}, u32[]{:S(2)}) collective-permute-start(f32[288,128]{1,0:T(8,128)S(1)} %get-tuple-element.33), channel_id=1, source_target_pairs={{0,1},{1,2},{2,3},{3,4},{4,5},{5,6},{6,7},{7,8},{8,9},{9,10},{10,1... | collective-permute-start | bytes 442376 | tf_op jit(solution)/shard_map/ppermute | solution.py:525
  3.7 6.8 %collective-permute-start.1 = (f32[288,128]{1,0:T(8,128)S(1)}, f32[288,128]{1,0:T(8,128)S(1)}, u32[]{:S(2)}, u32[]{:S(2)}) collective-permute-start(f32[288,128]{1,0:T(8,128)S(1)} %get-tuple-element.34), channel_id=1, source_target_pairs={{0,31},{1,0},{2,1},{3,2},{4,3},{5,4},{6,5},{7,6},{8,7},{9,8},{10,9... | collective-permute-start | bytes 442376 | tf_op jit(solution)/shard_map/ppermute | solution.py:525
  10.6 3.8 %collective-permute-done.lo = f32[288,128]{1,0:T(8,128)S(1)} collective-permute-done((f32[288,128]{1,0:T(8,128)S(1)}, f32[288,128]{1,0:T(8,128)S(1)}, u32[]{:S(2)}, u32[]{:S(2)}) %collective-permute-start) | collective-permute-done | bytes 147488 | tf_op jit(solution)/shard_map/ppermute | solution.py:525
  14.3 1.2 %shard_map.51 = (f32[6,64,128]{2,1,0:T(8,128)S(1)}, f32[6,64,128]{2,1,0:T(8,128)S(1)}, f32[8,64,128]{2,1,0:T(8,128)S(1)}, f32[128,128]{1,0:T(8,128)S(1)}, f32[32,16,128]{2,1,0:T(8,128)}) custom-call(f32[4,64,128]{2,1,0:T(8,128)S(1)} %get-tuple-element.29.w, f32[4,64,128]{2,1,0:T(8,128)S(1)} %get-tuple-element.30.y, f32[4,64,128]{2,1,0:T(8,128)S(1)} %get-tuple-element.31.x, ...), custom_call_target="tpu_custom_call" | custom-call | tf_op jit(solution)/shard_map/pallas_call | solution.py:24
  15.6 8.0 %all-to-all-start = ((f32[32,16,128]{2,1,0:T(8,128)}), f32[32,16,128]{2,1,0:T(8,128)S(1)}, u32[]{:S(2)}, u32[]{:S(2)}) async-start(f32[32,16,128]{2,1,0:T(8,128)} %get-tuple-element.35), calls=%async_computation | async-start | bytes 524288 | tf_op jit(solution)/shard_map/all_to_all | solution.py:529
  23.6 3.4 %collective-permute-start.2 = (f32[128,128]{1,0:T(8,128)S(1)}, f32[128,128]{1,0:T(8,128)S(1)}, u32[]{:S(2)}, u32[]{:S(2)}) collective-permute-start(f32[128,128]{1,0:T(8,128)S(1)} %get-tuple-element.37.pair), channel_id=1, source_target_pairs={{0,2},{1,3},{2,4},{3,5},{4,6},{5,7},{6,8},{7,9},{8,10},{9,11},{10,... | collective-permute-start | bytes 196616 | tf_op jit(solution)/shard_map/ppermute | solution.py:525
  27.0 2.3 %collective-permute-start.3 = (f32[128,128]{1,0:T(8,128)S(1)}, f32[128,128]{1,0:T(8,128)S(1)}, u32[]{:S(2)}, u32[]{:S(2)}) collective-permute-start(f32[128,128]{1,0:T(8,128)S(1)} %get-tuple-element.37.pair), channel_id=1, source_target_pairs={{0,30},{1,31},{2,0},{3,1},{4,2},{5,3},{6,4},{7,5},{8,6},{9,7},{10,... | collective-permute-start | bytes 196616 | tf_op jit(solution)/shard_map/ppermute | solution.py:525
  29.3 7.0 %all-to-all-done.got = f32[32,16,128]{2,1,0:T(8,128)S(1)} async-done(((f32[32,16,128]{2,1,0:T(8,128)}), f32[32,16,128]{2,1,0:T(8,128)S(1)}, u32[]{:S(2)}, u32[]{:S(2)}) %all-to-all-start) | async-done | bytes 262176 | tf_op jit(solution)/shard_map/all_to_all | solution.py:529
  36.3 2.0 %shard_map.52 = (f32[128,128]{1,0:T(8,128)S(1)}, f32[128,128]{1,0:T(8,128)S(1)}, f32[16,128]{1,0:T(8,128)S(1)}, f32[128,128]{1,0:T(8,128)S(1)}) custom-call(f32[32,16,128]{2,1,0:T(8,128)S(1)} %all-to-all-done.got), custom_call_target="tpu_custom_call" | custom-call | flops 2147483648 | tf_op jit(solution)/shard_map/pallas_call | solution.py:24
  38.4 2.1 %shard_map.53 = (f32[1,4,64,128]{3,2,1,0:T(8,128)}, f32[4,64,128]{2,1,0:T(8,128)S(1)}, f32[4,64,128]{2,1,0:T(8,128)S(1)}, f32[32,128]{1,0:T(8,128)S(1)}, f32[224...) custom-call(f32[128,128]{1,0:T(8,128)S(1)} %get-tuple-element.36.x2, ...), custom_call_target="tpu_custom_call" | custom-call | tf_op jit(solution)/shard_map/pallas_call | solution.py:24
  40.5 4.1 %all-to-all-start.1 = ((f32[160,4,128]{2,1,0:T(4,128)}), f32[160,4,128]{2,1,0:T(4,128)S(1)}, u32[]{:S(2)}, u32[]{:S(2)}) async-start(f32[160,4,128]{2,1,0:T(4,128)} %get-tuple-element.43), calls=%async_computation.1 | async-start | bytes 655360 | tf_op jit(solution)/shard_map/all_to_all | solution.py:529
  44.6 1.9 %collective-permute-start.4 = (f32[224,128]{1,0:T(8,128)S(1)}, f32[224,128]{1,0:T(8,128)S(1)}, u32[]{:S(2)}, u32[]{:S(2)}) collective-permute-start(f32[224,128]{1,0:T(8,128)S(1)} %get-tuple-element.50), channel_id=1, source_target_pairs={{0,1},{1,2},{2,3},{3,4},{4,5},{5,6},{6,7},{7,8},{8,9},{9,10},{10,1... | collective-permute-start | bytes 344072 | tf_op jit(solution)/shard_map/ppermute | solution.py:525
  46.5 3.6 %collective-permute-start.5 = (f32[224,128]{1,0:T(8,128)S(1)}, f32[224,128]{1,0:T(8,128)S(1)}, u32[]{:S(2)}, u32[]{:S(2)}) collective-permute-start(f32[224,128]{1,0:T(8,128)S(1)} %get-tuple-element.51), channel_id=1, source_target_pairs={{0,31},{1,0},{2,1},{3,2},{4,3},{5,4},{6,5},{7,6},{8,7},{9,8},{10,9... | collective-permute-start | bytes 344072 | tf_op jit(solution)/shard_map/ppermute | solution.py:525
  50.0 6.7 %collective-permute-done.4.lo = f32[224,128]{1,0:T(8,128)S(1)} collective-permute-done((f32[224,128]{1,0:T(8,128)S(1)}, f32[224,128]{1,0:T(8,128)S(1)}, u32[]{:S(2)}, u32[]{:S(2)}) %collective-permute-start.4) | collective-permute-done | bytes 114720 | tf_op jit(solution)/shard_map/ppermute | solution.py:525
  56.8 0.3 shard_map.54
  57.0 0.1 collective-permute-start.6
  57.1 5.6 %collective-permute-start.7 = (f32[64,128]{1,0:T(8,128)S(1)}, f32[64,128]{1,0:T(8,128)S(1)}, u32[]{:S(2)}, u32[]{:S(2)}) collective-permute-start(f32[64,128]{1,0:T(8,128)S(1)} %get-tuple-element.52.after.pair), channel_id=1, source_target_pairs={{0,30},{1,31},{2,0},{3,1},{4,2},{5,3},{6,4},{7,5},{8,6},{9,7},{10,... | collective-permute-start | bytes 98312 | tf_op jit(solution)/shard_map/ppermute | solution.py:525
  62.8 1.8 %shard_map.55.x2 = f32[128,128]{1,0:T(8,128)S(1)} custom-call(f32[160,4,128]{2,1,0:T(4,128)S(1)} %all-to-all-done.1.got, f32[128,128]{1,0:T(8,128)S(1)} %get-tuple-element.44.w2, f32[128,128]{1,0:T(8,128)S(1)} %get-tuple-element.45.d2, f32[16,128]{1,0:T(8,128)S(1)} %get-tuple-element.46.w3, f32[64,128]{1,0:T(8,128)S(1)} %get-tuple-element.52.after.pair), custom_call_target="tpu_custom_call" | custom-call | flops 2147483648 | tf_op jit(solution)/shard_map/pallas_call | solution.py:24
  64.6 0.1 collective-permute-done.6.lo2
  64.7 0.7 shard_map.56
  65.3 0.0 collective-permute-start.8
  65.4 4.4 %collective-permute-done.8 = f32[1,4,64,128]{3,2,1,0:T(8,128)S(1)} collective-permute-done((f32[1,4,64,128]{3,2,1,0:T(8,128)S(1)}, f32[1,4,64,128]{3,2,1,0:T(8,128)S(1)}, u32[]{:S(2)}, u32[]{:S(2)}) %collective-permute-start.8) | collective-permute-done | bytes 131104 | tf_op jit(solution)/shard_map/ppermute | solution.py:525
  69.7 0.7 broadcast_select_fusion
  (10 shorter events, 0.0 us)
Async XLA Ops:
  2.1 12.2 %collective-permute-start = (f32[288,128]{1,0:T(8,128)S(1)}, f32[288,128]{1,0:T(8,128)S(1)}, u32[]{:S(2)}, u32[]{:S(2)}) collective-permute-start(f32[288,128]{1,0:T(8,128)S(1)} %get-tuple-element.33), channel_id=1, source_target_pairs={{0,1},{1,2},{2,3},{3,4},{4,5},{5,6},{6,7},{7,8},{8,9},{9,10},{10,1... | collective-permute-start | bytes 442376 | tf_op jit(solution)/shard_map/ppermute | solution.py:525
  3.7 10.6 %collective-permute-start.1 = (f32[288,128]{1,0:T(8,128)S(1)}, f32[288,128]{1,0:T(8,128)S(1)}, u32[]{:S(2)}, u32[]{:S(2)}) collective-permute-start(f32[288,128]{1,0:T(8,128)S(1)} %get-tuple-element.34), channel_id=1, source_target_pairs={{0,31},{1,0},{2,1},{3,2},{4,3},{5,4},{6,5},{7,6},{8,7},{9,8},{10,9... | collective-permute-start | bytes 442376 | tf_op jit(solution)/shard_map/ppermute | solution.py:525
  15.6 20.8 %all-to-all-start = ((f32[32,16,128]{2,1,0:T(8,128)}), f32[32,16,128]{2,1,0:T(8,128)S(1)}, u32[]{:S(2)}, u32[]{:S(2)}) async-start(f32[32,16,128]{2,1,0:T(8,128)} %get-tuple-element.35), calls=%async_computation | async-start | bytes 524288 | tf_op jit(solution)/shard_map/all_to_all | solution.py:529
  23.6 14.8 %copy-start = (f32[1,2,4,64,128]{4,3,2,1,0:T(8,128)S(1)}, f32[1,2,4,64,128]{4,3,2,1,0:T(8,128)}, u32[]{:S(2)}) copy-start(f32[1,2,4,64,128]{4,3,2,1,0:T(8,128)} %src.3) | copy-start | bytes 786436
  23.6 14.8 %collective-permute-start.2 = (f32[128,128]{1,0:T(8,128)S(1)}, f32[128,128]{1,0:T(8,128)S(1)}, u32[]{:S(2)}, u32[]{:S(2)}) collective-permute-start(f32[128,128]{1,0:T(8,128)S(1)} %get-tuple-element.37.pair), channel_id=1, source_target_pairs={{0,2},{1,3},{2,4},{3,5},{4,6},{5,7},{6,8},{7,9},{8,10},{9,11},{10,... | collective-permute-start | bytes 196616 | tf_op jit(solution)/shard_map/ppermute | solution.py:525
  27.0 11.4 %collective-permute-start.3 = (f32[128,128]{1,0:T(8,128)S(1)}, f32[128,128]{1,0:T(8,128)S(1)}, u32[]{:S(2)}, u32[]{:S(2)}) collective-permute-start(f32[128,128]{1,0:T(8,128)S(1)} %get-tuple-element.37.pair), channel_id=1, source_target_pairs={{0,30},{1,31},{2,0},{3,1},{4,2},{5,3},{6,4},{7,5},{8,6},{9,7},{10,... | collective-permute-start | bytes 196616 | tf_op jit(solution)/shard_map/ppermute | solution.py:525
  40.5 22.2 %all-to-all-start.1 = ((f32[160,4,128]{2,1,0:T(4,128)}), f32[160,4,128]{2,1,0:T(4,128)S(1)}, u32[]{:S(2)}, u32[]{:S(2)}) async-start(f32[160,4,128]{2,1,0:T(4,128)} %get-tuple-element.43), calls=%async_computation.1 | async-start | bytes 655360 | tf_op jit(solution)/shard_map/all_to_all | solution.py:529
  44.6 12.2 %collective-permute-start.4 = (f32[224,128]{1,0:T(8,128)S(1)}, f32[224,128]{1,0:T(8,128)S(1)}, u32[]{:S(2)}, u32[]{:S(2)}) collective-permute-start(f32[224,128]{1,0:T(8,128)S(1)} %get-tuple-element.50), channel_id=1, source_target_pairs={{0,1},{1,2},{2,3},{3,4},{4,5},{5,6},{6,7},{7,8},{8,9},{9,10},{10,1... | collective-permute-start | bytes 344072 | tf_op jit(solution)/shard_map/ppermute | solution.py:525
  46.5 10.3 %collective-permute-start.5 = (f32[224,128]{1,0:T(8,128)S(1)}, f32[224,128]{1,0:T(8,128)S(1)}, u32[]{:S(2)}, u32[]{:S(2)}) collective-permute-start(f32[224,128]{1,0:T(8,128)S(1)} %get-tuple-element.51), channel_id=1, source_target_pairs={{0,31},{1,0},{2,1},{3,2},{4,3},{5,4},{6,5},{7,6},{8,7},{9,8},{10,9... | collective-permute-start | bytes 344072 | tf_op jit(solution)/shard_map/ppermute | solution.py:525
  57.0 7.6 %collective-permute-start.6 = (f32[64,128]{1,0:T(8,128)S(1)}, f32[64,128]{1,0:T(8,128)S(1)}, u32[]{:S(2)}, u32[]{:S(2)}) collective-permute-start(f32[64,128]{1,0:T(8,128)S(1)} %get-tuple-element.52.after.pair), channel_id=1, source_target_pairs={{0,2},{1,3},{2,4},{3,5},{4,6},{5,7},{6,8},{7,9},{8,10},{9,11},{10,... | collective-permute-start | bytes 98312 | tf_op jit(solution)/shard_map/ppermute | solution.py:525
  57.1 7.5 %collective-permute-start.7 = (f32[64,128]{1,0:T(8,128)S(1)}, f32[64,128]{1,0:T(8,128)S(1)}, u32[]{:S(2)}, u32[]{:S(2)}) collective-permute-start(f32[64,128]{1,0:T(8,128)S(1)} %get-tuple-element.52.after.pair), channel_id=1, source_target_pairs={{0,30},{1,31},{2,0},{3,1},{4,2},{5,3},{6,4},{7,5},{8,6},{9,7},{10,... | collective-permute-start | bytes 98312 | tf_op jit(solution)/shard_map/ppermute | solution.py:525
  64.7 5.1 %copy-start.1 = (f32[1,4,64,128]{3,2,1,0:T(8,128)S(1)}, f32[1,4,64,128]{3,2,1,0:T(8,128)}, u32[]{:S(2)}) copy-start(f32[1,4,64,128]{3,2,1,0:T(8,128)} %u.1) | copy-start | bytes 393220
  65.3 4.4 %collective-permute-start.8 = (f32[1,4,64,128]{3,2,1,0:T(8,128)S(1)}, f32[1,4,64,128]{3,2,1,0:T(8,128)S(1)}, u32[]{:S(2)}, u32[]{:S(2)}) collective-permute-start(f32[1,4,64,128]{3,2,1,0:T(8,128)S(1)} %shard_map.56), channel_id=1, source_target_pairs={{0,32},{1,33},{2,34},{3,35},{4,36},{5,37},{6,38},{7,39},{8,40},{9,... | collective-permute-start | bytes 393224 | tf_op jit(solution)/shard_map/ppermute | solution.py:525

commit v12 on v11

--- a/solution.py
+++ b/solution.py
@@ -296,7 +296,8 @@
     finish_down(False, w, y, x, block[...], None, lo, hi, wx, yx, xs, pair, rs)
 
 
-def wide_share(block, y, x, wx, w1, c1, send, rs):
+def wide_share_body(own, y, x, wx, w1, c1, send, rs):
+    block = own[...]
     lane = iota((32, 128), 1)
     zero = jnp.zeros((32, 128), F32)
     for k, (i, p) in enumerate(((0, 0), (5, 3))):
@@ -475,9 +476,9 @@
 
 
 def first_up_body(
-    x2, lo2, pair, hi2, wx, yx, xs, w, cap, src, u_out, y, x, block, up, dn, w1, send, *work
+    x2, lo2, pair, hi2, wx, yx, xs, w, cap, src, u_out, y, x, block, up, dn, w1, c1, *work
 ):
-    b_out, c1, rs, *work = work
+    b_out, rs, *work = work
 
     def out(p, u):
         u_out[0, p] = u
@@ -485,7 +486,6 @@
 
     fine_up(x2, lo2, pair, hi2, c1, wx, yx, xs, w1, work, out)
     own = local_down(lambda p: b_out[p], cap, w, y, x, rs, False)
-    wide_share(own, y, x, wx, w1, c1, send, rs)
     block[...] = own
     fill_edges(up, dn, y, x)
     up[pl.ds(192, 32), :] = own
@@ -565,7 +565,7 @@
         got,
         flops=LOW_FLOPS,
     )
-    fpoint, y, x, block, up, dn, w1, send = call(
+    fpoint, y, x, block, up, dn, w1, c1 = call(
         first_up_body,
         (
             f32(1, *PLANE4),
@@ -575,11 +575,12 @@
             f32(224, 128),
             f32(224, 128),
             f32(5, 32, 128),
-            WIDE_MESSAGE,
+            f32(5, 32, 128),
         ),
-        [PLANE4, (5, 32, 128), EDGE_SUMS, *WORK],
+        [PLANE4, EDGE_SUMS, *WORK],
         *(x2, *near(pair), wx, yx, xs, w, cap_in, src),
     )
+    (send,) = call(wide_share_body, (WIDE_MESSAGE,), [EDGE_SUMS], *(block, y, x, wx, w1, c1))
     got = gathered(send)
     lo, hi = both(up, dn, 1)
     yx, xs, pair = call(

time: 71.1 us -> 71.8 us (level)
    pallas_call x7 -> x8, Pallas kernels: 9.59 us -> 10.3 us  [call(): pl.pallas_call(body, out_shape=outs, in_specs=[space] * len(args), out_sp...]
where the time goes in v12:
time: 71.8 us; the launch traced here: 71.1 us
  starting transfers between devices  37.4 us (52%)
  waiting for transfers between devices  22 us (31%)
  Pallas kernels  10.3 us (14%)
  between operations  0.74 us (1%)
    ppermute x9, starting transfers between devices, moved(): return lax.ppermute(x, ('tm', 'space'), pairs)  25.3 us
    ppermute x9, waiting for transfers between devices, moved(): return lax.ppermute(x, ('tm', 'space'), pairs)  14.9 us
    all_to_all x2, starting transfers between devices, gathered(): return lax.all_to_all(send, 'space', 0, 0, tiled=True)  12.1 us
    pallas_call x8, Pallas kernels, call(): pl.pallas_call(body, out_shape=outs, in_specs=[space] * len(args), out_sp...  10.3 us
    all_to_all x2, waiting for transfers between devices, gathered(): return lax.all_to_all(send, 'space', 0, 0, tiled=True)  7.05 us
  transfers between devices with their start and end apart: 11, of which 5 were waited for; matrix products, arithmetic and copies ran while one was open for 0% of the time, Pallas kernels for 6%

profile of v12, /device:TPU:4, one launch (start us, length us, event | category | flops | bytes accessed | tf_op | source)
XLA Modules:
  0.0 71.1 jit_solution(2039195592574485552)
XLA Ops:
  0.6 1.5 %shard_map.50 = (f32[4,64,128]{2,1,0:T(8,128)S(1)}, f32[4,64,128]{2,1,0:T(8,128)S(1)}, f32[4,64,128]{2,1,0:T(8,128)S(1)}, f32[64,128]{1,0:T(8,128)S(1)}, f32[288...) custom-call(f32[1,4,64,128]{3,2,1,0:T(8,128)} %u.1, f32[1,2,4,64,128]{4,3,2,1,0:T(8,128)} %src.3, ...), custom_call_target="tpu_custom_call" | custom-call | tf_op jit(solution)/shard_map/pallas_call | solution.py:24
  2.1 1.7 %collective-permute-start = (f32[288,128]{1,0:T(8,128)S(1)}, f32[288,128]{1,0:T(8,128)S(1)}, u32[]{:S(2)}, u32[]{:S(2)}) collective-permute-start(f32[288,128]{1,0:T(8,128)S(1)} %get-tuple-element.33), channel_id=1, source_target_pairs={{0,1},{1,2},{2,3},{3,4},{4,5},{5,6},{6,7},{7,8},{8,9},{9,10},{10,1... | collective-permute-start | bytes 442376 | tf_op jit(solution)/shard_map/ppermute | solution.py:525
  3.7 6.8 %collective-permute-start.1 = (f32[288,128]{1,0:T(8,128)S(1)}, f32[288,128]{1,0:T(8,128)S(1)}, u32[]{:S(2)}, u32[]{:S(2)}) collective-permute-start(f32[288,128]{1,0:T(8,128)S(1)} %get-tuple-element.34), channel_id=1, source_target_pairs={{0,31},{1,0},{2,1},{3,2},{4,3},{5,4},{6,5},{7,6},{8,7},{9,8},{10,9... | collective-permute-start | bytes 442376 | tf_op jit(solution)/shard_map/ppermute | solution.py:525
  10.6 3.8 %collective-permute-done.lo = f32[288,128]{1,0:T(8,128)S(1)} collective-permute-done((f32[288,128]{1,0:T(8,128)S(1)}, f32[288,128]{1,0:T(8,128)S(1)}, u32[]{:S(2)}, u32[]{:S(2)}) %collective-permute-start) | collective-permute-done | bytes 147488 | tf_op jit(solution)/shard_map/ppermute | solution.py:525
  14.3 1.2 %shard_map.51 = (f32[6,64,128]{2,1,0:T(8,128)S(1)}, f32[6,64,128]{2,1,0:T(8,128)S(1)}, f32[8,64,128]{2,1,0:T(8,128)S(1)}, f32[128,128]{1,0:T(8,128)S(1)}, f32[32,16,128]{2,1,0:T(8,128)}) custom-call(f32[4,64,128]{2,1,0:T(8,128)S(1)} %get-tuple-element.29.w, f32[4,64,128]{2,1,0:T(8,128)S(1)} %get-tuple-element.30.y, f32[4,64,128]{2,1,0:T(8,128)S(1)} %get-tuple-element.31.x, ...), custom_call_target="tpu_custom_call" | custom-call | tf_op jit(solution)/shard_map/pallas_call | solution.py:24
  15.6 8.0 %all-to-all-start = ((f32[32,16,128]{2,1,0:T(8,128)}), f32[32,16,128]{2,1,0:T(8,128)S(1)}, u32[]{:S(2)}, u32[]{:S(2)}) async-start(f32[32,16,128]{2,1,0:T(8,128)} %get-tuple-element.35), calls=%async_computation | async-start | bytes 524288 | tf_op jit(solution)/shard_map/all_to_all | solution.py:529
  23.6 3.4 %collective-permute-start.2 = (f32[128,128]{1,0:T(8,128)S(1)}, f32[128,128]{1,0:T(8,128)S(1)}, u32[]{:S(2)}, u32[]{:S(2)}) collective-permute-start(f32[128,128]{1,0:T(8,128)S(1)} %get-tuple-element.37.pair), channel_id=1, source_target_pairs={{0,2},{1,3},{2,4},{3,5},{4,6},{5,7},{6,8},{7,9},{8,10},{9,11},{10,... | collective-permute-start | bytes 196616 | tf_op jit(solution)/shard_map/ppermute | solution.py:525
  27.0 2.3 %collective-permute-start.3 = (f32[128,128]{1,0:T(8,128)S(1)}, f32[128,128]{1,0:T(8,128)S(1)}, u32[]{:S(2)}, u32[]{:S(2)}) collective-permute-start(f32[128,128]{1,0:T(8,128)S(1)} %get-tuple-element.37.pair), channel_id=1, source_target_pairs={{0,30},{1,31},{2,0},{3,1},{4,2},{5,3},{6,4},{7,5},{8,6},{9,7},{10,... | collective-permute-start | bytes 196616 | tf_op jit(solution)/shard_map/ppermute | solution.py:525
  29.3 7.0 %all-to-all-done.got = f32[32,16,128]{2,1,0:T(8,128)S(1)} async-done(((f32[32,16,128]{2,1,0:T(8,128)}), f32[32,16,128]{2,1,0:T(8,128)S(1)}, u32[]{:S(2)}, u32[]{:S(2)}) %all-to-all-start) | async-done | bytes 262176 | tf_op jit(solution)/shard_map/all_to_all | solution.py:529
  36.3 2.0 %shard_map.52 = (f32[128,128]{1,0:T(8,128)S(1)}, f32[128,128]{1,0:T(8,128)S(1)}, f32[16,128]{1,0:T(8,128)S(1)}, f32[128,128]{1,0:T(8,128)S(1)}) custom-call(f32[32,16,128]{2,1,0:T(8,128)S(1)} %all-to-all-done.got), custom_call_target="tpu_custom_call" | custom-call | flops 2147483648 | tf_op jit(solution)/shard_map/pallas_call | solution.py:24
  38.4 1.5 %shard_map.53 = (f32[1,4,64,128]{3,2,1,0:T(8,128)}, f32[4,64,128]{2,1,0:T(8,128)S(1)}, f32[4,64,128]{2,1,0:T(8,128)S(1)}, f32[32,128]{1,0:T(8,128)S(1)}, f32[224...) custom-call(f32[128,128]{1,0:T(8,128)S(1)} %get-tuple-element.36.x2, ...), custom_call_target="tpu_custom_call" | custom-call | tf_op jit(solution)/shard_map/pallas_call | solution.py:24
  39.9 1.3 %shard_map.54 = f32[160,4,128]{2,1,0:T(4,128)} custom-call(f32[32,128]{1,0:T(8,128)S(1)} %get-tuple-element.43.own.block, f32[4,64,128]{2,1,0:T(8,128)S(1)} %get-tuple-element.44.y, f32[4,64,128]{2,1,0:T(8,128)S(1)} %get-tuple-element.45.x, f32[6,64,128]{2,1,0:T(8,128)S(1)} %get-tuple-element.38.wx, f32[5,32,128]{2,1,0:T(8,128)S(1)} %get-tuple-element.46.w1, ...), custom_call_target="tpu_custom_call" | custom-call | tf_op jit(solution)/shard_map/pallas_call | solution.py:24
  41.2 4.1 %all-to-all-start.1 = ((f32[160,4,128]{2,1,0:T(4,128)}), f32[160,4,128]{2,1,0:T(4,128)S(1)}, u32[]{:S(2)}, u32[]{:S(2)}) async-start(f32[160,4,128]{2,1,0:T(4,128)} %shard_map.54), calls=%async_computation.1 | async-start | bytes 655360 | tf_op jit(solution)/shard_map/all_to_all | solution.py:529
  45.3 1.9 %collective-permute-start.4 = (f32[224,128]{1,0:T(8,128)S(1)}, f32[224,128]{1,0:T(8,128)S(1)}, u32[]{:S(2)}, u32[]{:S(2)}) collective-permute-start(f32[224,128]{1,0:T(8,128)S(1)} %get-tuple-element.51), channel_id=1, source_target_pairs={{0,1},{1,2},{2,3},{3,4},{4,5},{5,6},{6,7},{7,8},{8,9},{9,10},{10,1... | collective-permute-start | bytes 344072 | tf_op jit(solution)/shard_map/ppermute | solution.py:525
  47.1 3.6 %collective-permute-start.5 = (f32[224,128]{1,0:T(8,128)S(1)}, f32[224,128]{1,0:T(8,128)S(1)}, u32[]{:S(2)}, u32[]{:S(2)}) collective-permute-start(f32[224,128]{1,0:T(8,128)S(1)} %get-tuple-element.52), channel_id=1, source_target_pairs={{0,31},{1,0},{2,1},{3,2},{4,3},{5,4},{6,5},{7,6},{8,7},{9,8},{10,9... | collective-permute-start | bytes 344072 | tf_op jit(solution)/shard_map/ppermute | solution.py:525
  50.7 6.7 %collective-permute-done.4.lo = f32[224,128]{1,0:T(8,128)S(1)} collective-permute-done((f32[224,128]{1,0:T(8,128)S(1)}, f32[224,128]{1,0:T(8,128)S(1)}, u32[]{:S(2)}, u32[]{:S(2)}) %collective-permute-start.4) | collective-permute-done | bytes 114720 | tf_op jit(solution)/shard_map/ppermute | solution.py:525
  57.4 0.3 shard_map.55
  57.7 0.1 collective-permute-start.6
  57.8 5.6 %collective-permute-start.7 = (f32[64,128]{1,0:T(8,128)S(1)}, f32[64,128]{1,0:T(8,128)S(1)}, u32[]{:S(2)}, u32[]{:S(2)}) collective-permute-start(f32[64,128]{1,0:T(8,128)S(1)} %get-tuple-element.53.after.pair), channel_id=1, source_target_pairs={{0,30},{1,31},{2,0},{3,1},{4,2},{5,3},{6,4},{7,5},{8,6},{9,7},{10,... | collective-permute-start | bytes 98312 | tf_op jit(solution)/shard_map/ppermute | solution.py:525
  63.4 1.8 %shard_map.56.x2 = f32[128,128]{1,0:T(8,128)S(1)} custom-call(f32[160,4,128]{2,1,0:T(4,128)S(1)} %all-to-all-done.1.got, f32[128,128]{1,0:T(8,128)S(1)} %get-tuple-element.48.w2, f32[128,128]{1,0:T(8,128)S(1)} %get-tuple-element.49.d2, f32[16,128]{1,0:T(8,128)S(1)} %get-tuple-element.50.w3, f32[64,128]{1,0:T(8,128)S(1)} %get-tuple-element.53.after.pair), custom_call_target="tpu_custom_call" | custom-call | flops 2147483648 | tf_op jit(solution)/shard_map/pallas_call | solution.py:24
  65.3 0.1 collective-permute-done.6.lo2
  65.3 0.7 shard_map.57
  66.0 4.4 %collective-permute-done.8 = f32[1,4,64,128]{3,2,1,0:T(8,128)S(1)} collective-permute-done((f32[1,4,64,128]{3,2,1,0:T(8,128)S(1)}, f32[1,4,64,128]{3,2,1,0:T(8,128)S(1)}, u32[]{:S(2)}, u32[]{:S(2)}) %collective-permute-start.8) | collective-permute-done | bytes 131104 | tf_op jit(solution)/shard_map/ppermute | solution.py:525
  70.4 0.7 broadcast_select_fusion
  (11 shorter events, 0.0 us)
Async XLA Ops:
  2.1 12.2 %collective-permute-start = (f32[288,128]{1,0:T(8,128)S(1)}, f32[288,128]{1,0:T(8,128)S(1)}, u32[]{:S(2)}, u32[]{:S(2)}) collective-permute-start(f32[288,128]{1,0:T(8,128)S(1)} %get-tuple-element.33), channel_id=1, source_target_pairs={{0,1},{1,2},{2,3},{3,4},{4,5},{5,6},{6,7},{7,8},{8,9},{9,10},{10,1... | collective-permute-start | bytes 442376 | tf_op jit(solution)/shard_map/ppermute | solution.py:525
  3.7 10.6 %collective-permute-start.1 = (f32[288,128]{1,0:T(8,128)S(1)}, f32[288,128]{1,0:T(8,128)S(1)}, u32[]{:S(2)}, u32[]{:S(2)}) collective-permute-start(f32[288,128]{1,0:T(8,128)S(1)} %get-tuple-element.34), channel_id=1, source_target_pairs={{0,31},{1,0},{2,1},{3,2},{4,3},{5,4},{6,5},{7,6},{8,7},{9,8},{10,9... | collective-permute-start | bytes 442376 | tf_op jit(solution)/shard_map/ppermute | solution.py:525
  15.6 20.8 %all-to-all-start = ((f32[32,16,128]{2,1,0:T(8,128)}), f32[32,16,128]{2,1,0:T(8,128)S(1)}, u32[]{:S(2)}, u32[]{:S(2)}) async-start(f32[32,16,128]{2,1,0:T(8,128)} %get-tuple-element.35), calls=%async_computation | async-start | bytes 524288 | tf_op jit(solution)/shard_map/all_to_all | solution.py:529
  23.6 14.8 %copy-start = (f32[1,2,4,64,128]{4,3,2,1,0:T(8,128)S(1)}, f32[1,2,4,64,128]{4,3,2,1,0:T(8,128)}, u32[]{:S(2)}) copy-start(f32[1,2,4,64,128]{4,3,2,1,0:T(8,128)} %src.3) | copy-start | bytes 786436
  23.6 14.8 %collective-permute-start.2 = (f32[128,128]{1,0:T(8,128)S(1)}, f32[128,128]{1,0:T(8,128)S(1)}, u32[]{:S(2)}, u32[]{:S(2)}) collective-permute-start(f32[128,128]{1,0:T(8,128)S(1)} %get-tuple-element.37.pair), channel_id=1, source_target_pairs={{0,2},{1,3},{2,4},{3,5},{4,6},{5,7},{6,8},{7,9},{8,10},{9,11},{10,... | collective-permute-start | bytes 196616 | tf_op jit(solution)/shard_map/ppermute | solution.py:525
  27.0 11.4 %collective-permute-start.3 = (f32[128,128]{1,0:T(8,128)S(1)}, f32[128,128]{1,0:T(8,128)S(1)}, u32[]{:S(2)}, u32[]{:S(2)}) collective-permute-start(f32[128,128]{1,0:T(8,128)S(1)} %get-tuple-element.37.pair), channel_id=1, source_target_pairs={{0,30},{1,31},{2,0},{3,1},{4,2},{5,3},{6,4},{7,5},{8,6},{9,7},{10,... | collective-permute-start | bytes 196616 | tf_op jit(solution)/shard_map/ppermute | solution.py:525
  41.2 22.2 %all-to-all-start.1 = ((f32[160,4,128]{2,1,0:T(4,128)}), f32[160,4,128]{2,1,0:T(4,128)S(1)}, u32[]{:S(2)}, u32[]{:S(2)}) async-start(f32[160,4,128]{2,1,0:T(4,128)} %shard_map.54), calls=%async_computation.1 | async-start | bytes 655360 | tf_op jit(solution)/shard_map/all_to_all | solution.py:529
  45.3 12.2 %collective-permute-start.4 = (f32[224,128]{1,0:T(8,128)S(1)}, f32[224,128]{1,0:T(8,128)S(1)}, u32[]{:S(2)}, u32[]{:S(2)}) collective-permute-start(f32[224,128]{1,0:T(8,128)S(1)} %get-tuple-element.51), channel_id=1, source_target_pairs={{0,1},{1,2},{2,3},{3,4},{4,5},{5,6},{6,7},{7,8},{8,9},{9,10},{10,1... | collective-permute-start | bytes 344072 | tf_op jit(solution)/shard_map/ppermute | solution.py:525
  47.1 10.3 %collective-permute-start.5 = (f32[224,128]{1,0:T(8,128)S(1)}, f32[224,128]{1,0:T(8,128)S(1)}, u32[]{:S(2)}, u32[]{:S(2)}) collective-permute-start(f32[224,128]{1,0:T(8,128)S(1)} %get-tuple-element.52), channel_id=1, source_target_pairs={{0,31},{1,0},{2,1},{3,2},{4,3},{5,4},{6,5},{7,6},{8,7},{9,8},{10,9... | collective-permute-start | bytes 344072 | tf_op jit(solution)/shard_map/ppermute | solution.py:525
  57.7 7.6 %collective-permute-start.6 = (f32[64,128]{1,0:T(8,128)S(1)}, f32[64,128]{1,0:T(8,128)S(1)}, u32[]{:S(2)}, u32[]{:S(2)}) collective-permute-start(f32[64,128]{1,0:T(8,128)S(1)} %get-tuple-element.53.after.pair), channel_id=1, source_target_pairs={{0,2},{1,3},{2,4},{3,5},{4,6},{5,7},{6,8},{7,9},{8,10},{9,11},{10,... | collective-permute-start | bytes 98312 | tf_op jit(solution)/shard_map/ppermute | solution.py:525
  57.8 7.5 %collective-permute-start.7 = (f32[64,128]{1,0:T(8,128)S(1)}, f32[64,128]{1,0:T(8,128)S(1)}, u32[]{:S(2)}, u32[]{:S(2)}) collective-permute-start(f32[64,128]{1,0:T(8,128)S(1)} %get-tuple-element.53.after.pair), channel_id=1, source_target_pairs={{0,30},{1,31},{2,0},{3,1},{4,2},{5,3},{6,4},{7,5},{8,6},{9,7},{10,... | collective-permute-start | bytes 98312 | tf_op jit(solution)/shard_map/ppermute | solution.py:525
  65.3 5.1 %copy-start.1 = (f32[1,4,64,128]{3,2,1,0:T(8,128)S(1)}, f32[1,4,64,128]{3,2,1,0:T(8,128)}, u32[]{:S(2)}) copy-start(f32[1,4,64,128]{3,2,1,0:T(8,128)} %u.1) | copy-start | bytes 393220
  66.0 4.4 %collective-permute-start.8 = (f32[1,4,64,128]{3,2,1,0:T(8,128)S(1)}, f32[1,4,64,128]{3,2,1,0:T(8,128)S(1)}, u32[]{:S(2)}, u32[]{:S(2)}) collective-permute-start(f32[1,4,64,128]{3,2,1,0:T(8,128)S(1)} %shard_map.57), channel_id=1, source_target_pairs={{0,32},{1,33},{2,34},{3,35},{4,36},{5,37},{6,38},{7,39},{8,40},{9,... | collective-permute-start | bytes 393224 | tf_op jit(solution)/shard_map/ppermute | solution.py:525
